TPU v7x, 32 devices: a whole 2x2x4 slice. The times are simulated.
32 devices in a mesh: fsdp: 16 (over z, y, core), tp: 2 (over x).
Axes of the slice: x: 2, y: 2, z: 4, core: 2. Of those that a mesh axis runs over, the one named last changes fastest.
Arguments:
- block_input: float32 [4096, 2048], P(('fsdp', 'tp')), may hold values from -6 to 6
- upstream_grad: float32 [4096, 2048], P(('fsdp', 'tp')), may hold values from -6 to 6
- first_gain: float32 [2048], replicated, may hold values from 0.1 to 1.9
- second_gain: float32 [2048], replicated, may hold values from 0.1 to 1.9
- query_weight: bfloat16 [2048, 2048], P('fsdp', 'tp'), may hold values from -0.125 to 0.125
- key_weight: bfloat16 [2048, 2048], P('fsdp', 'tp'), may hold values from -0.125 to 0.125
- value_weight: bfloat16 [2048, 2048], P('fsdp', 'tp'), may hold values from -0.125 to 0.125
- output_weight: bfloat16 [2048, 2048], P('fsdp', 'tp'), may hold values from -2 to 2
- gate_weight: bfloat16 [16, 2048, 1024], P('fsdp', None, 'tp'), may hold values from -0.125 to 0.125
- up_weight: bfloat16 [16, 2048, 1024], P('fsdp', None, 'tp'), may hold values from -0.125 to 0.125
- down_weight: bfloat16 [16, 1024, 2048], P('fsdp', 'tp'), may hold values from -0.375 to 0.375
- routes: int32 [4096, 8], P('fsdp'), may hold values from 0 to 15, all different within a row; in each aligned block of 256 rows (0 to 255, 256 to 511, ...) at most 192 rows name the same one
- gate_values: float32 [4096, 8], P('fsdp'), may hold values from 0.03 to 0.4
Outputs:
- block_output: float32 [4096, 2048], P(('fsdp', 'tp'))
- input_grad: float32 [4096, 2048], P(('fsdp', 'tp'))
- first_gain_grad: float32 [2048], replicated
- second_gain_grad: float32 [2048], replicated
- query_grad: float32 [2048, 2048], P('fsdp', 'tp')
- key_grad: float32 [2048, 2048], P('fsdp', 'tp')
- value_grad: float32 [2048, 2048], P('fsdp', 'tp')
- output_grad: float32 [2048, 2048], P('fsdp', 'tp')
- gate_grad: float32 [16, 2048, 1024], P('fsdp', None, 'tp')
- up_grad: float32 [16, 2048, 1024], P('fsdp', None, 'tp')
- down_grad: float32 [16, 1024, 2048], P('fsdp', 'tp')
- route_grad: float32 [4096, 8], P(('fsdp', 'tp'))
Inputs may be any that keep to these rules, and one draw needn't show every extreme that they name: `routes`: each row names 8 different experts. Within each sequence's 256 rows no expert is named by more than 192 rows, and in some sequence one expert is named by exactly 192.
All inputs are finite; a program needn't handle non-finite values.
Results may differ from a plain program's by a relative error of at most 0.015.
Values may be sent and summed in bfloat16 or wider, within the bound.
A program may use at most 256 MiB of HBM per device.

v0:
```python
import jax
import jax.numpy as jnp
from jax import lax
from jax.sharding import PartitionSpec as P

HD = 128
TOP = 8
EXP_DEV = 1


epsilon = 1e-05


def route_slots(route_rows, expert_count, capacity):
    flat_routes = route_rows.reshape(-1)
    onehot = (flat_routes[:, None] == jnp.arange(expert_count, dtype=jnp.int32)[None, :]).astype(
        jnp.int32
    )
    earlier = jnp.cumsum(onehot, axis=0, dtype=jnp.int32) - onehot
    ranked = jnp.sum(earlier * onehot, axis=1, dtype=jnp.int32)
    return flat_routes * capacity + ranked


def pair_rows(row_block):
    return lax.all_gather(row_block, "tp", axis=0, tiled=True)


def pair_sums(term_block):
    return lax.psum_scatter(term_block, "tp", scatter_dimension=0, tiled=True)


def to_owners(buffer):
    return lax.all_to_all(buffer, "fsdp", split_axis=0, concat_axis=0, tiled=True)


def to_sources(buffer):
    return lax.all_to_all(buffer, "fsdp", split_axis=0, concat_axis=0, tiled=True)


def projections(query_weight, key_weight, value_weight, output_weight):
    return (
        lax.all_gather(query_weight, "fsdp", axis=0, tiled=True),
        lax.all_gather(key_weight, "fsdp", axis=0, tiled=True),
        lax.all_gather(value_weight, "fsdp", axis=0, tiled=True),
        lax.all_gather(output_weight, "fsdp", axis=0, tiled=True),
    )


def scatter_rows(row_block, slot_index, total_rows):
    return (
        jnp.zeros((total_rows, row_block.shape[1]), row_block.dtype).at[slot_index].set(row_block)
    )


def spread_rows(row_block, copies):
    return jnp.broadcast_to(
        row_block[:, None, :], (row_block.shape[0], copies, row_block.shape[1])
    ).reshape(-1, row_block.shape[1])


def contract_rows(left_block, right_block):
    return lax.dot_general(
        left_block, right_block, (((0,), (0,)), ((), ())), preferred_element_type=jnp.float32
    )


def contract_cols(left_block, right_block):
    return lax.dot_general(
        left_block, right_block, (((1,), (1,)), ((), ())), preferred_element_type=jnp.float32
    )


def send_out(full_buffer):
    return to_owners(full_buffer)


def send_back(group_parts):
    owner_count, local_experts, capacity, model_width = group_parts.shape
    return to_sources(group_parts).reshape(owner_count * local_experts * capacity, model_width)


def per_device(
    block_input,
    upstream_grad,
    first_gain,
    second_gain,
    query_weight,
    key_weight,
    value_weight,
    output_weight,
    gate_weight,
    up_weight,
    down_weight,
    routes,
    gate_values,
):
    pair_count = lax.axis_size("tp")
    owner_count = lax.axis_size("fsdp")
    local_rows = block_input.shape[0]
    seq_rows = local_rows * pair_count
    model_width = block_input.shape[1]
    head_cols = query_weight.shape[1]
    local_heads = head_cols // HD
    expert_count = EXP_DEV * owner_count
    capacity = 3 * seq_rows * TOP // (2 * expert_count)
    inv_root = HD ** (-0.5)
    first_scale = lax.rsqrt(jnp.mean(block_input * block_input, axis=1, keepdims=True) + epsilon)
    first_normed = (block_input * first_scale * first_gain).astype(jnp.bfloat16)
    normed_rows = pair_rows(first_normed)
    query_full, key_full, value_full, output_full = projections(
        query_weight, key_weight, value_weight, output_weight
    )
    query_rows = (
        jnp.dot(normed_rows, query_full, preferred_element_type=jnp.float32)
        .astype(jnp.bfloat16)
        .reshape(seq_rows, local_heads, HD)
    )
    key_rows = (
        jnp.dot(normed_rows, key_full, preferred_element_type=jnp.float32)
        .astype(jnp.bfloat16)
        .reshape(seq_rows, local_heads, HD)
    )
    value_rows = (
        jnp.dot(normed_rows, value_full, preferred_element_type=jnp.float32)
        .astype(jnp.bfloat16)
        .reshape(seq_rows, local_heads, HD)
    )
    scores = (
        jnp.einsum("shd,thd->hst", query_rows, key_rows, preferred_element_type=jnp.float32)
        * inv_root
    )
    row_top = jnp.max(scores, axis=2, keepdims=True)
    log_total = row_top + jnp.log(jnp.sum(jnp.exp(scores - row_top), axis=2, keepdims=True))
    soft_weights = jnp.exp(scores - log_total)
    mixed_rows = jnp.einsum(
        "hst,thd->shd",
        soft_weights.astype(jnp.bfloat16),
        value_rows,
        preferred_element_type=jnp.float32,
    )
    mixed_rows = mixed_rows.astype(jnp.bfloat16).reshape(seq_rows, head_cols)
    middle = block_input + pair_sums(contract_cols(mixed_rows, output_full))
    second_scale = lax.rsqrt(jnp.mean(middle * middle, axis=1, keepdims=True) + epsilon)
    second_normed = (middle * second_scale * second_gain).astype(jnp.bfloat16)
    moe_rows = pair_rows(second_normed)
    slot_index = route_slots(routes, expert_count, capacity)
    send_rows = scatter_rows(spread_rows(moe_rows, TOP), slot_index, expert_count * capacity)
    arrived = send_out(send_rows.reshape(owner_count, EXP_DEV, capacity, model_width))
    gate_act = jnp.einsum(
        "secd,edf->secf", arrived, gate_weight, preferred_element_type=jnp.float32
    )
    up_act = jnp.einsum("secd,edf->secf", arrived, up_weight, preferred_element_type=jnp.float32)
    sigmoid_gate = jax.nn.sigmoid(gate_act)
    hidden = (gate_act * sigmoid_gate * up_act).astype(jnp.bfloat16)
    expert_out = jnp.einsum(
        "secf,efd->secd", hidden, down_weight, preferred_element_type=jnp.float32
    ).astype(jnp.bfloat16)
    returned = send_back(expert_out)
    picked = returned[slot_index].reshape(seq_rows, TOP, model_width).astype(jnp.float32)
    mixture = jnp.sum(gate_values[:, :, None] * picked, axis=1)
    block_output = middle + pair_sums(mixture)
    upstream_rows = lax.all_gather(upstream_grad, "tp", axis=0, tiled=True)
    route_terms = jnp.sum(upstream_rows[:, None, :] * picked, axis=2)
    routed_cot = (
        (gate_values[:, :, None] * upstream_rows[:, None, :])
        .astype(jnp.bfloat16)
        .reshape(seq_rows * TOP, model_width)
    )
    cot_send = scatter_rows(routed_cot, slot_index, expert_count * capacity)
    cot_arrived = send_out(cot_send.reshape(owner_count, EXP_DEV, capacity, model_width))
    hidden_cot = jnp.einsum(
        "secd,efd->secf", cot_arrived, down_weight, preferred_element_type=jnp.float32
    )
    down_grad = jnp.einsum(
        "secf,secd->efd", hidden, cot_arrived, preferred_element_type=jnp.float32
    )
    gate_cot = (
        hidden_cot * up_act * sigmoid_gate * (1.0 + gate_act * (1.0 - sigmoid_gate))
    ).astype(jnp.bfloat16)
    up_cot = (hidden_cot * gate_act * sigmoid_gate).astype(jnp.bfloat16)
    gate_grad = jnp.einsum("secd,secf->edf", arrived, gate_cot, preferred_element_type=jnp.float32)
    up_grad = jnp.einsum("secd,secf->edf", arrived, up_cot, preferred_element_type=jnp.float32)
    input_cot = jnp.einsum(
        "secf,edf->secd", gate_cot, gate_weight, preferred_element_type=jnp.float32
    )
    input_cot = (
        input_cot
        + jnp.einsum("secf,edf->secd", up_cot, up_weight, preferred_element_type=jnp.float32)
    ).astype(jnp.bfloat16)
    came_back = send_back(input_cot)
    normed_cot = jnp.sum(
        came_back[slot_index].reshape(seq_rows, TOP, model_width).astype(jnp.float32), axis=1
    )
    second_cot, route_grad = (
        lax.psum_scatter(
            normed_cot.astype(jnp.bfloat16), "tp", scatter_dimension=0, tiled=True
        ).astype(jnp.float32),
        lax.psum_scatter(
            route_terms.astype(jnp.bfloat16), "tp", scatter_dimension=0, tiled=True
        ).astype(jnp.float32),
    )
    weighted_two = second_cot * second_gain
    second_term = jnp.sum(second_cot * middle * second_scale, axis=0)
    middle_grad = upstream_grad + second_scale * (
        weighted_two
        - middle
        * second_scale
        * second_scale
        * jnp.mean(weighted_two * middle, axis=1, keepdims=True)
    )
    middle_rows = pair_rows(middle_grad.astype(jnp.bfloat16))
    query_full, key_full, value_full, output_full = projections(
        query_weight, key_weight, value_weight, output_weight
    )
    out_term = contract_rows(middle_rows, mixed_rows)
    mixed_cot = (
        jnp.dot(middle_rows, output_full, preferred_element_type=jnp.float32)
        .astype(jnp.bfloat16)
        .reshape(seq_rows, local_heads, HD)
    )
    scores = (
        jnp.einsum("shd,thd->hst", query_rows, key_rows, preferred_element_type=jnp.float32)
        * inv_root
    )
    soft_weights = jnp.exp(scores - log_total)
    value_cot = jnp.einsum(
        "hst,shd->thd",
        soft_weights.astype(jnp.bfloat16),
        mixed_cot,
        preferred_element_type=jnp.float32,
    )
    value_cot = value_cot.astype(jnp.bfloat16).reshape(seq_rows, head_cols)
    soft_cot = jnp.einsum("shd,thd->hst", mixed_cot, value_rows, preferred_element_type=jnp.float32)
    score_cot = (
        soft_weights
        * (soft_cot - jnp.sum(soft_weights * soft_cot, axis=2, keepdims=True))
        * inv_root
    ).astype(jnp.bfloat16)
    query_cot = (
        jnp.einsum("hst,thd->shd", score_cot, key_rows, preferred_element_type=jnp.float32)
        .astype(jnp.bfloat16)
        .reshape(seq_rows, head_cols)
    )
    key_cot = (
        jnp.einsum("hst,shd->thd", score_cot, query_rows, preferred_element_type=jnp.float32)
        .astype(jnp.bfloat16)
        .reshape(seq_rows, head_cols)
    )
    query_term = contract_rows(normed_rows, query_cot)
    key_term = contract_rows(normed_rows, key_cot)
    value_term = contract_rows(normed_rows, value_cot)
    first_terms = (
        contract_cols(query_cot, query_full)
        + contract_cols(key_cot, key_full)
        + contract_cols(value_cot, value_full)
    )
    first_cot = pair_sums(first_terms)
    weighted_one = first_cot * first_gain
    first_term = jnp.sum(first_cot * block_input * first_scale, axis=0)
    input_grad = middle_grad + first_scale * (
        weighted_one
        - block_input
        * first_scale
        * first_scale
        * jnp.mean(weighted_one * block_input, axis=1, keepdims=True)
    )
    query_grad, key_grad, value_grad, output_grad = (
        lax.psum_scatter(query_term, "fsdp", scatter_dimension=0, tiled=True),
        lax.psum_scatter(key_term, "fsdp", scatter_dimension=0, tiled=True),
        lax.psum_scatter(value_term, "fsdp", scatter_dimension=0, tiled=True),
        lax.psum_scatter(out_term, "fsdp", scatter_dimension=0, tiled=True),
    )
    first_gain_grad, second_gain_grad = lax.psum((first_term, second_term), ("fsdp", "tp"))
    return (
        block_output,
        input_grad,
        first_gain_grad,
        second_gain_grad,
        query_grad,
        key_grad,
        value_grad,
        output_grad,
        gate_grad,
        up_grad,
        down_grad,
        route_grad,
    )


def solution(mesh):
    in_specs = (
        P(("fsdp", "tp"), None),
        P(("fsdp", "tp"), None),
        P(),
        P(),
        P("fsdp", "tp"),
        P("fsdp", "tp"),
        P("fsdp", "tp"),
        P("fsdp", "tp"),
        P("fsdp", None, "tp"),
        P("fsdp", None, "tp"),
        P("fsdp", "tp", None),
        P("fsdp", None),
        P("fsdp", None),
    )
    out_specs = (
        P(("fsdp", "tp"), None),
        P(("fsdp", "tp"), None),
        P(),
        P(),
        P("fsdp", "tp"),
        P("fsdp", "tp"),
        P("fsdp", "tp"),
        P("fsdp", "tp"),
        P("fsdp", None, "tp"),
        P("fsdp", None, "tp"),
        P("fsdp", "tp", None),
        P(("fsdp", "tp"), None),
    )
    return jax.shard_map(
        per_device, mesh=mesh, in_specs=in_specs, out_specs=out_specs, check_vma=False
    )
```

profile of v0, /device:TPU:0, one launch (start us, length us, event | category | flops | bytes accessed | tf_op | source)
XLA Modules:
  0.0 2036.9 jit_solution(673963974362242166)
XLA Ops:
  14.2 21.5 %all-gather.9.cloned.1.call-done = bf16[256,2048]{1,0:T(8,128)(2,1)} async-done(((bf16[128,2048]{1,0:T(8,128)(2,1)}), bf16[256,2048]{1,0:T(8,128)(2,1)}) %all-gather.9.cloned.1.call-update) | async-done | bytes 1048592 | tf_op jit(solution)/shard_map/all_gather | solution.py:25
  35.6 52.6 %all-gather.15.cloned.1.call-done = bf16[2048,1024]{1,0:T(8,128)(2,1)} async-done(((bf16[128,1024]{1,0:T(8,128)(2,1)}), bf16[2048,1024]{1,0:T(8,128)(2,1)}) %all-gather.15.cloned.1.call-update) | async-done | bytes 4194320 | tf_op jit(solution)/shard_map/all_gather | solution.py:43
  94.8 44.5 %all-gather.13.cloned.1.call-done = bf16[2048,1024]{1,0:T(8,128)(2,1)} async-done(((bf16[128,1024]{1,0:T(8,128)(2,1)}), bf16[2048,1024]{1,0:T(8,128)(2,1)}) %all-gather.13.cloned.1.call-update) | async-done | bytes 4194320 | tf_op jit(solution)/shard_map/all_gather | solution.py:42
  149.0 41.3 %all-gather.11.cloned.1.call-done = bf16[2048,1024]{1,0:T(8,128)(2,1)} async-done(((bf16[128,1024]{1,0:T(8,128)(2,1)}), bf16[2048,1024]{1,0:T(8,128)(2,1)}) %all-gather.11.cloned.1.call-update) | async-done | bytes 4194320 | tf_op jit(solution)/shard_map/all_gather | solution.py:44
  196.1 45.2 %all-gather.17.cloned.1.call-done = bf16[2048,1024]{1,0:T(8,128)(2,1)} async-done(((bf16[128,1024]{1,0:T(8,128)(2,1)}), bf16[2048,1024]{1,0:T(8,128)(2,1)}) %all-gather.17.cloned.1.call-update) | async-done | bytes 4194320 | tf_op jit(solution)/shard_map/all_gather | solution.py:45
  247.2 29.7 %reduce-scatter.12.cloned.1.call-done = f32[128,2048]{1,0:T(8,128)} async-done(((f32[256,2048]{1,0:T(8,128)}), f32[128,2048]{1,0:T(8,128)}) %reduce-scatter.12.cloned.1.call-update) | async-done | bytes 1048592 | tf_op jit(solution)/shard_map/reduce_scatter | solution.py:29
  285.7 16.1 all-gather.19.cloned.1.call-done
  301.7 19.7 scatter_custom_fusion
  328.2 34.8 %all-gather.21.cloned.1.call-done = f32[256,2048]{1,0:T(8,128)} async-done(((f32[128,2048]{1,0:T(8,128)}), f32[256,2048]{1,0:T(8,128)}) %all-gather.21.cloned.1.call-update) | async-done | bytes 2097168 | tf_op jit(solution)/shard_map/all_gather | solution.py:162
  363.0 20.2 scatter_custom_fusion.1
  383.2 167.6 %all-to-all-done = bf16[16,1,192,2048]{3,2,1,0:T(8,128)(2,1)} async-done(((bf16[16,1,192,2048]{3,2,1,0:T(8,128)(2,1)}), bf16[16,1,192,2048]{3,2,1,0:T(8,128)(2,1)}, u32[]{:S(2)}, u32[]{:S(2)}) %all-to-all-start) | async-done | bytes 12582944 | tf_op jit(solution)/shard_map/all_to_all | solution.py:33
  550.8 53.8 %all-to-all-start.2 = ((bf16[16,1,192,2048]{3,2,1,0:T(8,128)(2,1)}), bf16[16,1,192,2048]{3,2,1,0:T(8,128)(2,1)}, u32[]{:S(2)}, u32[]{:S(2)}) async-start(bf16[16,1,192,2048]{3,2,1,0:T(8,128)(2,1)} %bitcast.229), calls=%async_computation.4 | async-start | bytes 25165824 | tf_op jit(solution)/shard_map/all_to_all | solution.py:33
  604.6 12.1 fusion.13
  628.1 200.1 %all-to-all-done.2 = bf16[16,1,192,2048]{3,2,1,0:T(8,128)(2,1)} async-done(((bf16[16,1,192,2048]{3,2,1,0:T(8,128)(2,1)}), bf16[16,1,192,2048]{3,2,1,0:T(8,128)(2,1)}, u32[]{:S(2)}, u32[]{:S(2)}) %all-to-all-start.2) | async-done | bytes 12582944 | tf_op jit(solution)/shard_map/all_to_all | solution.py:33
  828.2 18.0 fusion.27
  846.2 12.2 fusion.48
  858.4 15.8 fusion.4
  874.2 53.4 %all-to-all-start.3 = ((bf16[16,1,192,2048]{3,2,1,0:T(8,128)(2,1)}), bf16[16,1,192,2048]{3,2,1,0:T(8,128)(2,1)}, u32[]{:S(2)}, u32[]{:S(2)}) async-start(bf16[16,1,192,2048]{3,2,1,0:T(8,128)(2,1)} %fusion.4), calls=%async_computation.5 | async-start | bytes 25165824 | tf_op jit(solution)/shard_map/all_to_all | solution.py:37
  927.6 11.6 convert_bitcast_fusion
  939.2 212.0 %all-to-all-done.3 = bf16[16,1,192,2048]{3,2,1,0:T(8,128)(2,1)} async-done(((bf16[16,1,192,2048]{3,2,1,0:T(8,128)(2,1)}), bf16[16,1,192,2048]{3,2,1,0:T(8,128)(2,1)}, u32[]{:S(2)}, u32[]{:S(2)}) %all-to-all-start.3) | async-done | bytes 12582944 | tf_op jit(solution)/shard_map/all_to_all | solution.py:37
  1151.2 53.4 %all-to-all-start.1 = ((bf16[16,1,192,2048]{3,2,1,0:T(8,128)(2,1)}), bf16[16,1,192,2048]{3,2,1,0:T(8,128)(2,1)}, u32[]{:S(2)}, u32[]{:S(2)}) async-start(bf16[16,1,192,2048]{3,2,1,0:T(8,128)(2,1)} %convert_bitcast_fusion), calls=%async_computation.2 | async-start | bytes 25165824 | tf_op jit(solution)/shard_map/all_to_all | solution.py:37
  1204.7 23.0 %gather_fusion.1 = bf16[2048,2048]{1,0:T(8,128)(2,1)} fusion(bf16[3072,2048]{1,0:T(8,128)(2,1)} %bitcast.45, s32[2048]{0:T(1024)S(1)} %broadcast_clamp_fusion), kind=kCustom, calls=%fused_computation.1 | custom fusion | bytes 16785408 | tf_op jit(solution)/shard_map/gather | solution.py:192
  1238.9 20.8 %reduce-scatter.16.cloned.1.call-done = bf16[128,2048]{1,0:T(8,128)(2,1)} async-done(((bf16[256,2048]{1,0:T(8,128)(2,1)}), bf16[128,2048]{1,0:T(8,128)(2,1)}) %reduce-scatter.16.cloned.1.call-update) | async-done | bytes 524304 | tf_op jit(solution)/shard_map/reduce_scatter | solution.py:195
  1263.4 164.8 %all-to-all-done.1 = bf16[16,1,192,2048]{3,2,1,0:T(8,128)(2,1)} async-done(((bf16[16,1,192,2048]{3,2,1,0:T(8,128)(2,1)}), bf16[16,1,192,2048]{3,2,1,0:T(8,128)(2,1)}, u32[]{:S(2)}, u32[]{:S(2)}) %all-to-all-start.1) | async-done | bytes 12582944 | tf_op jit(solution)/shard_map/all_to_all | solution.py:37
  1428.2 22.8 %gather_fusion = bf16[2048,2048]{1,0:T(8,128)(2,1)} fusion(bf16[3072,2048]{1,0:T(8,128)(2,1)} %bitcast.27, s32[2048]{0:T(1024)S(1)} %broadcast_clamp_fusion), kind=kCustom, calls=%fused_computation | custom fusion | bytes 16785408 | tf_op jit(solution)/shard_map/gather | solution.py:159
  1507.4 12.1 fusion.42
  1543.1 22.1 %reduce-scatter.18.cloned.1.call-done = f32[128,2048]{1,0:T(8,128)} async-done(((f32[256,2048]{1,0:T(8,128)}), f32[128,2048]{1,0:T(8,128)}) %reduce-scatter.18.cloned.1.call-update) | async-done | bytes 1048592 | tf_op jit(solution)/shard_map/reduce_scatter | solution.py:29
  1566.9 66.9 %all-reduce = (f32[2048]{0:T(1024)}, f32[2048]{0:T(1024)}) all-reduce(f32[2048]{0:T(1024)S(1)} %get-tuple-element.14, f32[2048]{0:T(1024)S(1)} %get-tuple-element.16), channel_id=1, replica_groups=mesh['fsdp'=16,'tp'=2] {'fsdp','tp'}, use_global_device_ids=true, to_apply=%region_19.20 | all-reduce | flops 4096 | bytes 32768 | tf_op jit(solution)/shard_map/psum | solution.py:273
  1638.6 68.7 %reduce-scatter.26.cloned.1.call-done = f32[128,1024]{1,0:T(8,128)} async-done(((f32[2048,1024]{1,0:T(8,128)}), f32[128,1024]{1,0:T(8,128)}) %reduce-scatter.26.cloned.1.call-update) | async-done | bytes 524304 | tf_op jit(solution)/shard_map/reduce_scatter | solution.py:271
  1707.4 107.6 %reduce-scatter.24.cloned.1.call-done = f32[128,1024]{1,0:T(8,128)} async-done(((f32[2048,1024]{1,0:T(8,128)}), f32[128,1024]{1,0:T(8,128)}) %reduce-scatter.24.cloned.1.call-update) | async-done | bytes 524304 | tf_op jit(solution)/shard_map/reduce_scatter | solution.py:270
  1815.0 107.6 %reduce-scatter.22.cloned.1.call-done = f32[128,1024]{1,0:T(8,128)} async-done(((f32[2048,1024]{1,0:T(8,128)}), f32[128,1024]{1,0:T(8,128)}) %reduce-scatter.22.cloned.1.call-update) | async-done | bytes 524304 | tf_op jit(solution)/shard_map/reduce_scatter | solution.py:269
  1922.6 107.6 %reduce-scatter.20.cloned.1.call-done = f32[128,1024]{1,0:T(8,128)} async-done(((f32[2048,1024]{1,0:T(8,128)}), f32[128,1024]{1,0:T(8,128)}) %reduce-scatter.20.cloned.1.call-update) | async-done | bytes 524304 | tf_op jit(solution)/shard_map/reduce_scatter | solution.py:268
  (172 shorter events, 162.8 us)
Async XLA Ops:
  7.2 821.0 %copy-start = (bf16[1,512,2048]{2,1,0:T(8,128)(2,1)S(1)}, bf16[1,512,2048]{2,1,0:T(8,128)(2,1)}, u32[]{:S(2)}) copy-start(bf16[1,512,2048]{2,1,0:T(8,128)(2,1)} %param.23) | copy-start | bytes 6291460
  7.2 28.4 %all-gather.9.cloned.1.call-start = ((), (), s32[]{:S(2)}) async-start(), calls=%async_computation.13 | async-start | bytes 1572864 | tf_op jit(solution)/shard_map/all_gather | solution.py:25
  11.5 76.7 %all-gather.15.cloned.1.call-start = ((), (), s32[]{:S(2)}) async-start(), calls=%async_computation.16 | async-start | bytes 4456448 | tf_op jit(solution)/shard_map/all_gather | solution.py:43
  12.2 127.1 %all-gather.13.cloned.1.call-start = ((), (), s32[]{:S(2)}) async-start(), calls=%async_computation.15 | async-start | bytes 4456448 | tf_op jit(solution)/shard_map/all_gather | solution.py:42
  13.0 177.3 %all-gather.11.cloned.1.call-start = ((), (), s32[]{:S(2)}) async-start(), calls=%async_computation.14 | async-start | bytes 4456448 | tf_op jit(solution)/shard_map/all_gather | solution.py:44
  13.5 227.7 %all-gather.17.cloned.1.call-start = ((), (), s32[]{:S(2)}) async-start(), calls=%async_computation.17 | async-start | bytes 4456448 | tf_op jit(solution)/shard_map/all_gather | solution.py:45
  14.1 262.8 %reduce-scatter.12.cloned.1.call-start = ((), (), s32[]{:S(2)}) async-start(), calls=%async_computation.18 | async-start | bytes 3145728 | tf_op jit(solution)/shard_map/reduce_scatter | solution.py:29
  35.6 103.7 %copy-start.9 = (bf16[256,2048]{1,0:T(8,128)(2,1)S(1)}, bf16[256,2048]{1,0:T(8,128)(2,1)}, u32[]{:S(2)}) copy-start(bf16[256,2048]{1,0:T(8,128)(2,1)} %all-gather.9.cloned.1.call-done) | copy-start | bytes 3145732
  149.0 47.1 %copy-start.23 = (f32[8,256]{1,0:T(8,128)}, f32[8,256]{1,0:T(8,128)S(1)}, u32[]{:S(2)}) copy-start(f32[8,256]{1,0:T(8,128)S(1)} %log_add_fusion) | copy-start | bytes 24580
  241.2 35.7 %copy-start.5 = (f32[128,2048]{1,0:T(8,128)S(1)}, f32[128,2048]{1,0:T(8,128)}, u32[]{:S(2)}) copy-start(f32[128,2048]{1,0:T(8,128)} %param.13) | copy-start | bytes 3145732
  246.3 33.0 %copy-start.21 = (f32[2048]{0:T(1024)S(1)}, f32[2048]{0:T(1024)}, u32[]{:S(2)}) copy-start(f32[2048]{0:T(1024)} %param.16) | copy-start | bytes 24580
  246.3 55.4 %all-gather.19.cloned.1.call-start = ((), (), s32[]{:S(2)}) async-start(), calls=%async_computation.19 | async-start | bytes 1572864 | tf_op jit(solution)/shard_map/all_gather | solution.py:25
  321.4 229.4 %all-to-all-start = ((bf16[16,1,192,2048]{3,2,1,0:T(8,128)(2,1)}), bf16[16,1,192,2048]{3,2,1,0:T(8,128)(2,1)}, u32[]{:S(2)}, u32[]{:S(2)}) async-start(bf16[16,1,192,2048]{3,2,1,0:T(8,128)(2,1)} %bitcast.228), calls=%async_computation.1 | async-start | bytes 25165824 | tf_op jit(solution)/shard_map/all_to_all | solution.py:33
  327.2 35.8 %all-gather.21.cloned.1.call-start = ((), (), s32[]{:S(2)}) async-start(), calls=%async_computation.21 | async-start | bytes 3145728 | tf_op jit(solution)/shard_map/all_gather | solution.py:162
  328.1 55.2 %copy-start.18 = (f32[256,8]{1,0:T(8,128)}, f32[256,8]{1,0:T(8,128)S(1)}, u32[]{:S(2)}) copy-start(f32[256,8]{1,0:T(8,128)S(1)} %copy.79) | copy-start | bytes 24580
  550.8 277.4 %all-to-all-start.2 = ((bf16[16,1,192,2048]{3,2,1,0:T(8,128)(2,1)}), bf16[16,1,192,2048]{3,2,1,0:T(8,128)(2,1)}, u32[]{:S(2)}, u32[]{:S(2)}) async-start(bf16[16,1,192,2048]{3,2,1,0:T(8,128)(2,1)} %bitcast.229), calls=%async_computation.4 | async-start | bytes 25165824 | tf_op jit(solution)/shard_map/all_to_all | solution.py:33
  874.2 277.0 %all-to-all-start.3 = ((bf16[16,1,192,2048]{3,2,1,0:T(8,128)(2,1)}), bf16[16,1,192,2048]{3,2,1,0:T(8,128)(2,1)}, u32[]{:S(2)}, u32[]{:S(2)}) async-start(bf16[16,1,192,2048]{3,2,1,0:T(8,128)(2,1)} %fusion.4), calls=%async_computation.5 | async-start | bytes 25165824 | tf_op jit(solution)/shard_map/all_to_all | solution.py:37
  1151.2 277.0 %all-to-all-start.1 = ((bf16[16,1,192,2048]{3,2,1,0:T(8,128)(2,1)}), bf16[16,1,192,2048]{3,2,1,0:T(8,128)(2,1)}, u32[]{:S(2)}, u32[]{:S(2)}) async-start(bf16[16,1,192,2048]{3,2,1,0:T(8,128)(2,1)} %convert_bitcast_fusion), calls=%async_computation.2 | async-start | bytes 25165824 | tf_op jit(solution)/shard_map/all_to_all | solution.py:37
  1204.6 55.1 %reduce-scatter.16.cloned.1.call-start = ((), (), s32[]{:S(2)}) async-start(), calls=%async_computation.22 | async-start | bytes 1572864 | tf_op jit(solution)/shard_map/reduce_scatter | solution.py:195
  1227.6 33.5 %copy-start.11 = (f32[128,2048]{1,0:T(8,128)S(1)}, f32[128,2048]{1,0:T(8,128)}, u32[]{:S(2)}) copy-start(f32[128,2048]{1,0:T(8,128)} %param.14) | copy-start | bytes 3145732
  1238.9 222.6 %all-gather.23.cloned.1.call-start = ((), (), s32[]{:S(2)}) async-start(), calls=%async_computation.23 | async-start | bytes 1572864 | tf_op jit(solution)/shard_map/all_gather | solution.py:25
  1263.3 278.3 %reduce-scatter.28.cloned.1.call-start = ((), (), s32[]{:S(2)}) async-start(), calls=%async_computation.29 | async-start | bytes 98304
  1461.4 103.8 %reduce-scatter.18.cloned.1.call-start = ((), (), s32[]{:S(2)}) async-start(), calls=%async_computation.24 | async-start | bytes 3145728 | tf_op jit(solution)/shard_map/reduce_scatter | solution.py:29
  1485.4 148.4 %reduce-scatter.14.cloned.1.call-start = ((), (), s32[]{:S(2)}) async-start(), calls=%async_computation.20 | async-start | bytes 3145728 | tf_op jit(solution)/shard_map/reduce_scatter | solution.py:29
  1486.1 221.3 %reduce-scatter.26.cloned.1.call-start = ((), (), s32[]{:S(2)}) async-start(), calls=%async_computation.28 | async-start | bytes 8912896 | tf_op jit(solution)/shard_map/reduce_scatter | solution.py:271
  1491.3 323.7 %reduce-scatter.24.cloned.1.call-start = ((), (), s32[]{:S(2)}) async-start(), calls=%async_computation.27 | async-start | bytes 8912896 | tf_op jit(solution)/shard_map/reduce_scatter | solution.py:270
  1497.1 425.5 %reduce-scatter.22.cloned.1.call-start = ((), (), s32[]{:S(2)}) async-start(), calls=%async_computation.26 | async-start | bytes 8912896 | tf_op jit(solution)/shard_map/reduce_scatter | solution.py:269
  1501.8 528.4 %reduce-scatter.20.cloned.1.call-start = ((), (), s32[]{:S(2)}) async-start(), calls=%async_computation.25 | async-start | bytes 8912896 | tf_op jit(solution)/shard_map/reduce_scatter | solution.py:268
  1530.6 34.6 %copy-start.6 = (f32[128,2048]{1,0:T(8,128)S(1)}, f32[128,2048]{1,0:T(8,128)}, u32[]{:S(2)}) copy-start(f32[128,2048]{1,0:T(8,128)} %param.13) | copy-start | bytes 3145732
  1530.6 34.6 %copy-start.25 = (f32[2048]{0:T(1024)S(1)}, f32[2048]{0:T(1024)}, u32[]{:S(2)}) copy-start(f32[2048]{0:T(1024)} %param.15) | copy-start | bytes 24580
  1530.6 34.6 %copy-start.31 = (f32[128]{0:T(128)S(1)}, f32[128]{0:T(128)}, u32[]{:S(2)}) copy-start(f32[128]{0:T(128)} %copy-done.30) | copy-start | bytes 1540
  1565.2 465.0 %copy-start.1 = (bf16[1,512,2048]{2,1,0:T(8,128)(2,1)S(1)}, bf16[1,512,2048]{2,1,0:T(8,128)(2,1)}, u32[]{:S(2)}) copy-start(bf16[1,512,2048]{2,1,0:T(8,128)(2,1)} %param.23) | copy-start | bytes 6291460
  (26 other events, 247.5 us)
Sparse Core Ops, SparseCore 0:
  11.6 23.9 all-gather.8
  37.8 50.3 all-gather.14
  90.4 48.8 all-gather.12
  141.3 48.8 all-gather.10
  192.3 48.8 all-gather.16
  246.4 30.4 reduce-scatter.11
  280.4 21.2 all-gather.18
  329.5 33.4 all-gather.20
  1239.0 20.7 reduce-scatter.15
  1263.5 21.2 all-gather.22
  1461.5 57.7 reduce-scatter.27
  1521.4 43.7 reduce-scatter.17
  1567.5 31.8 reduce-scatter.13
  1603.9 103.4 reduce-scatter.25
  1711.9 103.0 reduce-scatter.23
  1819.5 103.0 reduce-scatter.21
  1927.1 103.0 reduce-scatter.19
where the time goes:
time: 2040 us
  waiting for transfers between devices  1470 us (72%)
  matrix products  177 us (9%)
  starting transfers between devices  168 us (8%)
  local copies, waits for them, and re-layouts  79.6 us (4%)
  blocking collectives  66.9 us (3%)
  other arithmetic  62.9 us (3%)
    all_to_all x2, waiting for transfers between devices, to_sources(): lax.all_to_all(buffer, 'fsdp', split_axis=0, concat_axis=0, tiled=True)  377 us
    all_to_all x2, waiting for transfers between devices, to_owners(): lax.all_to_all(buffer, 'fsdp', split_axis=0, concat_axis=0, tiled=True)  368 us
    reduce_scatter x1, waiting for transfers between devices, per_device(): lax.psum_scatter(key_term, 'fsdp', scatter_dimension=0, tiled=True)  108 us
    reduce_scatter x1, waiting for transfers between devices, per_device(): lax.psum_scatter(value_term, 'fsdp', scatter_dimension=0, tiled=True)  108 us
    reduce_scatter x1, waiting for transfers between devices, per_device(): lax.psum_scatter(query_term, 'fsdp', scatter_dimension=0, tiled=True)  108 us
    all_to_all x2, starting transfers between devices, to_sources(): lax.all_to_all(buffer, 'fsdp', split_axis=0, concat_axis=0, tiled=True)  107 us
    reduce_scatter x1, waiting for transfers between devices, per_device(): lax.psum_scatter(out_term, 'fsdp', scatter_dimension=0, tiled=True)  68.7 us
    psum x1, blocking collectives, per_device(): lax.psum((first_term, second_term), ('fsdp', 'tp'))  66.9 us
  transfers between devices with their start and end apart: 21, of which 18 were waited for; matrix products, arithmetic and copies ran while one was open for 12% of the time, Pallas kernels for 0%

commit v1 on v0

--- a/solution.py
+++ b/solution.py
@@ -79,7 +79,7 @@
     return to_sources(group_parts).reshape(owner_count * local_experts * capacity, model_width)
 
 
-def per_device(
+def per_device_slots(
     block_input,
     upstream_grad,
     first_gain,
@@ -287,7 +287,198 @@
     )
 
 
+def gate_columns(route_rows, gate_rows, expert_count):
+    names = jnp.arange(expert_count, dtype=jnp.int32)[None, None, :]
+    return jnp.sum(jnp.where(route_rows[:, :, None] == names, gate_rows[:, :, None], 0.0), axis=1)
+
+
+def half_of(rows):
+    count = rows.shape[0] // lax.axis_size("tp")
+    return lax.dynamic_slice_in_dim(rows, lax.axis_index("tp") * count, count, axis=0)
+
+
+def per_device_dense(
+    block_input,
+    upstream_grad,
+    first_gain,
+    second_gain,
+    query_weight,
+    key_weight,
+    value_weight,
+    output_weight,
+    gate_weight,
+    up_weight,
+    down_weight,
+    routes,
+    gate_values,
+):
+    pair_count = lax.axis_size("tp")
+    owner_count = lax.axis_size("fsdp")
+    local_rows = block_input.shape[0]
+    seq_rows = local_rows * pair_count
+    model_width = block_input.shape[1]
+    head_cols = query_weight.shape[1]
+    local_heads = head_cols // HD
+    expert_count = EXP_DEV * owner_count
+    inv_root = HD ** (-0.5)
+    bf16, f32 = jnp.bfloat16, jnp.float32
+
+    my_routes, my_gates = half_of(routes), half_of(gate_values)
+    gate_table = lax.all_gather(
+        gate_columns(my_routes, my_gates, expert_count), "fsdp", axis=0, tiled=True
+    )
+    expert_names = jnp.arange(expert_count, dtype=jnp.int32)[None, :]
+    gate_all = jnp.sum(
+        jnp.where(expert_names == lax.axis_index("fsdp"), gate_table, 0.0), axis=1, keepdims=True
+    )
+    gate_pair = lax.all_gather(gate_weight[0], "tp", axis=0)
+    up_pair = lax.all_gather(up_weight[0], "tp", axis=0)
+    down_pair = lax.all_gather(down_weight[0], "tp", axis=0)
+    upstream_all = lax.all_gather(upstream_grad.astype(bf16), "fsdp", axis=0, tiled=True)
+
+    first_scale = lax.rsqrt(jnp.mean(block_input * block_input, axis=1, keepdims=True) + epsilon)
+    first_normed = (block_input * first_scale * first_gain).astype(bf16)
+    normed_rows = pair_rows(first_normed)
+    query_full, key_full, value_full, output_full = projections(
+        query_weight, key_weight, value_weight, output_weight
+    )
+
+    def heads_of(weight_full):
+        return (
+            jnp.dot(normed_rows, weight_full, preferred_element_type=f32)
+            .astype(bf16)
+            .reshape(seq_rows, local_heads, HD)
+        )
+
+    query_rows, key_rows, value_rows = heads_of(query_full), heads_of(key_full), heads_of(value_full)
+    scores = jnp.einsum("shd,thd->hst", query_rows, key_rows, preferred_element_type=f32) * inv_root
+    row_top = jnp.max(scores, axis=2, keepdims=True)
+    log_total = row_top + jnp.log(jnp.sum(jnp.exp(scores - row_top), axis=2, keepdims=True))
+    soft_weights = jnp.exp(scores - log_total)
+    soft_rounded = soft_weights.astype(bf16)
+    mixed_rows = jnp.einsum("hst,thd->shd", soft_rounded, value_rows, preferred_element_type=f32)
+    mixed_rows = mixed_rows.astype(bf16).reshape(seq_rows, head_cols)
+    middle = block_input + pair_sums(contract_cols(mixed_rows, output_full))
+    second_scale = lax.rsqrt(jnp.mean(middle * middle, axis=1, keepdims=True) + epsilon)
+    second_normed = (middle * second_scale * second_gain).astype(bf16)
+
+    rows_all = lax.all_gather(second_normed, "fsdp", axis=0, tiled=True)
+    gate_act = jnp.einsum("td,gdf->gtf", rows_all, gate_pair, preferred_element_type=f32)
+    up_act = jnp.einsum("td,gdf->gtf", rows_all, up_pair, preferred_element_type=f32)
+    sigmoid_gate = jax.nn.sigmoid(gate_act)
+    hidden = gate_act * sigmoid_gate * up_act
+    hidden_gated = (hidden * gate_all).astype(bf16)
+    mixture_part = jnp.einsum("gtf,gfd->td", hidden_gated, down_pair, preferred_element_type=f32)
+    hidden_cot = jnp.einsum("td,gfd->gtf", upstream_all, down_pair, preferred_element_type=f32)
+    route_sums = jnp.sum(hidden * hidden_cot, axis=(0, 2))
+    hidden_cot = hidden_cot * gate_all
+    gate_cot = (
+        hidden_cot * up_act * sigmoid_gate * (1.0 + gate_act * (1.0 - sigmoid_gate))
+    ).astype(bf16)
+    up_cot = (hidden_cot * gate_act * sigmoid_gate).astype(bf16)
+    input_cot = jnp.einsum("gtf,gdf->td", gate_cot, gate_pair, preferred_element_type=f32)
+    input_cot = input_cot + jnp.einsum("gtf,gdf->td", up_cot, up_pair, preferred_element_type=f32)
+    second_cot = lax.psum_scatter(
+        input_cot.astype(bf16), "fsdp", scatter_dimension=0, tiled=True
+    ).astype(f32)
+    mixture = lax.psum_scatter(
+        mixture_part.astype(bf16), "fsdp", scatter_dimension=0, tiled=True
+    ).astype(f32)
+    block_output = middle + mixture
+    route_back = lax.all_to_all(
+        route_sums.reshape(owner_count, local_rows), "fsdp", split_axis=0, concat_axis=0, tiled=True
+    )
+    route_grad = jnp.sum(
+        jnp.where(my_routes[:, :, None] == expert_names[None], route_back.T[:, None, :], 0.0), axis=2
+    )
+    down_part = jnp.einsum("gtf,td->gfd", hidden_gated, upstream_all, preferred_element_type=f32)
+    gate_part = jnp.einsum("td,gtf->gdf", rows_all, gate_cot, preferred_element_type=f32)
+    up_part = jnp.einsum("td,gtf->gdf", rows_all, up_cot, preferred_element_type=f32)
+
+    def pair_grad(part):
+        return lax.psum_scatter(part.astype(bf16), "tp", scatter_dimension=0).astype(f32)
+
+    down_grad, gate_grad, up_grad = pair_grad(down_part), pair_grad(gate_part), pair_grad(up_part)
+
+    weighted_two = second_cot * second_gain
+    second_term = jnp.sum(second_cot * middle * second_scale, axis=0)
+    middle_grad = upstream_grad + second_scale * (
+        weighted_two
+        - middle
+        * second_scale
+        * second_scale
+        * jnp.mean(weighted_two * middle, axis=1, keepdims=True)
+    )
+    middle_rows = pair_rows(middle_grad.astype(bf16))
+    out_term = contract_rows(middle_rows, mixed_rows)
+    mixed_cot = (
+        jnp.dot(middle_rows, output_full, preferred_element_type=f32)
+        .astype(bf16)
+        .reshape(seq_rows, local_heads, HD)
+    )
+    value_cot = jnp.einsum("hst,shd->thd", soft_rounded, mixed_cot, preferred_element_type=f32)
+    value_cot = value_cot.astype(bf16).reshape(seq_rows, head_cols)
+    soft_cot = jnp.einsum("shd,thd->hst", mixed_cot, value_rows, preferred_element_type=f32)
+    score_cot = (
+        soft_weights
+        * (soft_cot - jnp.sum(soft_weights * soft_cot, axis=2, keepdims=True))
+        * inv_root
+    ).astype(bf16)
+    query_cot = (
+        jnp.einsum("hst,thd->shd", score_cot, key_rows, preferred_element_type=f32)
+        .astype(bf16)
+        .reshape(seq_rows, head_cols)
+    )
+    key_cot = (
+        jnp.einsum("hst,shd->thd", score_cot, query_rows, preferred_element_type=f32)
+        .astype(bf16)
+        .reshape(seq_rows, head_cols)
+    )
+    first_terms = (
+        contract_cols(query_cot, query_full)
+        + contract_cols(key_cot, key_full)
+        + contract_cols(value_cot, value_full)
+    )
+    first_cot = pair_sums(first_terms)
+    weighted_one = first_cot * first_gain
+    first_term = jnp.sum(first_cot * block_input * first_scale, axis=0)
+    input_grad = middle_grad + first_scale * (
+        weighted_one
+        - block_input
+        * first_scale
+        * first_scale
+        * jnp.mean(weighted_one * block_input, axis=1, keepdims=True)
+    )
+
+    def owner_grad(term):
+        return lax.psum_scatter(
+            term.astype(bf16), "fsdp", scatter_dimension=0, tiled=True
+        ).astype(f32)
+
+    query_grad = owner_grad(contract_rows(normed_rows, query_cot))
+    key_grad = owner_grad(contract_rows(normed_rows, key_cot))
+    value_grad = owner_grad(contract_rows(normed_rows, value_cot))
+    output_grad = owner_grad(out_term)
+    first_gain_grad, second_gain_grad = lax.psum((first_term, second_term), ("fsdp", "tp"))
+    return (
+        block_output,
+        input_grad,
+        first_gain_grad,
+        second_gain_grad,
+        query_grad,
+        key_grad,
+        value_grad,
+        output_grad,
+        gate_grad[None],
+        up_grad[None],
+        down_grad[None],
+        route_grad,
+    )
+
+
 def solution(mesh):
+    dense = 2 * TOP >= EXP_DEV * mesh.shape["fsdp"]
+    per_device = per_device_dense if dense else per_device_slots
     in_specs = (
         P(("fsdp", "tp"), None),
         P(("fsdp", "tp"), None),

time: 2040 us -> 1450 us (0.71)
  waiting for transfers between devices: 1470 us -> 1110 us
  starting transfers between devices: 168 us -> 5.04 us
  local copies, waits for them, and re-layouts: 79.6 us -> 17.7 us
  other arithmetic: 62.9 us -> 38.6 us
    all_to_all x4 -> x1, waiting for transfers between devices: 745 us -> 6.26 us  [per_device_dense(): lax.all_to_all(route_sums.reshape(owner_count, local_rows), 'fsdp', split...]
    all_gather x1 -> x5, waiting for transfers between devices: 34.8 us -> 293 us  [the longest x1 77.1 us: per_device_dense(): lax.all_gather(upstream_grad.astype(bf16), 'fsdp', axis=0, tiled=True)]
    all_to_all x4 -> x1, starting transfers between devices: 166 us -> 3.47 us  [per_device_dense(): lax.all_to_all(route_sums.reshape(owner_count, local_rows), 'fsdp', split...]
    reduce_scatter x5 -> x9, waiting for transfers between devices: 412 us -> 538 us  [the longest x4 295 us: owner_grad(): lax.psum_scatter(term.astype(bf16), 'fsdp', scatter_dimension=0, tiled=True)]
    gather x2 -> x0, local copies, waits for them, and re-layouts: 45.8 us -> none  [the longest x1 23 us: per_device(): came_back[slot_index].reshape(seq_rows, TOP, model_width)]
    psum x1, blocking collectives: 66.9 us -> 39.7 us  [per_device_dense(): lax.psum((first_term, second_term), ('fsdp', 'tp'))]
    convert_element_type x5 -> x10, other arithmetic: 5.93 us -> 28.3 us  [the longest x1 10.9 us: per_device_dense(): up_cot = (hidden_cot * gate_act * sigmoid_gate).astype(bf16)]
    dot_general x19, matrix products: 146 us -> 168 us  [the longest x1 19.5 us: per_device_dense(): jnp.einsum('td,gfd->gtf', upstream_all, down_pair, preferred_element_type...]
  transfers between devices with their start and end apart: 21 -> 23, of which waited for: 18 -> 21; matrix products, arithmetic and copies ran while one was open for 12% -> 12% of each run, Pallas kernels for 0% -> 0%
where the time goes in v1:
time: 1450 us; the launch traced here: 1440 us
  waiting for transfers between devices  1110 us (77%)
  matrix products  194 us (13%)
  blocking collectives  57.6 us (4%)
  other arithmetic  38.6 us (3%)
  local copies, waits for them, and re-layouts  17.7 us (1%)
  between operations  15.2 us (1%)
    reduce_scatter x4, waiting for transfers between devices, owner_grad(): lax.psum_scatter(term.astype(bf16), 'fsdp', scatter_dimension=0, tiled=True)  295 us
    reduce_scatter x1, waiting for transfers between devices, per_device_dense(): lax.psum_scatter(input_cot.astype(bf16), 'fsdp', scatter_dimension=0, til...  102 us
    all_gather x1, waiting for transfers between devices, per_device_dense(): lax.all_gather(upstream_grad.astype(bf16), 'fsdp', axis=0, tiled=True)  77.1 us
    all_gather x1, waiting for transfers between devices, per_device_dense(): rows_all = lax.all_gather(second_normed, 'fsdp', axis=0, tiled=True)  77.1 us
    reduce_scatter x3, waiting for transfers between devices, pair_grad(): lax.psum_scatter(part.astype(bf16), 'tp', scatter_dimension=0).astype(f32)  75.2 us
    reduce_scatter x1, waiting for transfers between devices, per_device_dense(): lax.psum_scatter(mixture_part.astype(bf16), 'fsdp', scatter_dimension=0,...  66.1 us
    reduce_scatter x2, waiting for transfers between devices, pair_sums(): return lax.psum_scatter(term_block, 'tp', scatter_dimension=0, tiled=True)  59.7 us
    all_gather x1, waiting for transfers between devices, per_device_dense(): up_pair = lax.all_gather(up_weight[0], 'tp', axis=0)  53.3 us
  transfers between devices with their start and end apart: 23, of which 21 were waited for; matrix products, arithmetic and copies ran while one was open for 12% of the time, Pallas kernels for 0%

profile of v1, /device:TPU:0, one launch (start us, length us, event | category | flops | bytes accessed | tf_op | source)
XLA Modules:
  0.0 1440.4 jit_solution(6409855540423342245)
XLA Ops:
  13.5 21.4 %all-gather.12.cloned.1.call-done = bf16[256,2048]{1,0:T(8,128)(2,1)} async-done(((bf16[128,2048]{1,0:T(8,128)(2,1)}), bf16[256,2048]{1,0:T(8,128)(2,1)}) %all-gather.12.cloned.1.call-update) | async-done | bytes 1048592 | tf_op jit(solution)/shard_map/all_gather | solution.py:25
  35.0 52.6 %all-gather.18.cloned.1.call-done = bf16[2048,1024]{1,0:T(8,128)(2,1)} async-done(((bf16[128,1024]{1,0:T(8,128)(2,1)}), bf16[2048,1024]{1,0:T(8,128)(2,1)}) %all-gather.18.cloned.1.call-update) | async-done | bytes 4194320 | tf_op jit(solution)/shard_map/all_gather | solution.py:43
  92.3 46.3 %all-gather.16.cloned.1.call-done = bf16[2048,1024]{1,0:T(8,128)(2,1)} async-done(((bf16[128,1024]{1,0:T(8,128)(2,1)}), bf16[2048,1024]{1,0:T(8,128)(2,1)}) %all-gather.16.cloned.1.call-update) | async-done | bytes 4194320 | tf_op jit(solution)/shard_map/all_gather | solution.py:42
  145.3 44.4 %all-gather.14.cloned.1.call-done = bf16[2048,1024]{1,0:T(8,128)(2,1)} async-done(((bf16[128,1024]{1,0:T(8,128)(2,1)}), bf16[2048,1024]{1,0:T(8,128)(2,1)}) %all-gather.14.cloned.1.call-update) | async-done | bytes 4194320 | tf_op jit(solution)/shard_map/all_gather | solution.py:44
  194.5 46.1 %all-gather.20.cloned.1.call-done = bf16[2048,1024]{1,0:T(8,128)(2,1)} async-done(((bf16[128,1024]{1,0:T(8,128)(2,1)}), bf16[2048,1024]{1,0:T(8,128)(2,1)}) %all-gather.20.cloned.1.call-update) | async-done | bytes 4194320 | tf_op jit(solution)/shard_map/all_gather | solution.py:45
  246.4 29.8 %reduce-scatter.12.cloned.1.call-done = f32[128,2048]{1,0:T(8,128)} async-done(((f32[256,2048]{1,0:T(8,128)}), f32[128,2048]{1,0:T(8,128)}) %reduce-scatter.12.cloned.1.call-update) | async-done | bytes 1048592 | tf_op jit(solution)/shard_map/reduce_scatter | solution.py:29
  281.2 53.3 %all-gather.26.cloned.1.call-done = bf16[2,2048,512]{2,1,0:T(8,128)(2,1)} async-done(((bf16[1,2048,512]{2,1,0:T(8,128)(2,1)}), bf16[2,2048,512]{2,1,0:T(8,128)(2,1)}) %all-gather.26.cloned.1.call-update) | async-done | bytes 4194320 | tf_op jit(solution)/shard_map/all_gather | solution.py:335
  334.4 77.1 %all-gather.22.cloned.1.call-done = bf16[2048,2048]{1,0:T(8,128)(2,1)} async-done(((bf16[128,2048]{1,0:T(8,128)(2,1)}), bf16[2048,2048]{1,0:T(8,128)(2,1)}) %all-gather.22.cloned.1.call-update) | async-done | bytes 8388624 | tf_op jit(solution)/shard_map/all_gather | solution.py:365
  411.5 14.5 %fusion.20 = f32[2048,2,512]{0,2,1:T(8,128)} fusion(bf16[2,2048,512]{2,1,0:T(8,128)(2,1)} %all-gather.26.cloned.1.call-done, bf16[2048,2048]{1,0:T(8,128)(2,1)} %all-gather.22.cloned.1.call-done), kind=kOutput, calls=%fused_computation.30 | convolution fusion | flops 8589934592 | bytes 20971520 | tf_op jit(solution)/shard_map/td,gdf->gtf/dot_general | solution.py:367
  426.0 42.4 %all-gather.24.cloned.1.call-done = bf16[2,2048,512]{2,1,0:T(8,128)(2,1)} async-done(((bf16[1,2048,512]{2,1,0:T(8,128)(2,1)}), bf16[2,2048,512]{2,1,0:T(8,128)(2,1)}) %all-gather.24.cloned.1.call-update) | async-done | bytes 4194320 | tf_op jit(solution)/shard_map/all_gather | solution.py:334
  468.4 14.6 %fusion.22 = f32[2048,2,512]{0,2,1:T(8,128)} fusion(bf16[2,2048,512]{2,1,0:T(8,128)(2,1)} %all-gather.24.cloned.1.call-done, bf16[2048,2048]{1,0:T(8,128)(2,1)} %all-gather.22.cloned.1.call-done), kind=kOutput, calls=%fused_computation.32 | convolution fusion | flops 8589934592 | bytes 20971520 | tf_op jit(solution)/shard_map/td,gdf->gtf/dot_general | solution.py:366
  483.0 43.6 %all-gather.28.cloned.1.call-done = bf16[2,512,2048]{2,1,0:T(8,128)(2,1)} async-done(((bf16[1,512,2048]{2,1,0:T(8,128)(2,1)}), bf16[2,512,2048]{2,1,0:T(8,128)(2,1)}) %all-gather.28.cloned.1.call-update) | async-done | bytes 4194320 | tf_op jit(solution)/shard_map/all_gather | solution.py:336
  526.5 77.1 %all-gather.30.cloned.1.call-done = bf16[2048,2048]{1,0:T(8,128)(2,1)} async-done(((bf16[128,2048]{1,0:T(8,128)(2,1)}), bf16[2048,2048]{1,0:T(8,128)(2,1)}) %all-gather.30.cloned.1.call-update) | async-done | bytes 8388624 | tf_op jit(solution)/shard_map/all_gather | solution.py:337
  603.6 19.5 %fusion.2 = (f32[2048]{0:T(1024)}, f32[2,512,2048]{2,1,0:T(8,128)}) fusion(f32[2048,2,512]{0,2,1:T(8,128)} %fusion.20, f32[2048,2,512]{0,2,1:T(8,128)} %fusion.22, bf16[2,512,2048]{2,1,0:T(8,128)(2,1)} %all-gather.28.cloned.1.call-done, bf16[2048,2048]{1,0:T(8,128)(2,1)} %all-gather.30.cloned.1.call-done), kind=kOutput, calls=%fused_computation.6 | convolution fusion | flops 8604612608 | bytes 37756928 | tf_op jit(solution)/shard_map/td,gfd->gtf/dot_general | solution.py:372
  633.5 17.9 %all_gather.44 = f32[2048,16]{0,1:T(8,128)S(1)} all-gather(f32[128,16]{0,1:T(8,128)S(1)} %get-tuple-element.65), channel_id=1, replica_groups=mesh['fsdp'=16,'tp'=2] {'fsdp'}, dimensions={0}, use_global_device_ids=true | all-gather | bytes 139264 | tf_op jit(solution)/shard_map/all_gather | solution.py:327
  651.5 10.9 fusion.15
  662.4 11.7 fusion.74
  674.1 15.8 %fusion.1 = bf16[2048,2048]{1,0:T(8,128)(2,1)} fusion(f32[2048,2048,1]{1,0,2:T(8,128)} %fusion.74, bf16[2,2048,512]{1,2,0:T(8,128)(2,1)S(1)} %get-tuple-element.70, bf16[2,2048,512]{2,1,0:T(8,128)(2,1)} %all-gather.26.cloned.1.call-done), kind=kOutput, calls=%fused_computation.2 | convolution fusion | flops 8598323200 | bytes 33554432 | tf_op jit(solution)/shard_map/gtf,gdf->td/dot_general | solution.py:380
  689.9 101.7 %reduce-scatter.16.cloned.1.call-done = bf16[128,2048]{1,0:T(8,128)(2,1)} async-done(((bf16[2048,2048]{1,0:T(8,128)(2,1)}), bf16[128,2048]{1,0:T(8,128)(2,1)}) %reduce-scatter.16.cloned.1.call-update) | async-done | bytes 524304 | tf_op jit(solution)/shard_map/reduce_scatter | solution.py:381
  795.3 16.7 %fusion.28 = bf16[2,512,2048]{2,1,0:T(8,128)(2,1)} fusion(bf16[2048,2048]{1,0:T(8,128)(2,1)} %all-gather.30.cloned.1.call-done, f32[2048]{0:T(1024)S(1)} %select_reduce_fusion, f32[2048,2,512]{0,2,1:T(8,128)} %fusion.20, f32[2048,2,512]{0,2,1:T(8,128)} %fusion.22), kind=kOutput, calls=%fused_computation.37 | convolution fusion | flops 8606711808 | bytes 29368320 | tf_op jit(solution)/shard_map/gtf,td->gfd/dot_general | solution.py:394
  812.1 13.8 convert_bitcast_fusion
  826.0 13.8 convert_bitcast_fusion.1
  869.8 16.3 %bitcast_convert_fusion = bf16[2048,2048]{1,0:T(8,128)(2,1)} fusion(bf16[2,512,2048]{2,1,0:T(8,128)(2,1)} %all-gather.28.cloned.1.call-done, f32[2048]{0:T(1024)S(1)} %select_reduce_fusion, f32[2048,2,512]{0,2,1:T(8,128)} %fusion.20, f32[2048,2,512]{0,2,1:T(8,128)} %fusion.22), kind=kOutput, calls=%fused_computation.3 | convolution fusion | flops 8608808960 | bytes 29368320 | tf_op jit(solution)/shard_map/gtf,gfd->td/dot_general | solution.py:371
  907.3 22.1 %reduce-scatter.30.cloned.1.call-done = bf16[1,2048,512]{1,2,0:T(8,128)(2,1)} async-done(((bf16[2,2048,512]{1,2,0:T(8,128)(2,1)}), bf16[1,2048,512]{1,2,0:T(8,128)(2,1)}) %reduce-scatter.30.cloned.1.call-update) | async-done | bytes 2097168 | tf_op jit(solution)/shard_map/reduce_scatter | solution.py:399
  933.6 53.0 %reduce-scatter.28.cloned.1.call-done = bf16[1,2048,512]{1,2,0:T(8,128)(2,1)} async-done(((bf16[2,2048,512]{1,2,0:T(8,128)(2,1)}), bf16[1,2048,512]{1,2,0:T(8,128)(2,1)}) %reduce-scatter.28.cloned.1.call-update) | async-done | bytes 2097168 | tf_op jit(solution)/shard_map/reduce_scatter | solution.py:399
  990.7 29.9 %reduce-scatter.18.cloned.1.call-done = f32[128,2048]{1,0:T(8,128)} async-done(((f32[256,2048]{1,0:T(8,128)}), f32[128,2048]{1,0:T(8,128)}) %reduce-scatter.18.cloned.1.call-update) | async-done | bytes 1048592 | tf_op jit(solution)/shard_map/reduce_scatter | solution.py:29
  1022.2 39.7 %all-reduce = (f32[2048]{0:T(1024)}, f32[2048]{0:T(1024)}) all-reduce(f32[2048]{0:T(1024)S(1)} %get-tuple-element.60, f32[2048]{0:T(1024)S(1)} %get-tuple-element.62), channel_id=1, replica_groups=mesh['fsdp'=16,'tp'=2] {'fsdp','tp'}, use_global_device_ids=true, to_apply=%region_14.15 | all-reduce | flops 4096 | bytes 32768 | tf_op jit(solution)/shard_map/psum | solution.py:462
  1061.9 66.1 %reduce-scatter.14.cloned.1.call-done = bf16[128,2048]{1,0:T(8,128)(2,1)} async-done(((bf16[2048,2048]{1,0:T(8,128)(2,1)}), bf16[128,2048]{1,0:T(8,128)(2,1)}) %reduce-scatter.14.cloned.1.call-update) | async-done | bytes 524304 | tf_op jit(solution)/shard_map/reduce_scatter | solution.py:384
  1131.4 73.0 %reduce-scatter.26.cloned.1.call-done = bf16[128,1024]{1,0:T(8,128)(2,1)} async-done(((bf16[2048,1024]{1,0:T(8,128)(2,1)}), bf16[128,1024]{1,0:T(8,128)(2,1)}) %reduce-scatter.26.cloned.1.call-update) | async-done | bytes 262160 | tf_op jit(solution)/shard_map/reduce_scatter | solution.py:454
  1206.2 73.8 %reduce-scatter.24.cloned.1.call-done = bf16[128,1024]{1,0:T(8,128)(2,1)} async-done(((bf16[2048,1024]{1,0:T(8,128)(2,1)}), bf16[128,1024]{1,0:T(8,128)(2,1)}) %reduce-scatter.24.cloned.1.call-update) | async-done | bytes 262160 | tf_op jit(solution)/shard_map/reduce_scatter | solution.py:454
  1281.7 73.9 %reduce-scatter.22.cloned.1.call-done = bf16[128,1024]{1,0:T(8,128)(2,1)} async-done(((bf16[2048,1024]{1,0:T(8,128)(2,1)}), bf16[128,1024]{1,0:T(8,128)(2,1)}) %reduce-scatter.22.cloned.1.call-update) | async-done | bytes 262160 | tf_op jit(solution)/shard_map/reduce_scatter | solution.py:454
  1357.5 73.8 %reduce-scatter.20.cloned.1.call-done = bf16[128,1024]{1,0:T(8,128)(2,1)} async-done(((bf16[2048,1024]{1,0:T(8,128)(2,1)}), bf16[128,1024]{1,0:T(8,128)(2,1)}) %reduce-scatter.20.cloned.1.call-update) | async-done | bytes 262160 | tf_op jit(solution)/shard_map/reduce_scatter | solution.py:454
  (156 shorter events, 118.7 us)
Async XLA Ops:
  7.2 273.9 %copy-start = (s32[256,8]{0,1:T(8,128)S(1)}, s32[256,8]{0,1:T(8,128)}, u32[]{:S(2)}) copy-start(s32[256,8]{0,1:T(8,128)} %param.24) | copy-start | bytes 24580
  7.2 27.8 %all-gather.12.cloned.1.call-start = ((), (), s32[]{:S(2)}) async-start(), calls=%async_computation.12 | async-start | bytes 1572864 | tf_op jit(solution)/shard_map/all_gather | solution.py:25
  10.8 76.7 %all-gather.18.cloned.1.call-start = ((), (), s32[]{:S(2)}) async-start(), calls=%async_computation.15 | async-start | bytes 4456448 | tf_op jit(solution)/shard_map/all_gather | solution.py:43
  11.6 127.1 %all-gather.16.cloned.1.call-start = ((), (), s32[]{:S(2)}) async-start(), calls=%async_computation.14 | async-start | bytes 4456448 | tf_op jit(solution)/shard_map/all_gather | solution.py:42
  12.3 177.3 %all-gather.14.cloned.1.call-start = ((), (), s32[]{:S(2)}) async-start(), calls=%async_computation.13 | async-start | bytes 4456448 | tf_op jit(solution)/shard_map/all_gather | solution.py:44
  12.9 227.7 %all-gather.20.cloned.1.call-start = ((), (), s32[]{:S(2)}) async-start(), calls=%async_computation.16 | async-start | bytes 4456448 | tf_op jit(solution)/shard_map/all_gather | solution.py:45
  13.5 262.6 %reduce-scatter.12.cloned.1.call-start = ((), (), s32[]{:S(2)}) async-start(), calls=%async_computation.17 | async-start | bytes 3145728 | tf_op jit(solution)/shard_map/reduce_scatter | solution.py:29
  35.0 103.7 %copy-start.6 = (bf16[256,2048]{1,0:T(8,128)(2,1)S(1)}, bf16[256,2048]{1,0:T(8,128)(2,1)}, u32[]{:S(2)}) copy-start(bf16[256,2048]{1,0:T(8,128)(2,1)} %all-gather.12.cloned.1.call-done) | copy-start | bytes 3145732
  145.3 49.2 %copy-start.23 = (f32[8,256]{1,0:T(8,128)}, f32[8,256]{1,0:T(8,128)S(1)}, u32[]{:S(2)}) copy-start(f32[8,256]{1,0:T(8,128)S(1)} %log_add_fusion) | copy-start | bytes 24580
  194.5 51.0 %copy-start.18 = (bf16[8,128,256]{2,1,0:T(8,128)(2,1)}, bf16[8,128,256]{2,1,0:T(8,128)(2,1)S(1)}, u32[]{:S(2)}) copy-start(bf16[8,128,256]{2,1,0:T(8,128)(2,1)S(1)} %convolution_convert_fusion.5) | copy-start | bytes 1572868
  245.6 88.9 %all-gather.26.cloned.1.call-start = ((), (), s32[]{:S(2)}) async-start(), calls=%async_computation.20 | async-start | bytes 6291456 | tf_op jit(solution)/shard_map/all_gather | solution.py:335
  246.3 165.2 %all-gather.22.cloned.1.call-start = ((), (), s32[]{:S(2)}) async-start(), calls=%async_computation.18 | async-start | bytes 8912896 | tf_op jit(solution)/shard_map/all_gather | solution.py:365
  278.6 189.8 %all-gather.24.cloned.1.call-start = ((), (), s32[]{:S(2)}) async-start(), calls=%async_computation.19 | async-start | bytes 6291456 | tf_op jit(solution)/shard_map/all_gather | solution.py:334
  279.4 247.2 %all-gather.28.cloned.1.call-start = ((), (), s32[]{:S(2)}) async-start(), calls=%async_computation.21 | async-start | bytes 6291456 | tf_op jit(solution)/shard_map/all_gather | solution.py:336
  280.0 323.7 %all-gather.30.cloned.1.call-start = ((), (), s32[]{:S(2)}) async-start(), calls=%async_computation.23 | async-start | bytes 8912896 | tf_op jit(solution)/shard_map/all_gather | solution.py:337
  623.1 9.8 all-to-all-start
  626.6 165.1 %reduce-scatter.16.cloned.1.call-start = ((), (), s32[]{:S(2)}) async-start(), calls=%async_computation.24 | async-start | bytes 8912896 | tf_op jit(solution)/shard_map/reduce_scatter | solution.py:381
  689.9 150.3 %all-gather.32.cloned.1.call-start = ((), (), s32[]{:S(2)}) async-start(), calls=%async_computation.25 | async-start | bytes 1572864 | tf_op jit(solution)/shard_map/all_gather | solution.py:25
  795.3 107.9 %reduce-scatter.32.cloned.1.call-start = ((), (), s32[]{:S(2)}) async-start(), calls=%async_computation.33 | async-start | bytes 6291456 | tf_op jit(solution)/shard_map/reduce_scatter | solution.py:399
  812.1 117.4 %reduce-scatter.30.cloned.1.call-start = ((), (), s32[]{:S(2)}) async-start(), calls=%async_computation.32 | async-start | bytes 6291456 | tf_op jit(solution)/shard_map/reduce_scatter | solution.py:399
  826.0 160.6 %reduce-scatter.28.cloned.1.call-start = ((), (), s32[]{:S(2)}) async-start(), calls=%async_computation.31 | async-start | bytes 6291456 | tf_op jit(solution)/shard_map/reduce_scatter | solution.py:399
  839.9 180.8 %reduce-scatter.18.cloned.1.call-start = ((), (), s32[]{:S(2)}) async-start(), calls=%async_computation.26 | async-start | bytes 3145728 | tf_op jit(solution)/shard_map/reduce_scatter | solution.py:29
  869.5 258.6 %reduce-scatter.14.cloned.1.call-start = ((), (), s32[]{:S(2)}) async-start(), calls=%async_computation.22 | async-start | bytes 8912896 | tf_op jit(solution)/shard_map/reduce_scatter | solution.py:384
  886.1 318.3 %reduce-scatter.26.cloned.1.call-start = ((), (), s32[]{:S(2)}) async-start(), calls=%async_computation.30 | async-start | bytes 4456448 | tf_op jit(solution)/shard_map/reduce_scatter | solution.py:454
  890.7 389.2 %reduce-scatter.24.cloned.1.call-start = ((), (), s32[]{:S(2)}) async-start(), calls=%async_computation.29 | async-start | bytes 4456448 | tf_op jit(solution)/shard_map/reduce_scatter | solution.py:454
  895.4 460.3 %reduce-scatter.22.cloned.1.call-start = ((), (), s32[]{:S(2)}) async-start(), calls=%async_computation.28 | async-start | bytes 4456448 | tf_op jit(solution)/shard_map/reduce_scatter | solution.py:454
  898.8 532.5 %reduce-scatter.20.cloned.1.call-start = ((), (), s32[]{:S(2)}) async-start(), calls=%async_computation.27 | async-start | bytes 4456448 | tf_op jit(solution)/shard_map/reduce_scatter | solution.py:454
  933.6 87.0 %copy-start.5 = (f32[128,2048]{1,0:T(8,128)S(1)}, f32[128,2048]{1,0:T(8,128)}, u32[]{:S(2)}) copy-start(f32[128,2048]{1,0:T(8,128)} %param.13) | copy-start | bytes 3145732
  933.6 87.0 %copy-start.25 = (f32[2048]{0:T(1024)S(1)}, f32[2048]{0:T(1024)}, u32[]{:S(2)}) copy-start(f32[2048]{0:T(1024)} %param.15) | copy-start | bytes 24580
  933.6 87.0 %copy-start.27 = (f32[128]{0:T(128)S(1)}, f32[128]{0:T(128)}, u32[]{:S(2)}) copy-start(f32[128]{0:T(128)} %copy-done.26) | copy-start | bytes 1540
  933.6 194.4 %copy-start.9 = (f32[128,2048]{1,0:T(8,128)S(1)}, f32[128,2048]{1,0:T(8,128)}, u32[]{:S(2)}) copy-start(f32[128,2048]{1,0:T(8,128)} %param.14) | copy-start | bytes 3145732
  1061.9 371.2 %copy-start.1 = (s32[256,8]{0,1:T(8,128)S(1)}, s32[256,8]{0,1:T(8,128)}, u32[]{:S(2)}) copy-start(s32[256,8]{0,1:T(8,128)} %param.24) | copy-start | bytes 24580
  (21 other events, 235.2 us)
Sparse Core Ops, SparseCore 0:
  11.0 23.9 all-gather.11
  37.2 50.3 all-gather.17
  89.7 48.8 all-gather.15
  140.7 48.8 all-gather.13
  191.6 48.8 all-gather.19
  245.7 30.4 reduce-scatter.11
  277.7 56.7 all-gather.25
  337.2 74.2 all-gather.21
  413.1 55.2 all-gather.23
  469.8 56.7 all-gather.27
  529.3 74.2 all-gather.29
  690.0 101.6 reduce-scatter.15
  795.4 20.9 all-gather.31
  818.5 54.3 reduce-scatter.31
  875.1 54.3 reduce-scatter.29
  932.2 54.3 reduce-scatter.27
  988.7 31.8 reduce-scatter.17
  1024.6 103.4 reduce-scatter.13
  1131.9 72.4 reduce-scatter.25
  1208.1 71.8 reduce-scatter.23
  1283.8 71.8 reduce-scatter.21
  1359.5 71.7 reduce-scatter.19

commit v2 on v1

--- a/solution.py
+++ b/solution.py
@@ -1,6 +1,10 @@
+import functools
+
 import jax
 import jax.numpy as jnp
 from jax import lax
+from jax.experimental import pallas as pl
+from jax.experimental.pallas import tpu as pltpu
 from jax.sharding import PartitionSpec as P
 
 HD = 128
@@ -287,6 +291,363 @@
     )
 
 
+MESH = pl.DeviceIdType.MESH
+
+
+def place():
+    here = lax.axis_index("fsdp")
+    return here // 4, (here // 2) % 2, here % 2, lax.axis_index("tp")
+
+
+def index_of(z, y, c):
+    return (z * 2 + y) * 2 + c
+
+
+LEVELS = 4
+LEVEL_ORDER = tuple(
+    sum(level << (2 * z) for z, level in enumerate(turn))
+    for turn in ((3, 3, 0, 0), (2, 2, 1, 1), (1, 0, 3, 2), (0, 1, 2, 3))
+)
+
+
+def level_at(turn, z):
+    return (LEVEL_ORDER[turn] >> (2 * z)) % 4
+
+
+def line_ends(z):
+    return (z + 1) // LEVELS, (LEVELS - z) // LEVELS
+
+
+def plane_greet():
+    z, y, c, x = place()
+    top, bottom = line_ends(z)
+    barrier = pltpu.get_barrier_semaphore()
+    for partner in ((index_of(z, 1 - y, c), x), (index_of(z, y, 1 - c), x)):
+        pl.semaphore_signal(barrier, inc=1, device_id=partner, device_id_type=MESH)
+
+    @pl.when(top == 0)
+    def _():
+        above = (index_of(z + 1, y, c), x)
+        pl.semaphore_signal(barrier, inc=1, device_id=above, device_id_type=MESH)
+
+    @pl.when(bottom == 0)
+    def _():
+        below = (index_of(z - 1, y, c), x)
+        pl.semaphore_signal(barrier, inc=1, device_id=below, device_id_type=MESH)
+
+    pl.semaphore_wait(barrier, 4 - top - bottom)
+
+
+def remote(src, dst, send_sem, recv_sem, target):
+    return pltpu.make_async_remote_copy(
+        src_ref=src,
+        dst_ref=dst,
+        send_sem=send_sem,
+        recv_sem=recv_sem,
+        device_id=target,
+        device_id_type=MESH,
+    )
+
+
+class PlaneGather:
+    def __init__(self, mine, full, send_sems, recv_sems):
+        self.mine, self.full = mine, full
+        self.send_sems, self.recv_sems = send_sems, recv_sems
+        self.z, self.y, self.c, self.x = place()
+        self.top, self.bottom = line_ends(self.z)
+        self.sent = []
+
+    def _send(self, src, slot, target, unless=None):
+        k = len(self.sent)
+        copy = remote(
+            src, self.full.at[slot], self.send_sems.at[k], self.recv_sems.at[slot], target
+        )
+        if unless is None:
+            copy.start()
+        else:
+            pl.when(unless == 0)(copy.start)
+        self.sent.append((copy, unless))
+
+    def arrived(self, slot):
+        here = self.full.at[slot]
+        k = self.send_sems.shape[0] - 1
+        remote(here, here, self.send_sems.at[k], self.recv_sems.at[slot], (0, self.x)).wait_recv()
+
+    def start(self):
+        z, y, c, x = self.z, self.y, self.c, self.x
+        own = index_of(z, y, c)
+        self._send(self.mine, own, (index_of(z + 1, y, c), x), self.top)
+        self._send(self.mine, own, (index_of(z - 1, y, c), x), self.bottom)
+        self._send(self.mine, own, (index_of(z, 1 - y, c), x))
+        self._send(self.mine, own, (index_of(z, y, 1 - c), x))
+
+    def from_line(self, step):
+        z, y, c, x = self.z, self.y, self.c, self.x
+        level = level_at(3 - step, z)
+        slot = index_of(level, y, c)
+        self.arrived(slot)
+        onward = z + 1 - 2 * ((level + LEVELS - z) // LEVELS)
+        self._send(self.full.at[slot], slot, (index_of(onward, y, c), x), self.top + self.bottom)
+        self._send(self.full.at[slot], slot, (index_of(z, 1 - y, c), x))
+        self._send(self.full.at[slot], slot, (index_of(z, y, 1 - c), x))
+
+    def from_side(self, step):
+        z, y, c, x = self.z, self.y, self.c, self.x
+        slot = index_of(level_at(3 - step, z), 1 - y, c)
+        self.arrived(slot)
+        self._send(self.full.at[slot], slot, (index_of(z, y, 1 - c), x))
+
+    def from_core(self, step, side):
+        z, y, c = self.z, self.y, self.c
+        self.arrived(index_of(level_at(3 - step, z), (y + side) % 2, 1 - c))
+
+    def finish(self):
+        for copy, unless in self.sent:
+            if unless is None:
+                copy.wait_send()
+            else:
+                pl.when(unless == 0)(copy.wait_send)
+
+
+GATHER_SENDS = 18
+
+
+def gather_kernel(count, *refs):
+    mine, full = refs[:count], refs[count : 2 * count]
+    send_sems, recv_sems, own_sems = refs[2 * count :]
+    z, y, c, x = place()
+    plane_greet()
+    own = index_of(z, y, c)
+    plans = [
+        PlaneGather(mine[a], full[a], send_sems.at[a], recv_sems.at[a]) for a in range(count)
+    ]
+    kept = [
+        pltpu.make_async_copy(mine[a], full[a].at[own], own_sems.at[a]) for a in range(count)
+    ]
+    for plan in plans:
+        plan.start()
+    for copy in kept:
+        copy.start()
+    for step in range(1, LEVELS):
+        for plan in plans:
+            plan.from_line(step)
+        for plan in plans:
+            plan.from_side(step - 1)
+    for plan in plans:
+        plan.from_side(LEVELS - 1)
+    for plan in plans:
+        for step in range(LEVELS):
+            for side in range(2):
+                plan.from_core(step, side)
+    for plan in plans:
+        plan.finish()
+    for copy in kept:
+        copy.wait()
+
+
+def plane_gather(arrays, collective_id, name):
+    owner_count = lax.axis_size("fsdp")
+    count = len(arrays)
+    nbytes = sum(a.size * a.dtype.itemsize for a in arrays)
+    return pl.pallas_call(
+        functools.partial(gather_kernel, count),
+        out_shape=[jax.ShapeDtypeStruct((owner_count,) + a.shape, a.dtype) for a in arrays],
+        in_specs=[pl.BlockSpec(memory_space=pltpu.VMEM)] * count,
+        out_specs=[pl.BlockSpec(memory_space=pl.ANY)] * count,
+        scratch_shapes=[
+            pltpu.SemaphoreType.DMA((count, GATHER_SENDS)),
+            pltpu.SemaphoreType.DMA((count, owner_count)),
+            pltpu.SemaphoreType.DMA((count,)),
+        ],
+        compiler_params=pltpu.CompilerParams(collective_id=collective_id, has_side_effects=True),
+        cost_estimate=pl.CostEstimate(
+            flops=0, bytes_accessed=owner_count * nbytes * 4, transcendentals=0
+        ),
+        name=name,
+    )(*arrays)
+
+
+class PlaneSums:
+    def __init__(self, own_parts, from_core, from_side, from_line, sems):
+        self.own, self.from_core = own_parts, from_core
+        self.from_side, self.from_line = from_side, from_line
+        self.core_s, self.core_r, self.side_s, self.side_r, self.line_s, self.line_r = sems
+        self.z, self.y, self.c, self.x = place()
+        self.top, self.bottom = line_ends(self.z)
+        self.sent = []
+
+    def slot_of(self, turn, side, core):
+        return index_of(level_at(turn, self.z), (self.y + side) % 2, (self.c + core) % 2)
+
+    def to_core(self, part, turn, side):
+        j = side * LEVELS + turn
+        copy = remote(
+            part,
+            self.from_core.at[j],
+            self.core_s.at[j],
+            self.core_r.at[j],
+            (index_of(self.z, self.y, 1 - self.c), self.x),
+        )
+        copy.start()
+        self.sent.append(copy)
+
+    def core_arrived(self, turn, side):
+        j = side * LEVELS + turn
+        here = self.from_core.at[j]
+        remote(here, here, self.core_s.at[j], self.core_r.at[j], (0, self.x)).wait_recv()
+
+    def to_side(self, turn):
+        copy = remote(
+            self.own.at[LEVELS + turn],
+            self.from_side.at[turn],
+            self.side_s.at[turn],
+            self.side_r.at[turn],
+            (index_of(self.z, 1 - self.y, self.c), self.x),
+        )
+        copy.start()
+        self.sent.append(copy)
+
+    def side_arrived(self, turn):
+        here = self.from_side.at[turn]
+        remote(here, here, self.side_s.at[turn], self.side_r.at[turn], (0, self.x)).wait_recv()
+
+    def line_arrived(self, slot):
+        here = self.from_line.at[slot]
+        remote(here, here, self.line_s.at[0], self.line_r.at[slot], (0, self.x)).wait_recv()
+
+    def to_line(self, turn, add):
+        z, y, c, x = self.z, self.y, self.c, self.x
+        level = level_at(turn, z)
+
+        @pl.when(self.top + self.bottom == 0)
+        def _():
+            self.line_arrived(level)
+            add(self.own.at[turn], self.from_line.at[level])
+
+        down = (z + LEVELS - level) // (LEVELS + 1)
+        onward = z + 1 - 2 * down
+        reached = 1 - jnp.minimum(1, jnp.abs(onward - level))
+        slot = level + down * reached * (LEVELS - level)
+        copy = remote(
+            self.own.at[turn],
+            self.from_line.at[slot],
+            self.line_s.at[turn],
+            self.line_r.at[slot],
+            (index_of(onward, y, c), x),
+        )
+        copy.start()
+        self.sent.append(copy)
+
+    def finish(self):
+        for copy in self.sent:
+            copy.wait_send()
+
+
+def add_block(one, two, out):
+    step = 32
+
+    @pl.loop(0, out.shape[0] // step)
+    def _(i):
+        rows = pl.ds(pl.multiple_of(i * step, step), step)
+        value = one[rows, :].astype(jnp.float32) + two[rows, :].astype(jnp.float32)
+        out[rows, :] = value.astype(out.dtype)
+
+
+def total_block(plan, total):
+    step = 32
+    mine = plan.own.at[LEVELS - 1]
+    below, above = plan.from_line.at[plan.z], plan.from_line.at[LEVELS]
+
+    @pl.loop(0, total.shape[0] // step)
+    def _(i):
+        rows = pl.ds(pl.multiple_of(i * step, step), step)
+        total[rows, :] = mine[rows, :].astype(jnp.float32)
+
+    for end, block, slot in ((plan.bottom, below, plan.z), (plan.top, above, LEVELS)):
+
+        @pl.when(end == 0)
+        def _():
+            plan.line_arrived(slot)
+
+            @pl.loop(0, total.shape[0] // step)
+            def _(i):
+                rows = pl.ds(pl.multiple_of(i * step, step), step)
+                total[rows, :] = total[rows, :] + block[rows, :].astype(jnp.float32)
+
+
+def sums_kernel(count, *refs):
+    parts, totals = refs[:count], refs[count : 2 * count]
+    buffers = [refs[(2 + i) * count : (3 + i) * count] for i in range(4)]
+    sems, own_sems = refs[6 * count : 6 * count + 6], refs[6 * count + 6]
+    plane_greet()
+    plans = [
+        PlaneSums(*(b[a] for b in buffers), tuple(s.at[a] for s in sems)) for a in range(count)
+    ]
+    loads = {}
+    for a, plan in enumerate(plans):
+        for side in (1, 0):
+            for turn in range(LEVELS):
+                plan.to_core(parts[a].at[plan.slot_of(turn, side, 1)], turn, side)
+                j = side * LEVELS + turn
+                load = pltpu.make_async_copy(
+                    parts[a].at[plan.slot_of(turn, side, 0)], plan.own.at[j], own_sems.at[a, j]
+                )
+                load.start()
+                loads[a, j] = load
+    for side in (1, 0):
+        for turn in range(LEVELS):
+            for a, plan in enumerate(plans):
+                j = side * LEVELS + turn
+                loads[a, j].wait()
+                plan.core_arrived(turn, side)
+                add_block(plan.own.at[j], plan.from_core.at[j], plan.own.at[j])
+                if side == 1:
+                    plan.to_side(turn)
+    for turn in range(LEVELS):
+        for plan in plans:
+            plan.side_arrived(turn)
+            add_block(plan.own.at[turn], plan.from_side.at[turn], plan.own.at[turn])
+            if turn < LEVELS - 1:
+                plan.to_line(turn, lambda one, two: add_block(one, two, one))
+    for a, plan in enumerate(plans):
+        total_block(plan, totals[a])
+    for plan in plans:
+        plan.finish()
+
+
+def plane_sums(parts, collective_id, name):
+    count = len(parts)
+    shapes = [p.shape[1:] for p in parts]
+    types = [p.dtype for p in parts]
+
+    def scratch(blocks):
+        return [pltpu.VMEM((blocks,) + s, t) for s, t in zip(shapes, types)]
+
+    def sems(blocks):
+        return [pltpu.SemaphoreType.DMA((count, blocks))] * 2
+
+    nbytes = sum(p.size * p.dtype.itemsize for p in parts)
+    return pl.pallas_call(
+        functools.partial(sums_kernel, count),
+        out_shape=[jax.ShapeDtypeStruct(s, jnp.float32) for s in shapes],
+        in_specs=[pl.BlockSpec(memory_space=pl.ANY)] * count,
+        out_specs=[pl.BlockSpec(memory_space=pltpu.VMEM)] * count,
+        scratch_shapes=scratch(2 * LEVELS)
+        + scratch(2 * LEVELS)
+        + scratch(LEVELS)
+        + scratch(LEVELS + 1)
+        + sems(2 * LEVELS)
+        + sems(LEVELS)
+        + sems(LEVELS + 1)
+        + [pltpu.SemaphoreType.DMA((count, 2 * LEVELS))],
+        compiler_params=pltpu.CompilerParams(
+            collective_id=collective_id, has_side_effects=True, vmem_limit_bytes=60 * 2**20
+        ),
+        cost_estimate=pl.CostEstimate(flops=0, bytes_accessed=4 * nbytes, transcendentals=0),
+        name=name,
+    )(*parts)
+
+
 def gate_columns(route_rows, gate_rows, expert_count):
     names = jnp.arange(expert_count, dtype=jnp.int32)[None, None, :]
     return jnp.sum(jnp.where(route_rows[:, :, None] == names, gate_rows[:, :, None], 0.0), axis=1)
@@ -334,13 +695,17 @@
     gate_pair = lax.all_gather(gate_weight[0], "tp", axis=0)
     up_pair = lax.all_gather(up_weight[0], "tp", axis=0)
     down_pair = lax.all_gather(down_weight[0], "tp", axis=0)
-    upstream_all = lax.all_gather(upstream_grad.astype(bf16), "fsdp", axis=0, tiled=True)
 
     first_scale = lax.rsqrt(jnp.mean(block_input * block_input, axis=1, keepdims=True) + epsilon)
     first_normed = (block_input * first_scale * first_gain).astype(bf16)
     normed_rows = pair_rows(first_normed)
-    query_full, key_full, value_full, output_full = projections(
-        query_weight, key_weight, value_weight, output_weight
+    query_full, key_full, value_full, output_full, upstream_all = (
+        blocks.reshape(-1, blocks.shape[2])
+        for blocks in plane_gather(
+            [query_weight, key_weight, value_weight, output_weight, upstream_grad.astype(bf16)],
+            1,
+            "gather_weights",
+        )
     )
 
     def heads_of(weight_full):
@@ -362,7 +727,8 @@
     second_scale = lax.rsqrt(jnp.mean(middle * middle, axis=1, keepdims=True) + epsilon)
     second_normed = (middle * second_scale * second_gain).astype(bf16)
 
-    rows_all = lax.all_gather(second_normed, "fsdp", axis=0, tiled=True)
+    (rows_all,) = plane_gather([second_normed], 2, "gather_rows")
+    rows_all = rows_all.reshape(-1, model_width)
     gate_act = jnp.einsum("td,gdf->gtf", rows_all, gate_pair, preferred_element_type=f32)
     up_act = jnp.einsum("td,gdf->gtf", rows_all, up_pair, preferred_element_type=f32)
     sigmoid_gate = jax.nn.sigmoid(gate_act)
@@ -378,12 +744,12 @@
     up_cot = (hidden_cot * gate_act * sigmoid_gate).astype(bf16)
     input_cot = jnp.einsum("gtf,gdf->td", gate_cot, gate_pair, preferred_element_type=f32)
     input_cot = input_cot + jnp.einsum("gtf,gdf->td", up_cot, up_pair, preferred_element_type=f32)
-    second_cot = lax.psum_scatter(
-        input_cot.astype(bf16), "fsdp", scatter_dimension=0, tiled=True
-    ).astype(f32)
-    mixture = lax.psum_scatter(
-        mixture_part.astype(bf16), "fsdp", scatter_dimension=0, tiled=True
-    ).astype(f32)
+    blocks = (owner_count, local_rows, model_width)
+    second_cot, mixture = plane_sums(
+        [input_cot.astype(bf16).reshape(blocks), mixture_part.astype(bf16).reshape(blocks)],
+        3,
+        "sum_rows",
+    )
     block_output = middle + mixture
     route_back = lax.all_to_all(
         route_sums.reshape(owner_count, local_rows), "fsdp", split_axis=0, concat_axis=0, tiled=True
@@ -450,15 +816,19 @@
         * jnp.mean(weighted_one * block_input, axis=1, keepdims=True)
     )
 
-    def owner_grad(term):
-        return lax.psum_scatter(
-            term.astype(bf16), "fsdp", scatter_dimension=0, tiled=True
-        ).astype(f32)
-
-    query_grad = owner_grad(contract_rows(normed_rows, query_cot))
-    key_grad = owner_grad(contract_rows(normed_rows, key_cot))
-    value_grad = owner_grad(contract_rows(normed_rows, value_cot))
-    output_grad = owner_grad(out_term)
+    query_grad, key_grad, value_grad, output_grad = plane_sums(
+        [
+            term.astype(bf16).reshape((owner_count,) + query_weight.shape)
+            for term in (
+                contract_rows(normed_rows, query_cot),
+                contract_rows(normed_rows, key_cot),
+                contract_rows(normed_rows, value_cot),
+                out_term,
+            )
+        ],
+        4,
+        "sum_gradients",
+    )
     first_gain_grad, second_gain_grad = lax.psum((first_term, second_term), ("fsdp", "tp"))
     return (
         block_output,
@@ -477,7 +847,7 @@
 
 
 def solution(mesh):
-    dense = 2 * TOP >= EXP_DEV * mesh.shape["fsdp"]
+    dense = 2 * TOP >= EXP_DEV * mesh.shape["fsdp"] and mesh.shape["fsdp"] == 4 * LEVELS
     per_device = per_device_dense if dense else per_device_slots
     in_specs = (
         P(("fsdp", "tp"), None),

time: 1450 us -> 874 us (0.60)
  waiting for transfers between devices: 1110 us -> 144 us
  Pallas kernels: 0 us -> 397 us
    reduce_scatter x6 -> x0, waiting for transfers between devices: 462 us -> none  [the longest x4 295 us: owner_grad(): lax.psum_scatter(term.astype(bf16), 'fsdp', scatter_dimension=0, tiled=True)]
    pallas_call x0 -> x4, Pallas kernels: none -> 397 us  [the longest x2 200 us: plane_gather(): pl.pallas_call(functools.partial(gather_kernel, count), out_shape=[jax.Sh...]
    all_gather x6 -> x0, waiting for transfers between devices: 343 us -> none  [the longest x1 77.1 us: per_device_dense(): lax.all_gather(upstream_grad.astype(bf16), 'fsdp', axis=0, tiled=True)]
    reduce_scatter x3, waiting for transfers between devices: 75.2 us -> 0.02 us  [pair_grad(): lax.psum_scatter(part.astype(bf16), 'tp', scatter_dimension=0).astype(f32)]
    all_gather x1, waiting for transfers between devices: 42.4 us -> 0.02 us  [per_device_dense(): gate_pair = lax.all_gather(gate_weight[0], 'tp', axis=0)]
    reduce_scatter x2, waiting for transfers between devices: 59.7 us -> 30.4 us  [pair_sums(): return lax.psum_scatter(term_block, 'tp', scatter_dimension=0, tiled=True)]
  transfers between devices with their start and end apart: 23 -> 11, of which waited for: 21 -> 5; matrix products, arithmetic and copies ran while one was open for 12% -> 12% of each run, Pallas kernels for 0% -> 34%
where the time goes in v2:
time: 874 us; the launch traced here: 867 us
  Pallas kernels  397 us (45%)
  matrix products  191 us (22%)
  waiting for transfers between devices  144 us (16%)
  blocking collectives  58.8 us (7%)
  other arithmetic  35.6 us (4%)
  local copies, waits for them, and re-layouts  19.4 us (2%)
  between operations  15.1 us (2%)
    pallas_call x2, Pallas kernels, plane_gather(): pl.pallas_call(functools.partial(gather_kernel, count), out_shape=[jax.Sh...  200 us
    pallas_call x2, Pallas kernels, plane_sums(): pl.pallas_call(functools.partial(sums_kernel, count), out_shape=[jax.Shap...  197 us
    all_gather x1, waiting for transfers between devices, per_device_dense(): down_pair = lax.all_gather(down_weight[0], 'tp', axis=0)  43.6 us
    all_gather x1, waiting for transfers between devices, per_device_dense(): up_pair = lax.all_gather(up_weight[0], 'tp', axis=0)  43 us
    psum x1, blocking collectives, per_device_dense(): lax.psum((first_term, second_term), ('fsdp', 'tp'))  40.8 us
    reduce_scatter x2, waiting for transfers between devices, pair_sums(): return lax.psum_scatter(term_block, 'tp', scatter_dimension=0, tiled=True)  30.4 us
    dot_general x1, matrix products, per_device_dense(): jnp.einsum('td,gfd->gtf', upstream_all, down_pair, preferred_element_type...  20.6 us
    all_gather x2, waiting for transfers between devices, pair_rows(): return lax.all_gather(row_block, 'tp', axis=0, tiled=True)  18.6 us
  transfers between devices with their start and end apart: 11, of which 5 were waited for; matrix products, arithmetic and copies ran while one was open for 12% of the time, Pallas kernels for 34%

profile of v2, /device:TPU:0, one launch (start us, length us, event | category | flops | bytes accessed | tf_op | source)
XLA Modules:
  0.0 866.9 jit_solution(14847476197076651494)
XLA Ops:
  13.5 144.7 %gather_weights.1 = (bf16[16,128,1024]{2,1,0:T(8,128)(2,1)}, bf16[16,128,1024]{2,1,0:T(8,128)(2,1)}, bf16[16,128,1024]{2,1,0:T(8,128)(2,1)}, bf16[16,128,1024]{2,1,0:T(8,128)(2,1)}, bf16[16,128,2048]{2,1,0:T(8,128)(2,1)}) custom-call(bf16[128,1024]{1,0:T(8,128)(2,1)} %refs_0_.1, bf16[128,1024]{1,0:T(8,128)(2,1)} %refs_1_.1, bf16[128,1024]{1,0:T(8,128)(2,1)} %refs_2_.1, ...), custom_call_target="tpu_custom_call" | custom-call | bytes 100663296 | tf_op jit(solution)/shard_map/gather_weights/pallas_call | solution.py:452
  158.2 3.8 convolution_convert_fusion.9
  163.1 3.5 convolution_convert_fusion.8
  178.2 30.4 %reduce-scatter.6.cloned.1.call-done = f32[128,2048]{1,0:T(8,128)} async-done(((f32[256,2048]{1,0:T(8,128)}), f32[128,2048]{1,0:T(8,128)}) %reduce-scatter.6.cloned.1.call-update) | async-done | bytes 1048592 | tf_op jit(solution)/shard_map/reduce_scatter | solution.py:33
  212.0 55.4 %gather_rows.1 = bf16[16,128,2048]{2,1,0:T(8,128)(2,1)} custom-call(bf16[128,2048]{1,0:T(8,128)(2,1)} %multiply_convert_fusion.4.refs_0_), custom_call_target="tpu_custom_call" | custom-call | bytes 33554432 | tf_op jit(solution)/shard_map/gather_rows/pallas_call | solution.py:452
  267.5 14.6 %fusion.52 = f32[2048,2,512]{0,2,1:T(8,128)} fusion(bf16[2048,2048,1]{1,0,2:T(8,128)(2,1)} %bitcast.167, bf16[2,2048,512]{2,1,0:T(8,128)(2,1)} %all-gather.12.cloned.1.call-done), kind=kOutput, calls=%fused_computation.88 | convolution fusion | flops 8589934592 | bytes 20971520 | tf_op jit(solution)/shard_map/td,gdf->gtf/dot_general | solution.py:732
  282.0 43.0 %all-gather.10.cloned.1.call-done = bf16[2,2048,512]{2,1,0:T(8,128)(2,1)} async-done(((bf16[1,2048,512]{2,1,0:T(8,128)(2,1)}), bf16[2,2048,512]{2,1,0:T(8,128)(2,1)}) %all-gather.10.cloned.1.call-update) | async-done | bytes 4194320 | tf_op jit(solution)/shard_map/all_gather | solution.py:696
  325.0 14.5 %fusion.51 = f32[2048,2,512]{0,2,1:T(8,128)} fusion(bf16[2048,2048,1]{1,0,2:T(8,128)(2,1)} %bitcast.168, bf16[2,2048,512]{2,1,0:T(8,128)(2,1)} %all-gather.10.cloned.1.call-done), kind=kOutput, calls=%fused_computation.87 | convolution fusion | flops 8589934592 | bytes 20971520 | tf_op jit(solution)/shard_map/td,gdf->gtf/dot_general | solution.py:733
  339.6 43.6 %all-gather.8.cloned.1.call-done = bf16[2,512,2048]{2,1,0:T(8,128)(2,1)} async-done(((bf16[1,512,2048]{2,1,0:T(8,128)(2,1)}), bf16[2,512,2048]{2,1,0:T(8,128)(2,1)}) %all-gather.8.cloned.1.call-update) | async-done | bytes 4194320 | tf_op jit(solution)/shard_map/all_gather | solution.py:697
  383.2 20.6 %fusion.12 = (f32[2048]{0:T(1024)}, f32[2048,2,512]{0,2,1:T(8,128)}) fusion(f32[2048,2,512]{0,2,1:T(8,128)} %fusion.51, f32[2048,2,512]{0,2,1:T(8,128)} %fusion.52, bf16[2048,2048,1]{1,0,2:T(8,128)(2,1)} %bitcast.192, bf16[2,512,2048]{2,1,0:T(8,128)(2,1)} %all-gather.8.cloned.1.call-done), kind=kOutput, calls=%fused_computation.21 | convolution fusion | flops 8604612608 | bytes 37756928 | tf_op jit(solution)/shard_map/td,gfd->gtf/dot_general | solution.py:738
  403.8 5.6 all-to-all-start
  409.5 6.3 all-to-all-done
  416.4 18.0 %all_gather.20 = f32[2048,16]{0,1:T(8,128)S(1)} all-gather(f32[128,16]{0,1:T(8,128)S(1)} %get-tuple-element.87), channel_id=1, replica_groups=mesh['fsdp'=16,'tp'=2] {'fsdp'}, dimensions={0}, use_global_device_ids=true | all-gather | bytes 139264 | tf_op jit(solution)/shard_map/all_gather | solution.py:688
  434.5 12.9 %fusion.9 = (bf16[2,2048,512]{1,2,0:T(8,128)(2,1)}, bf16[2,2048,512]{1,2,0:T(8,128)(2,1)S(1)}) fusion(f32[2048,2,512]{0,2,1:T(8,128)} %fusion.52, f32[2048,2,512]{0,2,1:T(8,128)} %get-tuple-element.100, f32[2048]{0:T(1024)S(1)} %select_reduce_fusion, f32[2048,2,512]{0,2,1:T(8,128)} %fusion.51), kind=kLoop, calls=%fused_computation.15 | loop fusion | flops 29360128 | bytes 33562624 | tf_op jit(solution)/shard_map/convert_element_type | solution.py:744
  447.4 16.5 %bitcast_convert_fusion = bf16[2048,2048]{1,0:T(8,128)(2,1)} fusion(bf16[2,512,2048]{2,1,0:T(8,128)(2,1)} %all-gather.8.cloned.1.call-done, f32[2048]{0:T(1024)S(1)} %select_reduce_fusion, f32[2048,2,512]{0,2,1:T(8,128)S(1)} %copy-done.8, f32[2048,2,512]{0,2,1:T(8,128)} %fusion.51), kind=kOutput, calls=%fused_computation.1 | convolution fusion | flops 8608808960 | bytes 29368320 | tf_op jit(solution)/shard_map/gtf,gfd->td/dot_general | solution.py:737
  463.9 14.1 %fusion.53 = f32[2048,2048,1]{1,0,2:T(8,128)} fusion(bf16[2,2048,512]{1,2,0:T(8,128)(2,1)S(1)} %get-tuple-element.95, bf16[2,2048,512]{2,1,0:T(8,128)(2,1)} %all-gather.12.cloned.1.call-done), kind=kOutput, calls=%fused_computation.89 | convolution fusion | flops 8589934592 | bytes 25165824 | tf_op jit(solution)/shard_map/gtf,gdf->td/dot_general | solution.py:745
  478.0 16.7 %fusion.1 = bf16[2048,2048]{1,0:T(8,128)(2,1)} fusion(f32[2048,2048,1]{1,0,2:T(8,128)} %fusion.53, bf16[2,2048,512]{1,2,0:T(8,128)(2,1)} %get-tuple-element.94, bf16[2,2048,512]{2,1,0:T(8,128)(2,1)} %all-gather.10.cloned.1.call-done), kind=kOutput, calls=%fused_computation.3 | convolution fusion | flops 8598323200 | bytes 33554432 | tf_op jit(solution)/shard_map/gtf,gdf->td/dot_general | solution.py:746
  494.7 97.7 %sum_rows.1 = (f32[128,2048]{1,0:T(8,128)}, f32[128,2048]{1,0:T(8,128)}) custom-call(bf16[16,128,2048]{2,1,0:T(8,128)(2,1)} %bitcast.172, bf16[16,128,2048]{2,1,0:T(8,128)(2,1)} %bitcast.171), custom_call_target="tpu_custom_call" | custom-call | bytes 67108864 | tf_op jit(solution)/shard_map/sum_rows/pallas_call | solution.py:630
  593.9 3.8 fusion.49
  598.0 18.6 %all-gather.14.cloned.1.call-done = bf16[256,2048]{1,0:T(8,128)(2,1)} async-done(((bf16[128,2048]{1,0:T(8,128)(2,1)}), bf16[256,2048]{1,0:T(8,128)(2,1)}) %all-gather.14.cloned.1.call-update) | async-done | bytes 1048592 | tf_op jit(solution)/shard_map/all_gather | solution.py:29
  616.6 3.8 convolution_convert_fusion.7
  623.9 4.4 fusion.22
  628.3 3.6 fusion.25
  631.9 3.8 fusion.54
  640.6 16.4 %convolution_convert_fusion = bf16[2,512,2048]{2,1,0:T(8,128)(2,1)} fusion(bf16[2048,2048,1]{1,0,2:T(8,128)(2,1)} %bitcast.193, f32[2048]{0:T(1024)S(1)} %select_reduce_fusion, f32[2048,2,512]{0,2,1:T(8,128)} %fusion.52, f32[2048,2,512]{0,2,1:T(8,128)} %fusion.51), kind=kOutput, calls=%fused_computation.25 | convolution fusion | flops 8606711808 | bytes 29368320 | tf_op jit(solution)/shard_map/gtf,td->gfd/dot_general | solution.py:760
  657.4 13.9 %convert_bitcast_fusion = bf16[2,2048,512]{1,2,0:T(8,128)(2,1)} fusion(bf16[2,2048,512]{1,2,0:T(8,128)(2,1)} %get-tuple-element.94, bf16[2048,2048,1]{1,0,2:T(8,128)(2,1)} %bitcast.169), kind=kOutput, calls=%fused_computation.23 | convolution fusion | flops 8592031744 | bytes 16777216 | tf_op jit(solution)/shard_map/td,gtf->gdf/dot_general | solution.py:762
  671.3 13.9 %convert_bitcast_fusion.1 = bf16[2,2048,512]{1,2,0:T(8,128)(2,1)} fusion(bf16[2,2048,512]{1,2,0:T(8,128)(2,1)} %copy-done.9, bf16[2048,2048,1]{1,0,2:T(8,128)(2,1)} %bitcast.170), kind=kOutput, calls=%fused_computation.24 | convolution fusion | flops 8592031744 | bytes 16777216 | tf_op jit(solution)/shard_map/td,gtf->gdf/dot_general | solution.py:761
  699.9 98.9 %sum_gradients.1 = (f32[128,1024]{1,0:T(8,128)}, f32[128,1024]{1,0:T(8,128)}, f32[128,1024]{1,0:T(8,128)}, f32[128,1024]{1,0:T(8,128)}) custom-call(bf16[16,128,1024]{2,1,0:T(8,128)(2,1)} %bitcast.166, bf16[16,128,1024]{2,1,0:T(8,128)(2,1)} %bitcast.165, bf16[16,128,1024]{2,1,0:T(8,128)(2,1)} %bitcast.164, bf16[16,128,1024]{2,1,0:T(8,128)(2,1)} %bitcast.163), custom_call_target="tpu_custom_call" | custom-call | bytes 67108864 | tf_op jit(solution)/shard_map/sum_gradients/pallas_call | solution.py:630
  800.4 40.8 %all-reduce = (f32[2048]{0:T(1024)}, f32[2048]{0:T(1024)}) all-reduce(f32[2048]{0:T(1024)S(1)} %get-tuple-element.84, f32[2048]{0:T(1024)S(1)} %get-tuple-element.82), channel_id=1, replica_groups=mesh['fsdp'=16,'tp'=2] {'fsdp','tp'}, use_global_device_ids=true, to_apply=%region_12.13 | all-reduce | flops 4096 | bytes 32768 | tf_op jit(solution)/shard_map/psum | solution.py:832
  843.8 4.1 convert_element_type.142
  847.9 4.1 copy.114
  852.1 4.3 copy.113
  (122 shorter events, 55.5 us)
Async XLA Ops:
  7.2 171.0 %copy-start = (s32[256,8]{0,1:T(8,128)S(1)}, s32[256,8]{0,1:T(8,128)}, u32[]{:S(2)}) copy-start(s32[256,8]{0,1:T(8,128)} %param.24) | copy-start | bytes 24580
  7.2 151.0 %all-gather.6.cloned.1.call-start = ((), (), s32[]{:S(2)}) async-start(), calls=%async_computation.6 | async-start | bytes 1572864 | tf_op jit(solution)/shard_map/all_gather | solution.py:29
  11.3 197.3 %reduce-scatter.6.cloned.1.call-start = ((), (), s32[]{:S(2)}) async-start(), calls=%async_computation.7 | async-start | bytes 3145728 | tf_op jit(solution)/shard_map/reduce_scatter | solution.py:33
  158.2 4.9 copy-start.4
  167.6 2.5 copy-start.10
  170.1 3.5 copy-start.28
  176.2 32.4 %copy-start.2 = (f32[128,2048]{1,0:T(8,128)S(1)}, f32[128,2048]{1,0:T(8,128)}, u32[]{:S(2)}) copy-start(f32[128,2048]{1,0:T(8,128)} %param.13) | copy-start | bytes 3145732
  176.2 91.2 %all-gather.12.cloned.1.call-start = ((), (), s32[]{:S(2)}) async-start(), calls=%async_computation.10 | async-start | bytes 6291456 | tf_op jit(solution)/shard_map/all_gather | solution.py:695
  177.0 34.1 %copy-start.23 = (f32[2048]{0:T(1024)S(1)}, f32[2048]{0:T(1024)}, u32[]{:S(2)}) copy-start(f32[2048]{0:T(1024)} %param.16) | copy-start | bytes 24580
  177.0 148.1 %all-gather.10.cloned.1.call-start = ((), (), s32[]{:S(2)}) async-start(), calls=%async_computation.9 | async-start | bytes 6291456 | tf_op jit(solution)/shard_map/all_gather | solution.py:696
  177.6 205.6 %all-gather.8.cloned.1.call-start = ((), (), s32[]{:S(2)}) async-start(), calls=%async_computation.8 | async-start | bytes 6291456 | tf_op jit(solution)/shard_map/all_gather | solution.py:697
  403.8 12.0 %all-to-all-start = ((f32[16,1,128]{2,1,0:T(1,128)}), f32[16,1,128]{2,1,0:T(1,128)S(1)}, u32[]{:S(2)}, u32[]{:S(2)}) async-start(f32[16,1,128]{2,1,0:T(1,128)} %bitcast.37), calls=%async_computation.5 | async-start | bytes 16384 | tf_op jit(solution)/shard_map/all_to_all | solution.py:754
  409.5 207.1 %all-gather.14.cloned.1.call-start = ((), (), s32[]{:S(2)}) async-start(), calls=%async_computation.11 | async-start | bytes 1572864 | tf_op jit(solution)/shard_map/all_gather | solution.py:29
  434.5 12.9 %copy-start.8 = (f32[2048,2,512]{0,2,1:T(8,128)S(1)}, f32[2048,2,512]{0,2,1:T(8,128)}, u32[]{:S(2)}) copy-start(f32[2048,2,512]{0,2,1:T(8,128)} %fusion.52) | copy-start | bytes 25165828
  447.4 16.5 %copy-start.9 = (bf16[2,2048,512]{1,2,0:T(8,128)(2,1)}, bf16[2,2048,512]{1,2,0:T(8,128)(2,1)S(1)}, u32[]{:S(2)}) copy-start(bf16[2,2048,512]{1,2,0:T(8,128)(2,1)S(1)} %get-tuple-element.95) | copy-start | bytes 12582916
  494.7 97.7 %copy-start.7 = (f32[128,2048]{1,0:T(8,128)S(1)}, f32[128,2048]{1,0:T(8,128)}, u32[]{:S(2)}) copy-start(f32[128,2048]{1,0:T(8,128)} %copy-done.6) | copy-start | bytes 3145732
  597.7 201.1 %reduce-scatter.8.cloned.1.call-start = ((), (), s32[]{:S(2)}) async-start(), calls=%async_computation.12 | async-start | bytes 3145728 | tf_op jit(solution)/shard_map/reduce_scatter | solution.py:33
  631.9 3.8 copy-start.12
  640.6 203.2 %reduce-scatter.14.cloned.1.call-start = ((), (), s32[]{:S(2)}) async-start(), calls=%async_computation.15 | async-start | bytes 6291456 | tf_op jit(solution)/shard_map/reduce_scatter | solution.py:765
  657.1 190.8 %reduce-scatter.12.cloned.1.call-start = ((), (), s32[]{:S(2)}) async-start(), calls=%async_computation.14 | async-start | bytes 6291456 | tf_op jit(solution)/shard_map/reduce_scatter | solution.py:765
  671.3 180.8 %reduce-scatter.10.cloned.1.call-start = ((), (), s32[]{:S(2)}) async-start(), calls=%async_computation.13 | async-start | bytes 6291456 | tf_op jit(solution)/shard_map/reduce_scatter | solution.py:765
  686.6 3.2 copy-start.5
  693.2 3.3 copy-start.18
  699.9 99.0 %copy-start.3 = (f32[128,2048]{1,0:T(8,128)S(1)}, f32[128,2048]{1,0:T(8,128)}, u32[]{:S(2)}) copy-start(f32[128,2048]{1,0:T(8,128)} %param.13) | copy-start | bytes 3145732
  699.9 99.0 %copy-start.24 = (f32[2048]{0:T(1024)S(1)}, f32[2048]{0:T(1024)}, u32[]{:S(2)}) copy-start(f32[2048]{0:T(1024)} %param.15) | copy-start | bytes 24580
  699.9 99.0 %copy-start.26 = (f32[128]{0:T(128)S(1)}, f32[128]{0:T(128)}, u32[]{:S(2)}) copy-start(f32[128]{0:T(128)} %copy-done.25) | copy-start | bytes 1540
  699.9 141.3 %copy-start.13 = (f32[128,2048]{1,0:T(8,128)S(1)}, f32[128,2048]{1,0:T(8,128)}, u32[]{:S(2)}) copy-start(f32[128,2048]{1,0:T(8,128)} %get-tuple-element.91) | copy-start | bytes 3145732
  847.9 11.6 %copy-start.1 = (s32[256,8]{0,1:T(8,128)S(1)}, s32[256,8]{0,1:T(8,128)}, u32[]{:S(2)}) copy-start(s32[256,8]{0,1:T(8,128)} %param.24) | copy-start | bytes 24580
  852.1 4.3 copy-start.22
  852.1 5.1 copy-start.21
  852.1 5.9 copy-start.20
  852.1 6.7 copy-start.19
  (8 other events, 9.9 us)
Sparse Core Ops, SparseCore 0:
  11.5 23.9 all-gather.5
  176.3 32.2 reduce-scatter.5
  210.2 56.6 all-gather.11
  268.3 56.7 all-gather.9
  326.4 56.7 all-gather.7
  597.8 18.7 all-gather.13
  640.7 31.8 reduce-scatter.7
  674.9 54.3 reduce-scatter.13
  731.7 54.3 reduce-scatter.11
  788.2 55.7 reduce-scatter.9

commit v3 on v2

--- a/solution.py
+++ b/solution.py
@@ -304,25 +304,31 @@
 
 
 LEVELS = 4
-LEVEL_ORDER = tuple(
-    sum(level << (2 * z) for z, level in enumerate(turn))
-    for turn in ((3, 3, 0, 0), (2, 2, 1, 1), (1, 0, 3, 2), (0, 1, 2, 3))
-)
+LEVEL_ORDER = sum(
+    level << (8 * turn + 2 * z)
+    for turn, row in enumerate(((3, 3, 0, 0), (2, 2, 1, 1), (1, 0, 3, 2), (0, 1, 2, 3)))
+    for z, level in enumerate(row)
+) - (1 << 32)
 
 
 def level_at(turn, z):
-    return (LEVEL_ORDER[turn] >> (2 * z)) % 4
+    return (jnp.int32(LEVEL_ORDER) >> (8 * turn + 2 * z)) & 3
 
 
 def line_ends(z):
     return (z + 1) // LEVELS, (LEVELS - z) // LEVELS
 
 
-def plane_greet():
+def plane_greet(pair=False, far=False):
     z, y, c, x = place()
     top, bottom = line_ends(z)
     barrier = pltpu.get_barrier_semaphore()
-    for partner in ((index_of(z, 1 - y, c), x), (index_of(z, y, 1 - c), x)):
+    partners = [(index_of(z, 1 - y, c), x), (index_of(z, y, 1 - c), x)]
+    if pair:
+        partners.append((index_of(z, y, c), 1 - x))
+    if far:
+        partners.append((index_of((z + 2) % LEVELS, y, c), x))
+    for partner in partners:
         pl.semaphore_signal(barrier, inc=1, device_id=partner, device_id_type=MESH)
 
     @pl.when(top == 0)
@@ -335,7 +341,7 @@
         below = (index_of(z - 1, y, c), x)
         pl.semaphore_signal(barrier, inc=1, device_id=below, device_id_type=MESH)
 
-    pl.semaphore_wait(barrier, 4 - top - bottom)
+    pl.semaphore_wait(barrier, len(partners) + 2 - top - bottom)
 
 
 def remote(src, dst, send_sem, recv_sem, target):
@@ -355,31 +361,25 @@
         self.send_sems, self.recv_sems = send_sems, recv_sems
         self.z, self.y, self.c, self.x = place()
         self.top, self.bottom = line_ends(self.z)
-        self.sent = []
-
-    def _send(self, src, slot, target, unless=None):
-        k = len(self.sent)
-        copy = remote(
-            src, self.full.at[slot], self.send_sems.at[k], self.recv_sems.at[slot], target
-        )
-        if unless is None:
-            copy.start()
-        else:
-            pl.when(unless == 0)(copy.start)
-        self.sent.append((copy, unless))
+
+    def _copy(self, number, src, slot, target):
+        return remote(
+            src, self.full.at[slot], self.send_sems.at[number], self.recv_sems.at[slot], target
+        )
 
     def arrived(self, slot):
         here = self.full.at[slot]
-        k = self.send_sems.shape[0] - 1
-        remote(here, here, self.send_sems.at[k], self.recv_sems.at[slot], (0, self.x)).wait_recv()
+        remote(here, here, self.send_sems.at[0], self.recv_sems.at[slot], (0, self.x)).wait_recv()
 
     def start(self):
         z, y, c, x = self.z, self.y, self.c, self.x
         own = index_of(z, y, c)
-        self._send(self.mine, own, (index_of(z + 1, y, c), x), self.top)
-        self._send(self.mine, own, (index_of(z - 1, y, c), x), self.bottom)
-        self._send(self.mine, own, (index_of(z, 1 - y, c), x))
-        self._send(self.mine, own, (index_of(z, y, 1 - c), x))
+        up = self._copy(0, self.mine, own, (index_of(z + 1, y, c), x))
+        down = self._copy(1, self.mine, own, (index_of(z - 1, y, c), x))
+        pl.when(self.top == 0)(up.start)
+        pl.when(self.bottom == 0)(down.start)
+        self._copy(2, self.mine, own, (index_of(z, 1 - y, c), x)).start()
+        self._copy(3, self.mine, own, (index_of(z, y, 1 - c), x)).start()
 
     def from_line(self, step):
         z, y, c, x = self.z, self.y, self.c, self.x
@@ -387,46 +387,64 @@
         slot = index_of(level, y, c)
         self.arrived(slot)
         onward = z + 1 - 2 * ((level + LEVELS - z) // LEVELS)
-        self._send(self.full.at[slot], slot, (index_of(onward, y, c), x), self.top + self.bottom)
-        self._send(self.full.at[slot], slot, (index_of(z, 1 - y, c), x))
-        self._send(self.full.at[slot], slot, (index_of(z, y, 1 - c), x))
+        src, number = self.full.at[slot], 4 + 3 * (step - 1)
+        forward = self._copy(number, src, slot, (index_of(onward, y, c), x))
+        pl.when(self.top + self.bottom == 0)(forward.start)
+        self._copy(number + 1, src, slot, (index_of(z, 1 - y, c), x)).start()
+        self._copy(number + 2, src, slot, (index_of(z, y, 1 - c), x)).start()
 
     def from_side(self, step):
         z, y, c, x = self.z, self.y, self.c, self.x
         slot = index_of(level_at(3 - step, z), 1 - y, c)
         self.arrived(slot)
-        self._send(self.full.at[slot], slot, (index_of(z, y, 1 - c), x))
+        self._copy(13 + step, self.full.at[slot], slot, (index_of(z, y, 1 - c), x)).start()
 
     def from_core(self, step, side):
         z, y, c = self.z, self.y, self.c
         self.arrived(index_of(level_at(3 - step, z), (y + side) % 2, 1 - c))
 
     def finish(self):
-        for copy, unless in self.sent:
-            if unless is None:
-                copy.wait_send()
+        for number in range(GATHER_SENDS):
+            wait = self._copy(number, self.mine, 0, (0, self.x)).wait_send
+            if number == 0:
+                pl.when(self.top == 0)(wait)
+            elif number == 1:
+                pl.when(self.bottom == 0)(wait)
+            elif number in (4, 7, 10):
+                pl.when(self.top + self.bottom == 0)(wait)
             else:
-                pl.when(unless == 0)(copy.wait_send)
-
-
-GATHER_SENDS = 18
-
-
-def gather_kernel(count, *refs):
-    mine, full = refs[:count], refs[count : 2 * count]
-    send_sems, recv_sems, own_sems = refs[2 * count :]
+                wait()
+
+
+GATHER_SENDS = 17
+
+
+def weights_kernel(count, *refs):
+    mine, normed, experts = refs[:count], refs[count], refs[count + 1 : count + 4]
+    outs = refs[count + 4 : 2 * count + 8]
+    full, normed_pair, others = outs[:count], outs[count], outs[count + 1 :]
+    send_sems, recv_sems, own_sems, pair_s, pair_r = refs[2 * count + 8 :]
     z, y, c, x = place()
-    plane_greet()
     own = index_of(z, y, c)
+    plane_greet(pair=True)
     plans = [
         PlaneGather(mine[a], full[a], send_sems.at[a], recv_sems.at[a]) for a in range(count)
     ]
+    swaps = [
+        remote(src, dst, pair_s.at[i], pair_r.at[i], (own, 1 - x))
+        for i, (src, dst) in enumerate(
+            [(normed, normed_pair.at[x])] + list(zip(experts, others))
+        )
+    ]
     kept = [
-        pltpu.make_async_copy(mine[a], full[a].at[own], own_sems.at[a]) for a in range(count)
+        pltpu.make_async_copy(src, dst, own_sems.at[i])
+        for i, (src, dst) in enumerate(
+            [(mine[a], full[a].at[own]) for a in range(count)] + [(normed, normed_pair.at[x])]
+        )
     ]
     for plan in plans:
         plan.start()
-    for copy in kept:
+    for copy in swaps + kept:
         copy.start()
     for step in range(1, LEVELS):
         for plan in plans:
@@ -441,35 +459,42 @@
                 plan.from_core(step, side)
     for plan in plans:
         plan.finish()
-    for copy in kept:
+    for copy in swaps + kept:
         copy.wait()
 
 
-def plane_gather(arrays, collective_id, name):
+def gather_weights(arrays, normed, experts, collective_id):
     owner_count = lax.axis_size("fsdp")
     count = len(arrays)
+    hbm = pl.BlockSpec(memory_space=pl.ANY)
+    vmem = pl.BlockSpec(memory_space=pltpu.VMEM)
     nbytes = sum(a.size * a.dtype.itemsize for a in arrays)
-    return pl.pallas_call(
-        functools.partial(gather_kernel, count),
-        out_shape=[jax.ShapeDtypeStruct((owner_count,) + a.shape, a.dtype) for a in arrays],
-        in_specs=[pl.BlockSpec(memory_space=pltpu.VMEM)] * count,
-        out_specs=[pl.BlockSpec(memory_space=pl.ANY)] * count,
+    outs = pl.pallas_call(
+        functools.partial(weights_kernel, count),
+        out_shape=[jax.ShapeDtypeStruct((owner_count,) + a.shape, a.dtype) for a in arrays]
+        + [jax.ShapeDtypeStruct((2,) + normed.shape, normed.dtype)]
+        + [jax.ShapeDtypeStruct(w.shape, w.dtype) for w in experts],
+        in_specs=[vmem] * (count + 1) + [hbm] * 3,
+        out_specs=[hbm] * (count + 4),
         scratch_shapes=[
             pltpu.SemaphoreType.DMA((count, GATHER_SENDS)),
             pltpu.SemaphoreType.DMA((count, owner_count)),
-            pltpu.SemaphoreType.DMA((count,)),
+            pltpu.SemaphoreType.DMA((count + 1,)),
+            pltpu.SemaphoreType.DMA((4,)),
+            pltpu.SemaphoreType.DMA((4,)),
         ],
         compiler_params=pltpu.CompilerParams(collective_id=collective_id, has_side_effects=True),
         cost_estimate=pl.CostEstimate(
             flops=0, bytes_accessed=owner_count * nbytes * 4, transcendentals=0
         ),
-        name=name,
-    )(*arrays)
+        name="gather_weights",
+    )(*arrays, normed, *experts)
+    return outs[:count], outs[count], outs[count + 1 :]
 
 
 class PlaneSums:
-    def __init__(self, own_parts, from_core, from_side, from_line, sems):
-        self.own, self.from_core = own_parts, from_core
+    def __init__(self, own_parts, from_core, from_side, from_line, sems, kept=0):
+        self.own, self.from_core, self.kept = own_parts, from_core, kept
         self.from_side, self.from_line = from_side, from_line
         self.core_s, self.core_r, self.side_s, self.side_r, self.line_s, self.line_r = sems
         self.z, self.y, self.c, self.x = place()
@@ -515,21 +540,22 @@
         here = self.from_line.at[slot]
         remote(here, here, self.line_s.at[0], self.line_r.at[slot], (0, self.x)).wait_recv()
 
-    def to_line(self, turn, add):
+    def to_line(self, turn):
         z, y, c, x = self.z, self.y, self.c, self.x
+        mine = self.own.at[self.kept + turn]
         level = level_at(turn, z)
 
         @pl.when(self.top + self.bottom == 0)
         def _():
             self.line_arrived(level)
-            add(self.own.at[turn], self.from_line.at[level])
+            add_block(mine, self.from_line.at[level], mine)
 
         down = (z + LEVELS - level) // (LEVELS + 1)
         onward = z + 1 - 2 * down
         reached = 1 - jnp.minimum(1, jnp.abs(onward - level))
         slot = level + down * reached * (LEVELS - level)
         copy = remote(
-            self.own.at[turn],
+            mine,
             self.from_line.at[slot],
             self.line_s.at[turn],
             self.line_r.at[slot],
@@ -555,7 +581,7 @@
 
 def total_block(plan, total):
     step = 32
-    mine = plan.own.at[LEVELS - 1]
+    mine = plan.own.at[plan.kept + LEVELS - 1]
     below, above = plan.from_line.at[plan.z], plan.from_line.at[LEVELS]
 
     @pl.loop(0, total.shape[0] // step)
@@ -575,14 +601,33 @@
                 total[rows, :] = total[rows, :] + block[rows, :].astype(jnp.float32)
 
 
-def sums_kernel(count, *refs):
-    parts, totals = refs[:count], refs[count : 2 * count]
-    buffers = [refs[(2 + i) * count : (3 + i) * count] for i in range(4)]
-    sems, own_sems = refs[6 * count : 6 * count + 6], refs[6 * count + 6]
-    plane_greet()
+def last_kernel(count, *refs):
+    parts, refs = refs[:count], refs[count:]
+    expert_parts, refs = refs[:3], refs[3:]
+    first_part, block_input, first_scale, first_gain, middle_grad, second_term = refs[:6]
+    refs = refs[6:]
+    totals, refs = refs[:count], refs[count:]
+    expert_grads, refs = refs[:3], refs[3:]
+    input_grad, gain_grads, refs = refs[0], refs[1], refs[2:]
+    buffers = [refs[i * count : (i + 1) * count] for i in range(4)]
+    refs = refs[4 * count :]
+    sems, own_sems, refs = refs[:6], refs[6], refs[7:]
+    first_other, gains, gains_in, refs = refs[0], refs[1], refs[2], refs[3:]
+    expert_other, expert_own, expert_sum = refs[:3], refs[3:6], refs[6:9]
+    pair_s, pair_r, load_sems, out_sems, gain_s, gain_r = refs[9:]
+    z, y, c, x = place()
+    own = index_of(z, y, c)
+    plane_greet(pair=True, far=True)
     plans = [
         PlaneSums(*(b[a] for b in buffers), tuple(s.at[a] for s in sems)) for a in range(count)
     ]
+    swaps = [
+        remote(src.at[1 - x], dst, pair_s.at[i], pair_r.at[i], (own, 1 - x))
+        for i, (src, dst) in enumerate(
+            [(first_part, first_other)] + list(zip(expert_parts, expert_other))
+        )
+    ]
+    swaps[0].start()
     loads = {}
     for a, plan in enumerate(plans):
         for side in (1, 0):
@@ -594,31 +639,136 @@
                 )
                 load.start()
                 loads[a, j] = load
-    for side in (1, 0):
-        for turn in range(LEVELS):
-            for a, plan in enumerate(plans):
-                j = side * LEVELS + turn
-                loads[a, j].wait()
-                plan.core_arrived(turn, side)
-                add_block(plan.own.at[j], plan.from_core.at[j], plan.own.at[j])
-                if side == 1:
-                    plan.to_side(turn)
-    for turn in range(LEVELS):
+
+    def core_step(turn, side):
+        for a, plan in enumerate(plans):
+            j = side * LEVELS + turn
+            loads[a, j].wait()
+            plan.core_arrived(turn, side)
+            add_block(plan.own.at[j], plan.from_core.at[j], plan.own.at[j])
+            if side == 1:
+                plan.to_side(turn)
+
+    def line_step(turn):
         for plan in plans:
             plan.side_arrived(turn)
             add_block(plan.own.at[turn], plan.from_side.at[turn], plan.own.at[turn])
             if turn < LEVELS - 1:
-                plan.to_line(turn, lambda one, two: add_block(one, two, one))
+                plan.to_line(turn)
+
+    def finish_norm():
+        swaps[0].wait_recv()
+        step = 16
+        width = input_grad.shape[1]
+        gains[...] = jnp.concatenate(
+            [jnp.zeros((1, width), jnp.float32), second_term[...], jnp.zeros((6, width), jnp.float32)],
+            axis=0,
+        )
+        gain = first_gain[...]
+
+        @pl.loop(0, input_grad.shape[0] // step)
+        def _(i):
+            rows = pl.ds(pl.multiple_of(i * step, step), step)
+            value = first_part[x, rows, :].astype(jnp.float32)
+            value = value + first_other[rows, :].astype(jnp.float32)
+            entry, scale = block_input[rows, :], first_scale[rows, :]
+            weighted = value * gain
+            mean = jnp.mean(weighted * entry, axis=1, keepdims=True)
+            input_grad[rows, :] = middle_grad[rows, :] + scale * (
+                weighted - entry * (scale * scale * mean)
+            )
+            gains[0:1, :] = gains[0:1, :] + jnp.sum(value * entry * scale, axis=0, keepdims=True)
+
+    hops = [
+        (index_of(z, y, 1 - c), x),
+        (own, 1 - x),
+        (index_of(z + 1 - 2 * (z % 2), y, c), x),
+        (index_of((z + 2) % LEVELS, y, c), x),
+        (index_of(z, 1 - y, c), x),
+    ]
+
+    def gain_copy(i):
+        return remote(gains, gains_in.at[i], gain_s.at[i], gain_r.at[i], hops[i])
+
+    def gain_add(i):
+        gain_copy(i).wait()
+        gains[...] = gains[...] + gains_in[i]
+
+    def expert_add(which):
+        other, grad = expert_other[which], expert_grads[which]
+        own_half, both = expert_own[which], expert_sum[which]
+        panel = own_half.shape[1]
+        panels = other.shape[0] // panel
+
+        def load(p):
+            rows = pl.ds(pl.multiple_of(p * panel, panel), panel)
+            return pltpu.make_async_copy(
+                expert_parts[which].at[x, rows], own_half.at[p % 2], load_sems.at[p % 2]
+            )
+
+        def store(p):
+            rows = pl.ds(pl.multiple_of(p * panel, panel), panel)
+            return pltpu.make_async_copy(both.at[p % 2], grad.at[rows], out_sems.at[p % 2])
+
+        load(0).start()
+        swaps[1 + which].wait_recv()
+
+        @pl.loop(0, panels)
+        def _(p):
+            load(p).wait()
+            pl.when(p + 1 < panels)(lambda: load(p + 1).start())
+            pl.when(p >= 2)(lambda: store(p - 2).wait())
+            at_panel = pl.multiple_of(p * panel, panel)
+
+            @pl.loop(0, panel // 16)
+            def _(i):
+                rows = pl.ds(pl.multiple_of(i * 16, 16), 16)
+                there = pl.ds(pl.multiple_of(at_panel + i * 16, 16), 16)
+                mine = own_half[p % 2, rows, :].astype(jnp.float32)
+                both[p % 2, rows, :] = mine + other[there, :].astype(jnp.float32)
+
+            store(p).start()
+
+        for p in (panels - 2, panels - 1):
+            store(p).wait()
+
+    core_step(0, 1)
+    for turn in range(LEVELS):
+        core_step(turn, 0)
+    finish_norm()
+    for i in range(4):
+        gain_copy(i).start()
+        gain_add(i)
+    gain_copy(4).start()
+    for swap in swaps[1:]:
+        swap.start()
+    for turn in range(1, LEVELS):
+        core_step(turn, 1)
+    line_step(0)
+    gain_add(4)
+    gain_grads[...] = gains[...]
+    line_step(1)
+    expert_add(0)
+    line_step(2)
+    expert_add(1)
+    line_step(3)
     for a, plan in enumerate(plans):
         total_block(plan, totals[a])
+    expert_add(2)
     for plan in plans:
         plan.finish()
-
-
-def plane_sums(parts, collective_id, name):
+    for swap in swaps:
+        swap.wait_send()
+
+
+def sum_gradients(parts, expert_parts, first_part, norm_args, collective_id):
+    f32 = jnp.float32
     count = len(parts)
     shapes = [p.shape[1:] for p in parts]
     types = [p.dtype for p in parts]
+    hbm = pl.BlockSpec(memory_space=pl.ANY)
+    vmem = pl.BlockSpec(memory_space=pltpu.VMEM)
+    width = first_part.shape[2]
 
     def scratch(blocks):
         return [pltpu.VMEM((blocks,) + s, t) for s, t in zip(shapes, types)]
@@ -626,12 +776,20 @@
     def sems(blocks):
         return [pltpu.SemaphoreType.DMA((count, blocks))] * 2
 
+    bf16 = jnp.bfloat16
+    halves = [p.shape[1:] for p in expert_parts]
+    panels = [(2, 2**17 // h[1], h[1]) for h in halves]
     nbytes = sum(p.size * p.dtype.itemsize for p in parts)
-    return pl.pallas_call(
-        functools.partial(sums_kernel, count),
-        out_shape=[jax.ShapeDtypeStruct(s, jnp.float32) for s in shapes],
-        in_specs=[pl.BlockSpec(memory_space=pl.ANY)] * count,
-        out_specs=[pl.BlockSpec(memory_space=pltpu.VMEM)] * count,
+    outs = pl.pallas_call(
+        functools.partial(last_kernel, count),
+        out_shape=[jax.ShapeDtypeStruct(s, f32) for s in shapes]
+        + [jax.ShapeDtypeStruct(h, f32) for h in halves]
+        + [
+            jax.ShapeDtypeStruct(first_part.shape[1:], f32),
+            jax.ShapeDtypeStruct((8, width), f32),
+        ],
+        in_specs=[hbm] * (count + 3) + [vmem] * 6,
+        out_specs=[vmem] * count + [hbm] * 3 + [vmem] * 2,
         scratch_shapes=scratch(2 * LEVELS)
         + scratch(2 * LEVELS)
         + scratch(LEVELS)
@@ -639,13 +797,439 @@
         + sems(2 * LEVELS)
         + sems(LEVELS)
         + sems(LEVELS + 1)
-        + [pltpu.SemaphoreType.DMA((count, 2 * LEVELS))],
+        + [pltpu.SemaphoreType.DMA((count, 2 * LEVELS))]
+        + [
+            pltpu.VMEM(first_part.shape[1:], first_part.dtype),
+            pltpu.VMEM((8, width), f32),
+            pltpu.VMEM((5, 8, width), f32),
+        ]
+        + [pltpu.VMEM(h, bf16) for h in halves]
+        + [pltpu.VMEM(p, bf16) for p in panels]
+        + [pltpu.VMEM(p, f32) for p in panels]
+        + [
+            pltpu.SemaphoreType.DMA((4,)),
+            pltpu.SemaphoreType.DMA((4,)),
+            pltpu.SemaphoreType.DMA((2,)),
+            pltpu.SemaphoreType.DMA((2,)),
+            pltpu.SemaphoreType.DMA((5,)),
+            pltpu.SemaphoreType.DMA((5,)),
+        ],
         compiler_params=pltpu.CompilerParams(
-            collective_id=collective_id, has_side_effects=True, vmem_limit_bytes=60 * 2**20
+            collective_id=collective_id, has_side_effects=True, vmem_limit_bytes=67_043_328
         ),
         cost_estimate=pl.CostEstimate(flops=0, bytes_accessed=4 * nbytes, transcendentals=0),
-        name=name,
-    )(*parts)
+        name="sum_gradients",
+    )(*parts, *expert_parts, first_part, *norm_args)
+    return outs[:count], outs[count : count + 3], outs[count + 3], outs[count + 4]
+
+
+ROUTE_COLS = 128
+
+
+def nn(left, right):
+    return lax.dot_general(
+        left, right, (((1,), (0,)), ((), ())), preferred_element_type=jnp.float32
+    )
+
+
+def nt(left, right):
+    return lax.dot_general(
+        left, right, (((1,), (1,)), ((), ())), preferred_element_type=jnp.float32
+    )
+
+
+def tn(left, right):
+    return lax.dot_general(
+        left, right, (((0,), (0,)), ((), ())), preferred_element_type=jnp.float32
+    )
+
+
+def pair_block(ref, pair):
+    value = ref[pl.ds(2 * pair, 2)]
+    return value.reshape(value.shape[0] * value.shape[1], value.shape[2])
+
+
+def experts_kernel(
+    rows,
+    gates,
+    upstream_hbm,
+    gate_own,
+    up_own,
+    down_own,
+    gate_other,
+    up_other,
+    down_other,
+    second_cot,
+    mixture_hbm,
+    gate_part,
+    up_part,
+    down_part,
+    rows_all,
+    ubuf,
+    wg,
+    wu,
+    wd,
+    hidden,
+    gcot,
+    ucot,
+    rext,
+    tmp,
+    own,
+    from_core,
+    from_side,
+    from_line,
+    mstage,
+    gstage,
+    gather_s,
+    gather_r,
+    core_s,
+    core_r,
+    side_s,
+    side_r,
+    line_s,
+    line_r,
+    load_sems,
+    u_sems,
+    out_sems,
+):
+    bf16, f32 = jnp.bfloat16, jnp.float32
+    z, y, c, x = place()
+    top, bottom = line_ends(z)
+    interior = 1 - top - bottom
+    me = lax.axis_index("fsdp")
+    halves, width, units = wg.shape
+    half_rows = rows.shape[0]
+    pair_rows_ = 2 * half_rows
+    pairs = 2 * LEVELS
+    panel = 512
+
+    loads = [
+        pltpu.make_async_copy(src, dst, load_sems.at[i])
+        for i, (src, dst) in enumerate(
+            (
+                (rows, rows_all.at[me]),
+                (gate_own, wg.at[x]),
+                (up_own, wu.at[x]),
+                (down_own, wd.at[x]),
+                (gate_other, wg.at[1 - x]),
+                (up_other, wu.at[1 - x]),
+                (down_other, wd.at[1 - x]),
+            )
+        )
+    ]
+    for load in loads:
+        load.start()
+
+    plane_greet()
+    gather = PlaneGather(rows, rows_all, gather_s, gather_r)
+    sums = PlaneSums(
+        own,
+        from_core,
+        from_side,
+        from_line,
+        (core_s, core_r, side_s, side_r, line_s, line_r),
+        LEVELS,
+    )
+    gather.start()
+
+    def forward_pair(b):
+        step = (0b11_10_11_01_10_00_01_00 >> (2 * b)) % 4
+        side = (0b11_01_01_00 >> b) % 2
+        return level_at(3 - step, z) * 2 + (y + side) % 2
+
+    def u_load(b):
+        pair = forward_pair(b)
+        return pltpu.make_async_copy(
+            upstream_hbm.at[pl.ds(2 * pair, 2)], ubuf.at[b % 2], u_sems.at[b % 2]
+        )
+
+    u_load(0).start()
+    for load in loads:
+        load.wait()
+
+    @pl.loop(0, 2 * pairs)
+    def _(turn):
+        b, h = turn // 2, turn % 2
+
+        def at(k, work, where=None):
+            @pl.when(turn == k)
+            def _():
+                if where is None:
+                    work()
+                else:
+                    pl.when(where == 1)(work)
+
+        at(0, lambda: gather.from_core(0, 0))
+        at(2, lambda: gather.from_line(1))
+        at(2, lambda: gather.from_line(2), interior)
+        at(2, lambda: gather.from_core(1, 0))
+        at(4, lambda: gather.from_side(0))
+        at(4, lambda: gather.from_core(0, 1))
+        at(6, lambda: gather.from_line(2), 1 - interior)
+        at(6, lambda: gather.from_line(3), interior)
+        at(6, lambda: gather.from_core(2, 0))
+        at(8, lambda: gather.from_side(1))
+        at(8, lambda: gather.from_core(1, 1))
+        at(10, lambda: gather.from_line(3), 1 - interior)
+        at(10, lambda: gather.from_core(3, 0))
+        at(12, lambda: gather.from_side(2))
+        at(12, lambda: gather.from_core(2, 1))
+        at(14, lambda: gather.from_side(3))
+        at(14, lambda: gather.from_core(3, 1))
+
+        @pl.when(h == 0)
+        def _():
+            u_load(b).wait()
+
+            @pl.when(b + 1 < pairs)
+            def _():
+                u_load(b + 1).start()
+
+        pair = forward_pair(b)
+        xs = pair_block(rows_all, pair)
+        us = pair_block(ubuf.at[b % 2], 0)
+        lane = lax.broadcasted_iota(jnp.int32, (pair_rows_, ROUTE_COLS), 1)
+        table = gates[pl.ds(2 * pair, 2)].reshape(pair_rows_, ROUTE_COLS)
+        gate_rows = jnp.sum(jnp.where(lane == me, table, 0.0), axis=1, keepdims=True)
+        gate_act = nn(xs, wg[h])
+        up_act = nn(xs, wu[h])
+        hidden_cot = nt(us, wd[h])
+        sig = lax.logistic(gate_act)
+        act = gate_act * sig
+        hid = act * up_act
+        at_rows = pl.ds(pl.multiple_of(pair * pair_rows_, pair_rows_), pair_rows_)
+        hidden[h, at_rows, :] = (hid * gate_rows).astype(bf16)
+        route = jnp.sum(hid * hidden_cot, axis=1, keepdims=True)
+        scaled = hidden_cot * gate_rows
+        gcot[h, at_rows, :] = (scaled * up_act * (sig * (1.0 + gate_act * (1.0 - sig)))).astype(bf16)
+        ucot[h, at_rows, :] = (scaled * act).astype(bf16)
+        placed = jnp.where(lane == me, route, 0.0)
+
+        @pl.when(h == 0)
+        def _():
+            rext[pair] = placed
+
+        @pl.when(h == 1)
+        def _():
+            rext[pair] = rext[pair] + placed
+
+    def core_send(b):
+        return remote(
+            tmp.at[b % 2, 1 - c],
+            from_core.at[b],
+            core_s.at[b],
+            core_r.at[b],
+            (index_of(z, y, 1 - c), x),
+        )
+
+    def take_core(b):
+        core_send(b).wait_recv()
+        add_block(tmp.at[b % 2, c], from_core.at[b], own.at[b])
+
+        @pl.when(b < LEVELS)
+        def _():
+            remote(
+                own.at[b],
+                from_side.at[b],
+                side_s.at[b],
+                side_r.at[b],
+                (index_of(z, 1 - y, c), x),
+            ).start()
+
+    def line_step(turn):
+        sums.side_arrived(turn)
+        add_block(own.at[LEVELS + turn], from_side.at[turn], own.at[LEVELS + turn])
+        if turn < LEVELS - 1:
+            sums.to_line(turn)
+
+    def last_step():
+        line_step(LEVELS - 1)
+        total_block(sums, second_cot)
+
+    @pl.loop(0, pairs)
+    def _(b):
+        pl.when((b == pairs - 1) & (interior == 0))(lambda: line_step(0))
+        pl.when(b >= 2)(lambda: core_send(b - 2).wait_send())
+        pair = level_at(b % LEVELS, z) * 2 + (y + 1 - b // LEVELS) % 2
+        at_rows = pl.ds(pl.multiple_of(pair * pair_rows_, pair_rows_), pair_rows_)
+
+        @pl.loop(0, width // panel)
+        def _(n):
+            cols = pl.ds(pl.multiple_of(n * panel, panel), panel)
+            acc = nt(gcot[0, at_rows, :], wg[0, cols, :])
+            acc = acc + nt(ucot[0, at_rows, :], wu[0, cols, :])
+            for h in range(1, halves):
+                acc = acc + nt(gcot[h, at_rows, :], wg[h, cols, :])
+                acc = acc + nt(ucot[h, at_rows, :], wu[h, cols, :])
+            tmp[b % 2, :, :, cols] = acc.astype(bf16).reshape(2, half_rows, panel)
+
+        core_send(b).start()
+        pl.when(b >= 1)(lambda: take_core(b - 1))
+
+    take_core(pairs - 1)
+    for b in (pairs - 2, pairs - 1):
+        core_send(b).wait_send()
+
+    def mixture_out(b):
+        return pltpu.make_async_copy(
+            mstage.at[b % 2], mixture_hbm.at[pl.ds(2 * b, 2)], out_sems.at[b % 2]
+        )
+
+    @pl.loop(0, pairs)
+    def _(b):
+        pl.when((b == 3) & (interior == 0))(lambda: line_step(1))
+        pl.when((b == 5) & (interior == 1))(lambda: line_step(0))
+        pl.when(b >= 2)(lambda: mixture_out(b - 2).wait())
+        at_rows = pl.ds(pl.multiple_of(b * pair_rows_, pair_rows_), pair_rows_)
+
+        @pl.loop(0, width // panel)
+        def _(n):
+            cols = pl.ds(pl.multiple_of(n * panel, panel), panel)
+            acc = nn(hidden[0, at_rows, :], wd[0, :, cols])
+            for h in range(1, halves):
+                acc = acc + nn(hidden[h, at_rows, :], wd[h, :, cols])
+            mstage[b % 2, :, :, cols] = acc.astype(bf16).reshape(2, half_rows, panel)
+
+        mstage[b % 2, :, :, pl.ds(width, ROUTE_COLS)] = (
+            rext[b].astype(bf16).reshape(2, half_rows, ROUTE_COLS)
+        )
+        mixture_out(b).start()
+
+    for b in (pairs - 2, pairs - 1):
+        mixture_out(b).wait()
+
+    block = 256
+
+    def part_out(p, which):
+        ref = (gate_part, up_part)[which]
+        return pltpu.make_async_copy(
+            gstage.at[p % 2, which],
+            ref.at[:, pl.ds(pl.multiple_of(p * block, block), block), :],
+            out_sems.at[2 + 2 * which + p % 2],
+        )
+
+    def gradient_steps(p):
+        pl.when((p == 1) & (interior == 0))(lambda: line_step(2))
+        pl.when((p == 2) & (interior == 1))(lambda: line_step(1))
+        pl.when((p == 3) & (interior == 1))(lambda: line_step(2))
+        pl.when(p == 7)(last_step)
+
+    @pl.loop(0, width // block)
+    def _(p):
+        gradient_steps(p)
+
+        @pl.when(p >= 2)
+        def _():
+            for which in range(2):
+                part_out(p - 2, which).wait()
+
+        cols = pl.ds(pl.multiple_of(p * block, block), block)
+        xp = rows_all[:, :, cols]
+        xp = xp.reshape(xp.shape[0] * xp.shape[1], block)
+        for which, ref in enumerate((gcot, ucot)):
+            for h in range(halves):
+                gstage[p % 2, which, h] = tn(xp, ref[h]).astype(bf16)
+            part_out(p, which).start()
+
+    for p in (width // block - 2, width // block - 1):
+        for which in range(2):
+            part_out(p, which).wait()
+
+    gather.finish()
+    again = pltpu.make_async_copy(upstream_hbm, rows_all, load_sems.at[0])
+    again.start()
+    again.wait()
+    per_half = units // block
+
+    def down_out(p):
+        return pltpu.make_async_copy(
+            tmp.at[p % 2],
+            down_part.at[p // per_half, pl.ds(2 * (p % per_half), 2)],
+            out_sems.at[p % 2],
+        )
+
+    @pl.loop(0, halves * per_half)
+    def _(p):
+        pl.when(p >= 2)(lambda: down_out(p - 2).wait())
+        units_at = pl.ds(pl.multiple_of((p % per_half) * block, block), block)
+        us = rows_all[...]
+        us = us.reshape(us.shape[0] * us.shape[1], width)
+        part = tn(hidden[p // per_half, :, units_at], us)
+        tmp[p % 2] = part.astype(bf16).reshape(2, half_rows, width)
+        down_out(p).start()
+
+    for p in (halves * per_half - 2, halves * per_half - 1):
+        down_out(p).wait()
+    for turn in range(LEVELS):
+        remote(
+            own.at[turn], from_side.at[turn], side_s.at[turn], side_r.at[turn], (0, x)
+        ).wait_send()
+    for turn in range(LEVELS - 1):
+        remote(
+            own.at[turn], from_line.at[turn], line_s.at[turn], line_r.at[turn], (0, x)
+        ).wait_send()
+
+
+def run_experts(rows, gates, upstream_all, own_weights, other_weights, collective_id):
+    bf16, f32 = jnp.bfloat16, jnp.float32
+    half_rows, width = rows.shape
+    owner_count = upstream_all.shape[0]
+    units = own_weights[0].shape[1]
+    halves = lax.axis_size("tp")
+    all_rows = owner_count * half_rows
+    block = (half_rows, width)
+    hbm = pl.BlockSpec(memory_space=pl.ANY)
+    vmem = pl.BlockSpec(memory_space=pltpu.VMEM)
+    dma = pltpu.SemaphoreType.DMA
+    flops = 2 * 9 * all_rows * width * units * halves
+    return pl.pallas_call(
+        experts_kernel,
+        out_shape=[
+            jax.ShapeDtypeStruct(block, f32),
+            jax.ShapeDtypeStruct((owner_count, half_rows, width + ROUTE_COLS), bf16),
+            jax.ShapeDtypeStruct((halves, width, units), bf16),
+            jax.ShapeDtypeStruct((halves, width, units), bf16),
+            jax.ShapeDtypeStruct((halves, units // half_rows, half_rows, width), bf16),
+        ],
+        in_specs=[vmem, vmem] + [hbm] * 7,
+        out_specs=[vmem, hbm, hbm, hbm, hbm],
+        scratch_shapes=[
+            pltpu.VMEM((owner_count,) + block, bf16),
+            pltpu.VMEM((2, 2) + block, bf16),
+            pltpu.VMEM((halves, width, units), bf16),
+            pltpu.VMEM((halves, width, units), bf16),
+            pltpu.VMEM((halves, units, width), bf16),
+            pltpu.VMEM((halves, all_rows, units), bf16),
+            pltpu.VMEM((halves, all_rows, units), bf16),
+            pltpu.VMEM((halves, all_rows, units), bf16),
+            pltpu.VMEM((owner_count // 2, 2 * half_rows, ROUTE_COLS), f32),
+            pltpu.VMEM((2, 2) + block, bf16),
+            pltpu.VMEM((2 * LEVELS,) + block, bf16),
+            pltpu.VMEM((2 * LEVELS,) + block, bf16),
+            pltpu.VMEM((LEVELS,) + block, bf16),
+            pltpu.VMEM((LEVELS + 1,) + block, bf16),
+            pltpu.VMEM((2, 2, half_rows, width + ROUTE_COLS), bf16),
+            pltpu.VMEM((2, 2, halves, 256, units), bf16),
+            dma((GATHER_SENDS,)),
+            dma((owner_count,)),
+            dma((2 * LEVELS,)),
+            dma((2 * LEVELS,)),
+            dma((LEVELS,)),
+            dma((LEVELS,)),
+            dma((LEVELS + 1,)),
+            dma((LEVELS + 1,)),
+            dma((7,)),
+            dma((2,)),
+            dma((6,)),
+        ],
+        compiler_params=pltpu.CompilerParams(
+            collective_id=collective_id, has_side_effects=True, vmem_limit_bytes=67_043_328
+        ),
+        cost_estimate=pl.CostEstimate(
+            flops=flops, bytes_accessed=64 * 2**20, transcendentals=all_rows * units * halves
+        ),
+        name="experts",
+    )(rows, gates, upstream_all, *own_weights, *other_weights)
 
 
 def gate_columns(route_rows, gate_rows, expert_count):
@@ -685,28 +1269,28 @@
     bf16, f32 = jnp.bfloat16, jnp.float32
 
     my_routes, my_gates = half_of(routes), half_of(gate_values)
-    gate_table = lax.all_gather(
-        gate_columns(my_routes, my_gates, expert_count), "fsdp", axis=0, tiled=True
-    )
+    gate_table = gate_columns(my_routes, my_gates, ROUTE_COLS)
     expert_names = jnp.arange(expert_count, dtype=jnp.int32)[None, :]
-    gate_all = jnp.sum(
-        jnp.where(expert_names == lax.axis_index("fsdp"), gate_table, 0.0), axis=1, keepdims=True
-    )
-    gate_pair = lax.all_gather(gate_weight[0], "tp", axis=0)
-    up_pair = lax.all_gather(up_weight[0], "tp", axis=0)
-    down_pair = lax.all_gather(down_weight[0], "tp", axis=0)
+    own_weights = (gate_weight[0], up_weight[0], down_weight[0])
 
     first_scale = lax.rsqrt(jnp.mean(block_input * block_input, axis=1, keepdims=True) + epsilon)
     first_normed = (block_input * first_scale * first_gain).astype(bf16)
-    normed_rows = pair_rows(first_normed)
-    query_full, key_full, value_full, output_full, upstream_all = (
-        blocks.reshape(-1, blocks.shape[2])
-        for blocks in plane_gather(
-            [query_weight, key_weight, value_weight, output_weight, upstream_grad.astype(bf16)],
-            1,
-            "gather_weights",
-        )
-    )
+    gathered, normed_pair, other_weights = gather_weights(
+        [
+            query_weight,
+            key_weight,
+            value_weight,
+            output_weight,
+            upstream_grad.astype(bf16),
+            gate_table,
+        ],
+        first_normed,
+        own_weights,
+        1,
+    )
+    query_full, key_full, value_full, output_full = (w.reshape(-1, head_cols) for w in gathered[:4])
+    upstream_all, gates_all = gathered[4:]
+    normed_rows = normed_pair.reshape(seq_rows, model_width)
 
     def heads_of(weight_full):
         return (
@@ -727,44 +1311,9 @@
     second_scale = lax.rsqrt(jnp.mean(middle * middle, axis=1, keepdims=True) + epsilon)
     second_normed = (middle * second_scale * second_gain).astype(bf16)
 
-    (rows_all,) = plane_gather([second_normed], 2, "gather_rows")
-    rows_all = rows_all.reshape(-1, model_width)
-    gate_act = jnp.einsum("td,gdf->gtf", rows_all, gate_pair, preferred_element_type=f32)
-    up_act = jnp.einsum("td,gdf->gtf", rows_all, up_pair, preferred_element_type=f32)
-    sigmoid_gate = jax.nn.sigmoid(gate_act)
-    hidden = gate_act * sigmoid_gate * up_act
-    hidden_gated = (hidden * gate_all).astype(bf16)
-    mixture_part = jnp.einsum("gtf,gfd->td", hidden_gated, down_pair, preferred_element_type=f32)
-    hidden_cot = jnp.einsum("td,gfd->gtf", upstream_all, down_pair, preferred_element_type=f32)
-    route_sums = jnp.sum(hidden * hidden_cot, axis=(0, 2))
-    hidden_cot = hidden_cot * gate_all
-    gate_cot = (
-        hidden_cot * up_act * sigmoid_gate * (1.0 + gate_act * (1.0 - sigmoid_gate))
-    ).astype(bf16)
-    up_cot = (hidden_cot * gate_act * sigmoid_gate).astype(bf16)
-    input_cot = jnp.einsum("gtf,gdf->td", gate_cot, gate_pair, preferred_element_type=f32)
-    input_cot = input_cot + jnp.einsum("gtf,gdf->td", up_cot, up_pair, preferred_element_type=f32)
-    blocks = (owner_count, local_rows, model_width)
-    second_cot, mixture = plane_sums(
-        [input_cot.astype(bf16).reshape(blocks), mixture_part.astype(bf16).reshape(blocks)],
-        3,
-        "sum_rows",
-    )
-    block_output = middle + mixture
-    route_back = lax.all_to_all(
-        route_sums.reshape(owner_count, local_rows), "fsdp", split_axis=0, concat_axis=0, tiled=True
-    )
-    route_grad = jnp.sum(
-        jnp.where(my_routes[:, :, None] == expert_names[None], route_back.T[:, None, :], 0.0), axis=2
-    )
-    down_part = jnp.einsum("gtf,td->gfd", hidden_gated, upstream_all, preferred_element_type=f32)
-    gate_part = jnp.einsum("td,gtf->gdf", rows_all, gate_cot, preferred_element_type=f32)
-    up_part = jnp.einsum("td,gtf->gdf", rows_all, up_cot, preferred_element_type=f32)
-
-    def pair_grad(part):
-        return lax.psum_scatter(part.astype(bf16), "tp", scatter_dimension=0).astype(f32)
-
-    down_grad, gate_grad, up_grad = pair_grad(down_part), pair_grad(gate_part), pair_grad(up_part)
+    second_cot, mixture_part, gate_part, up_part, down_part = run_experts(
+        second_normed, gates_all, upstream_all, own_weights, other_weights, 2
+    )
 
     weighted_two = second_cot * second_gain
     second_term = jnp.sum(second_cot * middle * second_scale, axis=0)
@@ -805,18 +1354,7 @@
         + contract_cols(key_cot, key_full)
         + contract_cols(value_cot, value_full)
     )
-    first_cot = pair_sums(first_terms)
-    weighted_one = first_cot * first_gain
-    first_term = jnp.sum(first_cot * block_input * first_scale, axis=0)
-    input_grad = middle_grad + first_scale * (
-        weighted_one
-        - block_input
-        * first_scale
-        * first_scale
-        * jnp.mean(weighted_one * block_input, axis=1, keepdims=True)
-    )
-
-    query_grad, key_grad, value_grad, output_grad = plane_sums(
+    sums, expert_grads, input_grad, gain_grads = sum_gradients(
         [
             term.astype(bf16).reshape((owner_count,) + query_weight.shape)
             for term in (
@@ -825,16 +1363,25 @@
                 contract_rows(normed_rows, value_cot),
                 out_term,
             )
-        ],
+        ]
+        + [mixture_part],
+        (gate_part, up_part, down_part.reshape(pair_count, -1, model_width)),
+        first_terms.astype(bf16).reshape(pair_count, local_rows, model_width),
+        (block_input, first_scale, first_gain[None], middle_grad, second_term[None]),
         4,
-        "sum_gradients",
-    )
-    first_gain_grad, second_gain_grad = lax.psum((first_term, second_term), ("fsdp", "tp"))
+    )
+    query_grad, key_grad, value_grad, output_grad, mixture = sums
+    gate_grad, up_grad, down_grad = expert_grads
+    block_output = middle + mixture[:, :model_width]
+    route_back = mixture[:, model_width : model_width + expert_count]
+    route_grad = jnp.sum(
+        jnp.where(my_routes[:, :, None] == expert_names[None], route_back[:, None, :], 0.0), axis=2
+    )
     return (
         block_output,
         input_grad,
-        first_gain_grad,
-        second_gain_grad,
+        gain_grads[0],
+        gain_grads[1],
         query_grad,
         key_grad,
         value_grad,

time: 874 us -> 640 us (0.73)
  matrix products: 191 us -> 49.6 us
  waiting for transfers between devices: 144 us -> 51.4 us
  Pallas kernels: 397 us -> 479 us
  blocking collectives: 58.8 us -> 0 us
  other arithmetic: 35.6 us -> 17.4 us
    dot_general x9 -> x0, matrix products: 141 us -> none  [the longest x1 20.6 us: per_device_dense(): jnp.einsum('td,gfd->gtf', upstream_all, down_pair, preferred_element_type...]
    all_gather x3 -> x0, waiting for transfers between devices: 86.7 us -> none  [the longest x1 43.6 us: per_device_dense(): down_pair = lax.all_gather(down_weight[0], 'tp', axis=0)]
    pallas_call x4 -> x3, Pallas kernels: 397 us -> 479 us  [the longest x1 185 us: sum_gradients(): pl.pallas_call(functools.partial(last_kernel, count), out_shape=[jax.Shap...]
    psum x1 -> x0, blocking collectives: 40.8 us -> none  [per_device_dense(): lax.psum((first_term, second_term), ('fsdp', 'tp'))]
    all_gather x1 -> x0, blocking collectives: 18 us -> none  [per_device_dense(): lax.all_gather(gate_columns(my_routes, my_gates, expert_count), 'fsdp', a...]
    convert_element_type x2 -> x0, other arithmetic: 17 us -> none  [the longest x1 12.9 us: per_device_dense(): up_cot = (hidden_cot * gate_act * sigmoid_gate).astype(bf16)]
    reduce_scatter x2 -> x1, waiting for transfers between devices: 30.4 us -> 32.2 us  [pair_sums(): return lax.psum_scatter(term_block, 'tp', scatter_dimension=0, tiled=True)]
    unnamed x64 -> x84, local copies, waits for them, and re-layouts: 17.2 us -> 18.9 us
  transfers between devices with their start and end apart: 11 -> 2, of which waited for: 5 -> 2; matrix products, arithmetic and copies ran while one was open for 12% -> 0% of each run, Pallas kernels for 34% -> 0%
where the time goes in v3:
time: 640 us; the launch traced here: 638 us
  Pallas kernels  479 us (75%)
  waiting for transfers between devices  51.4 us (8%)
  matrix products  49.6 us (8%)
  local copies, waits for them, and re-layouts  26.5 us (4%)
  other arithmetic  17.4 us (3%)
  between operations  14.5 us (2%)
    pallas_call x1, Pallas kernels, sum_gradients(): pl.pallas_call(functools.partial(last_kernel, count), out_shape=[jax.Shap...  185 us
    pallas_call x1, Pallas kernels, gather_weights(): pl.pallas_call(functools.partial(weights_kernel, count), out_shape=[jax.S...  155 us
    pallas_call x1, Pallas kernels, run_experts(): pl.pallas_call(experts_kernel, out_shape=[jax.ShapeDtypeStruct(block, f32...  140 us
    reduce_scatter x1, waiting for transfers between devices, pair_sums(): return lax.psum_scatter(term_block, 'tp', scatter_dimension=0, tiled=True)  32.2 us
    all_gather x1, waiting for transfers between devices, pair_rows(): return lax.all_gather(row_block, 'tp', axis=0, tiled=True)  19.2 us
    unnamed x84, local copies, waits for them, and re-layouts  18.9 us
    dot_general x4, matrix products, contract_rows(): lax.dot_general(left_block, right_block, (((0,), (0,)), ((), ())), prefer...  13.4 us
  transfers between devices with their start and end apart: 2, of which 2 were waited for; matrix products, arithmetic and copies ran while one was open for 0% of the time, Pallas kernels for 0%

profile of v3, /device:TPU:0, one launch (start us, length us, event | category | flops | bytes accessed | tf_op | source)
XLA Modules:
  0.0 638.4 jit_solution(15041297878489938866)
XLA Ops:
  9.4 1.4 multiply_reduce_fusion.5
  11.3 2.1 convert_element_type.69.refs_4_
  15.3 154.6 %gather_weights.1 = (bf16[16,128,1024]{2,1,0:T(8,128)(2,1)}, bf16[16,128,1024]{2,1,0:T(8,128)(2,1)}, bf16[16,128,1024]{2,1,0:T(8,128)(2,1)}, bf16[16,128,1024]{2...) custom-call(bf16[128,1024]{1,0:T(8,128)(2,1)} %refs_0_.1, ...), custom_call_target="tpu_custom_call" | custom-call | bytes 104857600 | tf_op jit(solution)/shard_map/gather_weights/pallas_call | solution.py:472
  169.9 3.8 convolution_convert_fusion.7
  174.0 4.4 convolution_convert_fusion.8
  180.6 2.2 copy-done.35
  185.7 2.6 fusion.39
  188.5 32.2 %reduce-scatter.2.cloned.1.call-done = f32[128,2048]{1,0:T(8,128)} async-done(((f32[256,2048]{1,0:T(8,128)}), f32[128,2048]{1,0:T(8,128)}) %reduce-scatter.2.cloned.1.call-update) | async-done | bytes 1048592 | tf_op jit(solution)/shard_map/reduce_scatter | solution.py:33
  220.7 1.4 multiply_reduce_fusion.4
  224.0 139.5 %experts.1 = (f32[128,2048]{1,0:T(8,128)}, bf16[16,128,2176]{2,1,0:T(8,128)(2,1)}, bf16[2,2048,512]{2,1,0:T(8,128)(2,1)}, bf16[2,2048,512]{2,1,0:T(8,128)(2,1)}, bf16[2,4,128,2048]{3,2,1,0:T(8,128)(2,1)}) custom-call(bf16[128,2048]{1,0:T(8,128)(2,1)} %multiply_convert_fusion.1.rows, f32[16,128,128]{2,1,0:T(8,128)} %get-tuple-element.42.gates, ...), custom_call_target="tpu_custom_call" | custom-call | flops 77309411328 | bytes 67108864 | tf_op jit(solution)/shard_map/experts/pallas_call | solution.py:1185
  363.6 2.6 multiply_reduce_fusion.2
  366.2 2.7 fusion.37
  369.7 19.2 %all-gather.2.cloned.1.call-done = bf16[256,2048]{1,0:T(8,128)(2,1)} async-done(((bf16[128,2048]{1,0:T(8,128)(2,1)}), bf16[256,2048]{1,0:T(8,128)(2,1)}) %all-gather.2.cloned.1.call-update) | async-done | bytes 1048592 | tf_op jit(solution)/shard_map/all_gather | solution.py:29
  388.9 4.6 convolution_convert_fusion.6
  393.4 1.4 copy.63
  394.8 2.8 fusion.22
  397.6 4.1 fusion.11
  401.8 3.5 fusion.14
  406.3 3.6 fusion.40
  409.9 3.3 convolution_convert_fusion.3
  413.2 3.3 convolution_convert_fusion.2
  417.9 3.3 convolution_convert_fusion.1
  421.2 2.6 fusion.1
  423.8 3.4 convolution_convert_fusion
  427.2 184.9 %sum_gradients.1 = (f32[128,1024]{1,0:T(8,128)}, f32[128,1024]{1,0:T(8,128)}, f32[128,1024]{1,0:T(8,128)}, f32[128,1024]{1,0:T(8,128)}, f32[128,2176]{1,0:T(8,12...) custom-call(bf16[16,128,1024]{2,1,0:T(8,128)(2,1)} %bitcast.75, ...), custom_call_target="tpu_custom_call" | custom-call | bytes 102760448 | tf_op jit(solution)/shard_map/sum_gradients/pallas_call | solution.py:783
  612.1 2.8 slice_add_fusion
  616.4 1.5 fusion.38
  622.1 2.1 copy.86
  624.3 1.6 copy-done.9
  625.8 2.1 copy.87
  628.0 1.6 copy-done.8
  629.5 2.0 copy.88
  (105 shorter events, 20.7 us)
Async XLA Ops:
  7.2 7.2 %copy-start.6 = (f32[128,2048]{1,0:T(8,128)S(1)}, f32[128,2048]{1,0:T(8,128)}, u32[]{:S(2)}) copy-start(f32[128,2048]{1,0:T(8,128)} %refs_9_.1) | copy-start | bytes 3145732
  7.2 7.2 %copy-start.31 = (f32[2048]{0:T(1024)S(1)}, f32[2048]{0:T(1024)}, u32[]{:S(2)}) copy-start(f32[2048]{0:T(1024)} %param.15) | copy-start | bytes 24580
  7.2 213.5 %reduce-scatter.2.cloned.1.call-start = ((), (), s32[]{:S(2)}) async-start(), calls=%async_computation.1 | async-start | bytes 3145728 | tf_op jit(solution)/shard_map/reduce_scatter | solution.py:33
  169.9 4.1 copy-start.4
  174.0 5.7 copy-start.15
  179.7 3.1 copy-start.35
  180.2 3.9 copy-start
  180.6 3.5 copy-start.25
  182.8 2.9 copy-start.37
  188.4 34.7 %copy-start.27 = (f32[2048]{0:T(1024)S(1)}, f32[2048]{0:T(1024)}, u32[]{:S(2)}) copy-start(f32[2048]{0:T(1024)} %param.16) | copy-start | bytes 24580
  188.4 200.5 %all-gather.2.cloned.1.call-start = ((), (), s32[]{:S(2)}) async-start(), calls=%async_computation.2 | async-start | bytes 1572864 | tf_op jit(solution)/shard_map/all_gather | solution.py:29
  363.5 2.6 copy-start.3
  363.5 2.6 copy-start.11
  363.5 2.6 copy-start.28
  363.6 2.6 copy-start.33
  366.2 2.8 copy-start.34
  393.4 4.2 copy-start.1
  393.4 4.2 copy-start.16
  393.4 4.2 copy-start.26
  406.3 3.6 copy-start.5
  413.2 3.3 copy-start.7
  417.9 3.3 copy-start.36
  421.2 2.6 copy-start.12
  421.2 2.6 copy-start.14
  612.1 3.7 copy-start.30
  612.1 5.9 copy-start.19
  612.1 6.9 %copy-start.24 = (f32[128,1024]{1,0:T(8,128)S(1)}, f32[128,1024]{1,0:T(8,128)}, u32[]{:S(2)}) copy-start(f32[128,1024]{1,0:T(8,128)} %get-tuple-element.90) | copy-start | bytes 1572868
  612.1 7.6 %copy-start.23 = (f32[128,1024]{1,0:T(8,128)S(1)}, f32[128,1024]{1,0:T(8,128)}, u32[]{:S(2)}) copy-start(f32[128,1024]{1,0:T(8,128)} %get-tuple-element.91) | copy-start | bytes 1572868
  618.0 2.6 copy-start.22
  618.0 4.2 copy-start.10
  622.1 3.7 copy-start.9
  625.8 3.7 copy-start.8
  (8 other events, 9.4 us)
Sparse Core Ops, SparseCore 0:
  188.5 32.0 reduce-scatter.1
  369.1 19.7 all-gather.1

commit v4 on v3

--- a/solution.py
+++ b/solution.py
@@ -603,18 +603,16 @@
 
 def last_kernel(count, *refs):
     parts, refs = refs[:count], refs[count:]
-    expert_parts, refs = refs[:3], refs[3:]
+    expert_parts, refs = refs[:2], refs[2:]
     first_part, block_input, first_scale, first_gain, middle_grad, second_term = refs[:6]
     refs = refs[6:]
     totals, refs = refs[:count], refs[count:]
-    expert_grads, refs = refs[:3], refs[3:]
+    expert_landed, refs = refs[:2], refs[2:]
     input_grad, gain_grads, refs = refs[0], refs[1], refs[2:]
     buffers = [refs[i * count : (i + 1) * count] for i in range(4)]
     refs = refs[4 * count :]
     sems, own_sems, refs = refs[:6], refs[6], refs[7:]
-    first_other, gains, gains_in, refs = refs[0], refs[1], refs[2], refs[3:]
-    expert_other, expert_own, expert_sum = refs[:3], refs[3:6], refs[6:9]
-    pair_s, pair_r, load_sems, out_sems, gain_s, gain_r = refs[9:]
+    first_other, gains, gains_in, pair_s, pair_r, gain_s, gain_r = refs
     z, y, c, x = place()
     own = index_of(z, y, c)
     plane_greet(pair=True, far=True)
@@ -622,9 +620,9 @@
         PlaneSums(*(b[a] for b in buffers), tuple(s.at[a] for s in sems)) for a in range(count)
     ]
     swaps = [
-        remote(src.at[1 - x], dst, pair_s.at[i], pair_r.at[i], (own, 1 - x))
+        remote(src, dst, pair_s.at[i], pair_r.at[i], (own, 1 - x))
         for i, (src, dst) in enumerate(
-            [(first_part, first_other)] + list(zip(expert_parts, expert_other))
+            [(first_part.at[1 - x], first_other)] + list(zip(expert_parts, expert_landed))
         )
     ]
     swaps[0].start()
@@ -693,44 +691,6 @@
     def gain_add(i):
         gain_copy(i).wait()
         gains[...] = gains[...] + gains_in[i]
-
-    def expert_add(which):
-        other, grad = expert_other[which], expert_grads[which]
-        own_half, both = expert_own[which], expert_sum[which]
-        panel = own_half.shape[1]
-        panels = other.shape[0] // panel
-
-        def load(p):
-            rows = pl.ds(pl.multiple_of(p * panel, panel), panel)
-            return pltpu.make_async_copy(
-                expert_parts[which].at[x, rows], own_half.at[p % 2], load_sems.at[p % 2]
-            )
-
-        def store(p):
-            rows = pl.ds(pl.multiple_of(p * panel, panel), panel)
-            return pltpu.make_async_copy(both.at[p % 2], grad.at[rows], out_sems.at[p % 2])
-
-        load(0).start()
-        swaps[1 + which].wait_recv()
-
-        @pl.loop(0, panels)
-        def _(p):
-            load(p).wait()
-            pl.when(p + 1 < panels)(lambda: load(p + 1).start())
-            pl.when(p >= 2)(lambda: store(p - 2).wait())
-            at_panel = pl.multiple_of(p * panel, panel)
-
-            @pl.loop(0, panel // 16)
-            def _(i):
-                rows = pl.ds(pl.multiple_of(i * 16, 16), 16)
-                there = pl.ds(pl.multiple_of(at_panel + i * 16, 16), 16)
-                mine = own_half[p % 2, rows, :].astype(jnp.float32)
-                both[p % 2, rows, :] = mine + other[there, :].astype(jnp.float32)
-
-            store(p).start()
-
-        for p in (panels - 2, panels - 1):
-            store(p).wait()
 
     core_step(0, 1)
     for turn in range(LEVELS):
@@ -747,18 +707,15 @@
     line_step(0)
     gain_add(4)
     gain_grads[...] = gains[...]
-    line_step(1)
-    expert_add(0)
-    line_step(2)
-    expert_add(1)
-    line_step(3)
+    for turn in range(1, LEVELS):
+        line_step(turn)
     for a, plan in enumerate(plans):
         total_block(plan, totals[a])
-    expert_add(2)
     for plan in plans:
         plan.finish()
-    for swap in swaps:
-        swap.wait_send()
+    swaps[0].wait_send()
+    for swap in swaps[1:]:
+        swap.wait()
 
 
 def sum_gradients(parts, expert_parts, first_part, norm_args, collective_id):
@@ -776,20 +733,17 @@
     def sems(blocks):
         return [pltpu.SemaphoreType.DMA((count, blocks))] * 2
 
-    bf16 = jnp.bfloat16
-    halves = [p.shape[1:] for p in expert_parts]
-    panels = [(2, 2**17 // h[1], h[1]) for h in halves]
     nbytes = sum(p.size * p.dtype.itemsize for p in parts)
     outs = pl.pallas_call(
         functools.partial(last_kernel, count),
         out_shape=[jax.ShapeDtypeStruct(s, f32) for s in shapes]
-        + [jax.ShapeDtypeStruct(h, f32) for h in halves]
+        + [jax.ShapeDtypeStruct(p.shape, p.dtype) for p in expert_parts]
         + [
             jax.ShapeDtypeStruct(first_part.shape[1:], f32),
             jax.ShapeDtypeStruct((8, width), f32),
         ],
-        in_specs=[hbm] * (count + 3) + [vmem] * 6,
-        out_specs=[vmem] * count + [hbm] * 3 + [vmem] * 2,
+        in_specs=[hbm] * (count + 2) + [vmem] * 6,
+        out_specs=[vmem] * count + [hbm] * 2 + [vmem] * 2,
         scratch_shapes=scratch(2 * LEVELS)
         + scratch(2 * LEVELS)
         + scratch(LEVELS)
@@ -802,15 +756,8 @@
             pltpu.VMEM(first_part.shape[1:], first_part.dtype),
             pltpu.VMEM((8, width), f32),
             pltpu.VMEM((5, 8, width), f32),
-        ]
-        + [pltpu.VMEM(h, bf16) for h in halves]
-        + [pltpu.VMEM(p, bf16) for p in panels]
-        + [pltpu.VMEM(p, f32) for p in panels]
-        + [
-            pltpu.SemaphoreType.DMA((4,)),
-            pltpu.SemaphoreType.DMA((4,)),
-            pltpu.SemaphoreType.DMA((2,)),
-            pltpu.SemaphoreType.DMA((2,)),
+            pltpu.SemaphoreType.DMA((3,)),
+            pltpu.SemaphoreType.DMA((3,)),
             pltpu.SemaphoreType.DMA((5,)),
             pltpu.SemaphoreType.DMA((5,)),
         ],
@@ -820,7 +767,7 @@
         cost_estimate=pl.CostEstimate(flops=0, bytes_accessed=4 * nbytes, transcendentals=0),
         name="sum_gradients",
     )(*parts, *expert_parts, first_part, *norm_args)
-    return outs[:count], outs[count : count + 3], outs[count + 3], outs[count + 4]
+    return outs[:count], outs[count : count + 2], outs[count + 2], outs[count + 3]
 
 
 ROUTE_COLS = 128
@@ -850,8 +797,11 @@
 
 
 def experts_kernel(
-    rows,
     gates,
+    second_gain,
+    out_part,
+    block_input,
+    upstream,
     upstream_hbm,
     gate_own,
     up_own,
@@ -859,13 +809,19 @@
     gate_other,
     up_other,
     down_other,
-    second_cot,
+    middle,
+    middle_grad,
+    second_term,
+    middle_pair,
     mixture_hbm,
-    gate_part,
-    up_part,
-    down_part,
+    gate_mine,
+    gate_theirs,
+    up_mine,
+    up_theirs,
+    down_mine,
+    down_landed,
     rows_all,
-    ubuf,
+    u_all,
     wg,
     wu,
     wd,
@@ -874,12 +830,13 @@
     ucot,
     rext,
     tmp,
-    own,
     from_core,
     from_side,
     from_line,
-    mstage,
     gstage,
+    wide,
+    second_scale,
+    route_half,
     gather_s,
     gather_r,
     core_s,
@@ -889,63 +846,88 @@
     line_s,
     line_r,
     load_sems,
-    u_sems,
     out_sems,
+    pair_s,
+    pair_r,
 ):
     bf16, f32 = jnp.bfloat16, jnp.float32
     z, y, c, x = place()
     top, bottom = line_ends(z)
     interior = 1 - top - bottom
     me = lax.axis_index("fsdp")
+    partner = (me, 1 - x)
     halves, width, units = wg.shape
-    half_rows = rows.shape[0]
+    half_rows = middle.shape[0]
     pair_rows_ = 2 * half_rows
     pairs = 2 * LEVELS
     panel = 512
+    block = 256
+    step = 16
 
     loads = [
         pltpu.make_async_copy(src, dst, load_sems.at[i])
         for i, (src, dst) in enumerate(
             (
-                (rows, rows_all.at[me]),
+                (out_part.at[1 - x], middle_grad),
+                (out_part.at[x], middle),
+                (block_input, wide),
                 (gate_own, wg.at[x]),
                 (up_own, wu.at[x]),
                 (down_own, wd.at[x]),
                 (gate_other, wg.at[1 - x]),
                 (up_other, wu.at[1 - x]),
                 (down_other, wd.at[1 - x]),
+                (upstream_hbm, u_all),
             )
         )
     ]
     for load in loads:
         load.start()
 
-    plane_greet()
-    gather = PlaneGather(rows, rows_all, gather_s, gather_r)
+    plane_greet(pair=True)
+    gather = PlaneGather(rows_all.at[me], rows_all, gather_s, gather_r)
     sums = PlaneSums(
-        own,
+        from_core,
         from_core,
         from_side,
         from_line,
         (core_s, core_r, side_s, side_r, line_s, line_r),
         LEVELS,
     )
+
+    loads[0].wait()
+
+    @pl.loop(0, half_rows // step)
+    def _(i):
+        at = pl.ds(pl.multiple_of(i * step, step), step)
+        tmp[0, 0, at, :] = middle_grad[at, :].astype(bf16)
+
+    meet = remote(tmp.at[0, 0], tmp.at[0, 1], pair_s.at[0], pair_r.at[0], partner)
+    meet.start()
+    loads[1].wait()
+    loads[2].wait()
+    meet.wait_recv()
+    gain = second_gain[...]
+
+    @pl.loop(0, half_rows // step)
+    def _(i):
+        at = pl.ds(pl.multiple_of(i * step, step), step)
+        value = wide[at, :] + (middle[at, :] + tmp[0, 1, at, :].astype(f32))
+        scale = lax.rsqrt(jnp.mean(value * value, axis=1, keepdims=True) + epsilon)
+        middle[at, :] = value
+        second_scale[at, :] = scale
+        rows_all[me, at, :] = (value * scale * gain).astype(bf16)
+
     gather.start()
+    again = pltpu.make_async_copy(upstream, wide, load_sems.at[2])
+    again.start()
+    for load in loads[3:]:
+        load.wait()
 
     def forward_pair(b):
-        step = (0b11_10_11_01_10_00_01_00 >> (2 * b)) % 4
+        turn = (0b11_10_11_01_10_00_01_00 >> (2 * b)) % 4
         side = (0b11_01_01_00 >> b) % 2
-        return level_at(3 - step, z) * 2 + (y + side) % 2
-
-    def u_load(b):
-        pair = forward_pair(b)
-        return pltpu.make_async_copy(
-            upstream_hbm.at[pl.ds(2 * pair, 2)], ubuf.at[b % 2], u_sems.at[b % 2]
-        )
-
-    u_load(0).start()
-    for load in loads:
-        load.wait()
+        return level_at(3 - turn, z) * 2 + (y + side) % 2
 
     @pl.loop(0, 2 * pairs)
     def _(turn):
@@ -977,17 +959,9 @@
         at(14, lambda: gather.from_side(3))
         at(14, lambda: gather.from_core(3, 1))
 
-        @pl.when(h == 0)
-        def _():
-            u_load(b).wait()
-
-            @pl.when(b + 1 < pairs)
-            def _():
-                u_load(b + 1).start()
-
         pair = forward_pair(b)
         xs = pair_block(rows_all, pair)
-        us = pair_block(ubuf.at[b % 2], 0)
+        us = pair_block(u_all, pair)
         lane = lax.broadcasted_iota(jnp.int32, (pair_rows_, ROUTE_COLS), 1)
         table = gates[pl.ds(2 * pair, 2)].reshape(pair_rows_, ROUTE_COLS)
         gate_rows = jnp.sum(jnp.where(lane == me, table, 0.0), axis=1, keepdims=True)
@@ -1003,15 +977,53 @@
         scaled = hidden_cot * gate_rows
         gcot[h, at_rows, :] = (scaled * up_act * (sig * (1.0 + gate_act * (1.0 - sig)))).astype(bf16)
         ucot[h, at_rows, :] = (scaled * act).astype(bf16)
-        placed = jnp.where(lane == me, route, 0.0)
 
         @pl.when(h == 0)
         def _():
-            rext[pair] = placed
+            route_half[...] = route
 
         @pl.when(h == 1)
         def _():
-            rext[pair] = rext[pair] + placed
+            total = route_half[...] + route
+            placed = jnp.where(lane == me, total, 0.0).astype(bf16)
+            rext[pl.ds(2 * pair, 2)] = placed.reshape(2, half_rows, ROUTE_COLS)
+
+    def down_panel(h, p):
+        units_at = pl.ds(pl.multiple_of(p * block, block), block)
+        us = u_all[...]
+        us = us.reshape(us.shape[0] * us.shape[1], width)
+        return tn(hidden[h, :, units_at], us).astype(bf16)
+
+    def down_send(p, k):
+        rows = pl.ds(pl.multiple_of(p * block, block), block)
+        return remote(
+            gstage.at[p, k // 2, k % 2],
+            down_landed.at[rows, pl.ds(k * units, units)],
+            pair_s.at[2 + 4 * p + k],
+            pair_r.at[2 + 4 * p + k],
+            partner,
+        )
+
+    def down_keep(p):
+        rows = pl.ds(pl.multiple_of(2 * p, 2), 2)
+        return pltpu.make_async_copy(tmp.at[p], down_mine.at[rows], out_sems.at[p])
+
+    @pl.loop(0, units // block)
+    def _(p):
+        part = down_panel(1 - x, p)
+        for k in range(width // units):
+            gstage[p, k // 2, k % 2] = part[:, k * units : (k + 1) * units]
+            down_send(p, k).start()
+
+    meet.wait_send()
+
+    @pl.loop(0, units // block)
+    def _(p):
+        tmp[p] = down_panel(x, p).reshape(2, half_rows, width)
+        down_keep(p).start()
+
+    for p in range(units // block):
+        down_keep(p).wait()
 
     def core_send(b):
         return remote(
@@ -1024,12 +1036,12 @@
 
     def take_core(b):
         core_send(b).wait_recv()
-        add_block(tmp.at[b % 2, c], from_core.at[b], own.at[b])
+        add_block(tmp.at[b % 2, c], from_core.at[b], from_core.at[b])
 
         @pl.when(b < LEVELS)
         def _():
             remote(
-                own.at[b],
+                from_core.at[b],
                 from_side.at[b],
                 side_s.at[b],
                 side_r.at[b],
@@ -1038,13 +1050,36 @@
 
     def line_step(turn):
         sums.side_arrived(turn)
-        add_block(own.at[LEVELS + turn], from_side.at[turn], own.at[LEVELS + turn])
+        mine = from_core.at[LEVELS + turn]
+        add_block(mine, from_side.at[turn], mine)
         if turn < LEVELS - 1:
             sums.to_line(turn)
 
     def last_step():
         line_step(LEVELS - 1)
-        total_block(sums, second_cot)
+        total_block(sums, middle_grad)
+        again.wait()
+        second_term[...] = jnp.zeros_like(second_term)
+
+        @pl.loop(0, half_rows // step)
+        def _(i):
+            at = pl.ds(pl.multiple_of(i * step, step), step)
+            cot, mid, scale = middle_grad[at, :], middle[at, :], second_scale[at, :]
+            weighted = cot * gain
+            mean = jnp.mean(weighted * mid, axis=1, keepdims=True)
+            value = wide[at, :] + scale * (weighted - mid * (scale * scale * mean))
+            middle_grad[at, :] = value
+            tmp[0, 0, at, :] = value.astype(bf16)
+            second_term[...] = second_term[...] + jnp.sum(cot * mid * scale, axis=0, keepdims=True)
+
+        pair_send().start()
+        pair_keep().start()
+
+    def pair_send():
+        return remote(tmp.at[0, 0], middle_pair.at[x], pair_s.at[1], pair_r.at[1], partner)
+
+    def pair_keep():
+        return pltpu.make_async_copy(tmp.at[0, 0], middle_pair.at[x], load_sems.at[0])
 
     @pl.loop(0, pairs)
     def _(b):
@@ -1072,14 +1107,20 @@
 
     def mixture_out(b):
         return pltpu.make_async_copy(
-            mstage.at[b % 2], mixture_hbm.at[pl.ds(2 * b, 2)], out_sems.at[b % 2]
+            u_all.at[pl.ds(2 * b, 2)],
+            mixture_hbm.at[pl.ds(2 * b, 2), :, pl.ds(0, width)],
+            out_sems.at[b],
         )
+
+    route_out = pltpu.make_async_copy(
+        rext, mixture_hbm.at[:, :, pl.ds(width, ROUTE_COLS)], load_sems.at[1]
+    )
+    route_out.start()
 
     @pl.loop(0, pairs)
     def _(b):
         pl.when((b == 3) & (interior == 0))(lambda: line_step(1))
         pl.when((b == 5) & (interior == 1))(lambda: line_step(0))
-        pl.when(b >= 2)(lambda: mixture_out(b - 2).wait())
         at_rows = pl.ds(pl.multiple_of(b * pair_rows_, pair_rows_), pair_rows_)
 
         @pl.loop(0, width // panel)
@@ -1088,128 +1129,108 @@
             acc = nn(hidden[0, at_rows, :], wd[0, :, cols])
             for h in range(1, halves):
                 acc = acc + nn(hidden[h, at_rows, :], wd[h, :, cols])
-            mstage[b % 2, :, :, cols] = acc.astype(bf16).reshape(2, half_rows, panel)
-
-        mstage[b % 2, :, :, pl.ds(width, ROUTE_COLS)] = (
-            rext[b].astype(bf16).reshape(2, half_rows, ROUTE_COLS)
-        )
+            u_all[pl.ds(2 * b, 2), :, cols] = acc.astype(bf16).reshape(2, half_rows, panel)
+
         mixture_out(b).start()
 
-    for b in (pairs - 2, pairs - 1):
+    for b in range(pairs):
         mixture_out(b).wait()
-
-    block = 256
-
-    def part_out(p, which):
-        ref = (gate_part, up_part)[which]
-        return pltpu.make_async_copy(
-            gstage.at[p % 2, which],
-            ref.at[:, pl.ds(pl.multiple_of(p * block, block), block), :],
-            out_sems.at[2 + 2 * which + p % 2],
-        )
-
-    def gradient_steps(p):
+    route_out.wait()
+    for p in range(units // block):
+        for k in range(width // units):
+            down_send(p, k).wait()
+
+    def part_outs(p):
+        rows = pl.ds(pl.multiple_of(p * block, block), block)
+        return [
+            pltpu.make_async_copy(
+                gstage.at[p % 2, which, k], ref.at[rows, :], out_sems.at[(p % 2) * 4 + 2 * which + k]
+            )
+            for which, refs in enumerate(((gate_mine, gate_theirs), (up_mine, up_theirs)))
+            for k, ref in enumerate(refs)
+        ]
+
+    def wait_outs(p):
+        for copy in part_outs(p):
+            copy.wait()
+
+    @pl.loop(0, width // block)
+    def _(p):
         pl.when((p == 1) & (interior == 0))(lambda: line_step(2))
         pl.when((p == 2) & (interior == 1))(lambda: line_step(1))
         pl.when((p == 3) & (interior == 1))(lambda: line_step(2))
-        pl.when(p == 7)(last_step)
-
-    @pl.loop(0, width // block)
-    def _(p):
-        gradient_steps(p)
-
-        @pl.when(p >= 2)
-        def _():
-            for which in range(2):
-                part_out(p - 2, which).wait()
-
+        pl.when(p == 6)(last_step)
+        pl.when(p >= 2)(lambda: wait_outs(p - 2))
         cols = pl.ds(pl.multiple_of(p * block, block), block)
         xp = rows_all[:, :, cols]
         xp = xp.reshape(xp.shape[0] * xp.shape[1], block)
         for which, ref in enumerate((gcot, ucot)):
-            for h in range(halves):
-                gstage[p % 2, which, h] = tn(xp, ref[h]).astype(bf16)
-            part_out(p, which).start()
+            for k, h in enumerate((x, 1 - x)):
+                gstage[p % 2, which, k] = tn(xp, ref[h]).astype(bf16)
+        for copy in part_outs(p):
+            copy.start()
 
     for p in (width // block - 2, width // block - 1):
-        for which in range(2):
-            part_out(p, which).wait()
-
+        wait_outs(p)
+    pair_send().wait()
+    pair_keep().wait()
     gather.finish()
-    again = pltpu.make_async_copy(upstream_hbm, rows_all, load_sems.at[0])
-    again.start()
-    again.wait()
-    per_half = units // block
-
-    def down_out(p):
-        return pltpu.make_async_copy(
-            tmp.at[p % 2],
-            down_part.at[p // per_half, pl.ds(2 * (p % per_half), 2)],
-            out_sems.at[p % 2],
-        )
-
-    @pl.loop(0, halves * per_half)
-    def _(p):
-        pl.when(p >= 2)(lambda: down_out(p - 2).wait())
-        units_at = pl.ds(pl.multiple_of((p % per_half) * block, block), block)
-        us = rows_all[...]
-        us = us.reshape(us.shape[0] * us.shape[1], width)
-        part = tn(hidden[p // per_half, :, units_at], us)
-        tmp[p % 2] = part.astype(bf16).reshape(2, half_rows, width)
-        down_out(p).start()
-
-    for p in (halves * per_half - 2, halves * per_half - 1):
-        down_out(p).wait()
     for turn in range(LEVELS):
         remote(
-            own.at[turn], from_side.at[turn], side_s.at[turn], side_r.at[turn], (0, x)
+            from_core.at[turn], from_side.at[turn], side_s.at[turn], side_r.at[turn], partner
         ).wait_send()
     for turn in range(LEVELS - 1):
         remote(
-            own.at[turn], from_line.at[turn], line_s.at[turn], line_r.at[turn], (0, x)
+            from_core.at[turn], from_line.at[turn], line_s.at[turn], line_r.at[turn], partner
         ).wait_send()
 
 
-def run_experts(rows, gates, upstream_all, own_weights, other_weights, collective_id):
+def run_experts(
+    gates, second_gain, out_part, block_input, upstream, upstream_all, own, other, collective_id
+):
     bf16, f32 = jnp.bfloat16, jnp.float32
-    half_rows, width = rows.shape
+    block = block_input.shape
+    half_rows, width = block
     owner_count = upstream_all.shape[0]
-    units = own_weights[0].shape[1]
+    units = own[0].shape[1]
     halves = lax.axis_size("tp")
     all_rows = owner_count * half_rows
-    block = (half_rows, width)
     hbm = pl.BlockSpec(memory_space=pl.ANY)
     vmem = pl.BlockSpec(memory_space=pltpu.VMEM)
     dma = pltpu.SemaphoreType.DMA
     flops = 2 * 9 * all_rows * width * units * halves
+    shape = jax.ShapeDtypeStruct
     return pl.pallas_call(
         experts_kernel,
         out_shape=[
-            jax.ShapeDtypeStruct(block, f32),
-            jax.ShapeDtypeStruct((owner_count, half_rows, width + ROUTE_COLS), bf16),
-            jax.ShapeDtypeStruct((halves, width, units), bf16),
-            jax.ShapeDtypeStruct((halves, width, units), bf16),
-            jax.ShapeDtypeStruct((halves, units // half_rows, half_rows, width), bf16),
-        ],
-        in_specs=[vmem, vmem] + [hbm] * 7,
-        out_specs=[vmem, hbm, hbm, hbm, hbm],
+            shape(block, f32),
+            shape(block, f32),
+            shape((1, width), f32),
+            shape((2,) + block, bf16),
+            shape((owner_count, half_rows, width + ROUTE_COLS), bf16),
+        ]
+        + [shape((width, units), bf16)] * 4
+        + [shape((units // half_rows,) + block, bf16), shape((units, width), bf16)],
+        in_specs=[vmem, vmem] + [hbm] * 10,
+        out_specs=[vmem] * 3 + [hbm] * 8,
         scratch_shapes=[
             pltpu.VMEM((owner_count,) + block, bf16),
-            pltpu.VMEM((2, 2) + block, bf16),
+            pltpu.VMEM((owner_count,) + block, bf16),
             pltpu.VMEM((halves, width, units), bf16),
             pltpu.VMEM((halves, width, units), bf16),
             pltpu.VMEM((halves, units, width), bf16),
             pltpu.VMEM((halves, all_rows, units), bf16),
             pltpu.VMEM((halves, all_rows, units), bf16),
             pltpu.VMEM((halves, all_rows, units), bf16),
-            pltpu.VMEM((owner_count // 2, 2 * half_rows, ROUTE_COLS), f32),
+            pltpu.VMEM((owner_count, half_rows, ROUTE_COLS), bf16),
             pltpu.VMEM((2, 2) + block, bf16),
-            pltpu.VMEM((2 * LEVELS,) + block, bf16),
             pltpu.VMEM((2 * LEVELS,) + block, bf16),
             pltpu.VMEM((LEVELS,) + block, bf16),
             pltpu.VMEM((LEVELS + 1,) + block, bf16),
-            pltpu.VMEM((2, 2, half_rows, width + ROUTE_COLS), bf16),
             pltpu.VMEM((2, 2, halves, 256, units), bf16),
+            pltpu.VMEM(block, f32),
+            pltpu.VMEM((half_rows, 1), f32),
+            pltpu.VMEM((2 * half_rows, 1), f32),
             dma((GATHER_SENDS,)),
             dma((owner_count,)),
             dma((2 * LEVELS,)),
@@ -1218,9 +1239,10 @@
             dma((LEVELS,)),
             dma((LEVELS + 1,)),
             dma((LEVELS + 1,)),
-            dma((7,)),
-            dma((2,)),
-            dma((6,)),
+            dma((10,)),
+            dma((8,)),
+            dma((10,)),
+            dma((10,)),
         ],
         compiler_params=pltpu.CompilerParams(
             collective_id=collective_id, has_side_effects=True, vmem_limit_bytes=67_043_328
@@ -1229,7 +1251,7 @@
             flops=flops, bytes_accessed=64 * 2**20, transcendentals=all_rows * units * halves
         ),
         name="experts",
-    )(rows, gates, upstream_all, *own_weights, *other_weights)
+    )(gates, second_gain, out_part, block_input, upstream, upstream_all, *own, *other)
 
 
 def gate_columns(route_rows, gate_rows, expert_count):
@@ -1307,24 +1329,31 @@
     soft_rounded = soft_weights.astype(bf16)
     mixed_rows = jnp.einsum("hst,thd->shd", soft_rounded, value_rows, preferred_element_type=f32)
     mixed_rows = mixed_rows.astype(bf16).reshape(seq_rows, head_cols)
-    middle = block_input + pair_sums(contract_cols(mixed_rows, output_full))
-    second_scale = lax.rsqrt(jnp.mean(middle * middle, axis=1, keepdims=True) + epsilon)
-    second_normed = (middle * second_scale * second_gain).astype(bf16)
-
-    second_cot, mixture_part, gate_part, up_part, down_part = run_experts(
-        second_normed, gates_all, upstream_all, own_weights, other_weights, 2
-    )
-
-    weighted_two = second_cot * second_gain
-    second_term = jnp.sum(second_cot * middle * second_scale, axis=0)
-    middle_grad = upstream_grad + second_scale * (
-        weighted_two
-        - middle
-        * second_scale
-        * second_scale
-        * jnp.mean(weighted_two * middle, axis=1, keepdims=True)
-    )
-    middle_rows = pair_rows(middle_grad.astype(bf16))
+    out_part = contract_cols(mixed_rows, output_full).reshape(pair_count, local_rows, model_width)
+    (
+        middle,
+        middle_grad,
+        second_term,
+        middle_pair,
+        mixture_part,
+        gate_mine,
+        gate_theirs,
+        up_mine,
+        up_theirs,
+        down_mine,
+        down_landed,
+    ) = run_experts(
+        gates_all,
+        second_gain[None],
+        out_part,
+        block_input,
+        upstream_grad,
+        upstream_all,
+        own_weights,
+        other_weights,
+        2,
+    )
+    middle_rows = middle_pair.reshape(seq_rows, model_width)
     out_term = contract_rows(middle_rows, mixed_rows)
     mixed_cot = (
         jnp.dot(middle_rows, output_full, preferred_element_type=f32)
@@ -1354,7 +1383,7 @@
         + contract_cols(key_cot, key_full)
         + contract_cols(value_cot, value_full)
     )
-    sums, expert_grads, input_grad, gain_grads = sum_gradients(
+    sums, landed, input_grad, gain_grads = sum_gradients(
         [
             term.astype(bf16).reshape((owner_count,) + query_weight.shape)
             for term in (
@@ -1365,13 +1394,20 @@
             )
         ]
         + [mixture_part],
-        (gate_part, up_part, down_part.reshape(pair_count, -1, model_width)),
+        (gate_theirs, up_theirs),
         first_terms.astype(bf16).reshape(pair_count, local_rows, model_width),
-        (block_input, first_scale, first_gain[None], middle_grad, second_term[None]),
+        (block_input, first_scale, first_gain[None], middle_grad, second_term),
         4,
     )
     query_grad, key_grad, value_grad, output_grad, mixture = sums
-    gate_grad, up_grad, down_grad = expert_grads
+    gate_grad, up_grad, down_grad = (
+        mine.astype(f32) + theirs.astype(f32)
+        for mine, theirs in (
+            (gate_mine, landed[0]),
+            (up_mine, landed[1]),
+            (down_mine.reshape(down_landed.shape), down_landed),
+        )
+    )
     block_output = middle + mixture[:, :model_width]
     route_back = mixture[:, model_width : model_width + expert_count]
     route_grad = jnp.sum(

time: 640 us -> 561 us (0.88)
  waiting for transfers between devices: 51.4 us -> 0 us
  local copies, waits for them, and re-layouts: 26.5 us -> 13.2 us
  between operations: 14.5 us -> 1.43 us
  Pallas kernels: 479 us -> 466 us
    pallas_call x1, Pallas kernels: 185 us -> 151 us  [sum_gradients(): pl.pallas_call(functools.partial(last_kernel, count), out_shape=[jax.Shap...]
    reduce_scatter x1 -> x0, waiting for transfers between devices: 32.2 us -> none  [pair_sums(): return lax.psum_scatter(term_block, 'tp', scatter_dimension=0, tiled=True)]
    pallas_call x1, Pallas kernels: 140 us -> 161 us  [run_experts(): pl.pallas_call(experts_kernel, out_shape=[shape(block, f32), shape(block,...]
    all_gather x1 -> x0, waiting for transfers between devices: 19.2 us -> none  [pair_rows(): return lax.all_gather(row_block, 'tp', axis=0, tiled=True)]
    broadcast_in_dim x0 -> x2, other arithmetic: none -> 13.5 us  [the longest x1 8.31 us: per_device_dense(): up_grad[None]]
    unnamed x84 -> x65, local copies, waits for them, and re-layouts: 18.9 us -> 7.2 us
  transfers between devices with their start and end apart: 2 -> 0, of which waited for: 2 -> 0; matrix products, arithmetic and copies ran while one was open for 0% -> 0% of each run, Pallas kernels for 0% -> 0%
where the time goes in v4:
time: 561 us; the launch traced here: 554 us
  Pallas kernels  466 us (83%)
  matrix products  52.7 us (9%)
  other arithmetic  21 us (4%)
  local copies, waits for them, and re-layouts  13.2 us (2%)
    pallas_call x1, Pallas kernels, run_experts(): pl.pallas_call(experts_kernel, out_shape=[shape(block, f32), shape(block,...  161 us
    pallas_call x1, Pallas kernels, gather_weights(): pl.pallas_call(functools.partial(weights_kernel, count), out_shape=[jax.S...  155 us
    pallas_call x1, Pallas kernels, sum_gradients(): pl.pallas_call(functools.partial(last_kernel, count), out_shape=[jax.Shap...  151 us
    dot_general x4, matrix products, contract_cols(): lax.dot_general(left_block, right_block, (((1,), (1,)), ((), ())), prefer...  16.4 us
    dot_general x4, matrix products, contract_rows(): lax.dot_general(left_block, right_block, (((0,), (0,)), ((), ())), prefer...  13.5 us

profile of v4, /device:TPU:0, one launch (start us, length us, event | category | flops | bytes accessed | tf_op | source)
XLA Modules:
  0.0 554.1 jit_solution(18422674738800680088)
XLA Ops:
  0.7 0.8 constant_dynamic-slice_fusion.1
  2.9 1.0 select_reduce_fusion.refs_5_
  3.9 1.4 multiply_reduce_fusion.2
  5.8 1.6 multiply_convert_fusion.1.refs_6_
  7.4 0.9 convert_element_type.84.refs_4_
  8.3 154.6 %gather_weights.1 = (bf16[16,128,1024]{2,1,0:T(8,128)(2,1)}, bf16[16,128,1024]{2,1,0:T(8,128)(2,1)}, bf16[16,128,1024]{2,1,0:T(8,128)(2,1)}, bf16[16,128,1024]{2...) custom-call(bf16[128,1024]{1,0:T(8,128)(2,1)} %refs_0_.1, ...), custom_call_target="tpu_custom_call" | custom-call | bytes 104857600 | tf_op jit(solution)/shard_map/gather_weights/pallas_call | solution.py:472
  162.9 3.8 convolution_convert_fusion.7
  167.0 3.6 convolution_convert_fusion.8
  171.7 2.2 copy-done.27
  174.0 1.3 fusion.18
  176.2 4.9 fusion.25.out_part
  181.1 160.6 %experts.1 = (f32[128,2048]{1,0:T(8,128)}, f32[128,2048]{1,0:T(8,128)}, f32[1,2048]{1,0:T(1,128)}, bf16[2,128,2048]{2,1,0:T(8,128)(2,1)}, bf16[16,128,2176]{2,1,...) custom-call(f32[16,128,128]{2,1,0:T(8,128)} %get-tuple-element.42.ga, ...), custom_call_target="tpu_custom_call" | custom-call | flops 77309411328 | bytes 67108864 | tf_op jit(solution)/shard_map/experts/pallas_call | solution.py:1203
  341.7 5.2 fusion.1
  346.9 2.0 convolution_convert_fusion.6
  349.0 1.4 copy.65
  350.4 2.8 fusion.23
  353.2 4.1 fusion.12
  357.3 5.0 fusion.41
  362.3 3.5 fusion.15
  365.8 4.3 convolution_add_fusion.1
  370.6 2.3 fusion.2
  372.9 3.4 convolution_convert_fusion
  376.3 3.2 convolution_convert_fusion.1
  379.6 3.6 convolution_convert_fusion.2
  383.2 3.3 convolution_convert_fusion.3
  387.2 150.6 %sum_gradients.1 = (f32[128,1024]{1,0:T(8,128)}, f32[128,1024]{1,0:T(8,128)}, f32[128,1024]{1,0:T(8,128)}, f32[128,1024]{1,0:T(8,128)}, f32[128,2176]{1,0:T(8,12...) custom-call(bf16[16,128,1024]{2,1,0:T(8,128)(2,1)} %bitcast.87, ...), custom_call_target="tpu_custom_call" | custom-call | bytes 102760448 | tf_op jit(solution)/shard_map/sum_gradients/pallas_call | solution.py:737
  537.8 8.3 %add_bitcast_fusion = (f32[1,2048,512]{2,1,0:T(8,128)}, f32[1,2048,512]{2,1,0:T(8,128)}) fusion(bf16[2048,512]{1,0:T(8,128)(2,1)} %get-tuple-element.69, bf16[2048,512]{1,0:T(8,128)(2,1)} %get-tuple-element.68, bf16[2048,512]{1,0:T(8,128)(2,1)} %get-tuple-element.67, bf16[2048,512]{1,0:T(8,128)(2,1)} %get-tuple-element.66), kind=kLoop, calls=%fused_computation.3 | loop fusion | flops 6291456 | bytes 16777216 | tf_op jit(solution)/shard_map/broadcast_in_dim | solution.py:1426
  546.2 1.1 slice_add_fusion
  548.0 1.5 fusion.40
  549.5 1.0 copy.82
  550.5 0.8 copy.83
  552.1 0.8 copy.85
  (77 shorter events, 7.8 us)
Async XLA Ops:
  0.6 5.1 copy-start.4
  0.7 6.8 %copy-start.15 = (f32[128,2048]{1,0:T(8,128)S(1)}, f32[128,2048]{1,0:T(8,128)}, u32[]{:S(2)}) copy-start(f32[128,2048]{1,0:T(8,128)} %upstream.1) | copy-start | bytes 3145732
  1.5 0.6 copy-start.24
  162.9 4.1 copy-start.2
  166.9 3.9 copy-start.10
  170.8 0.9 copy-start.9
  170.8 3.1 copy-start.27
  171.3 3.9 copy-start
  171.7 3.5 copy-start.22
  175.3 0.8 copy-start.12
  176.1 5.0 copy-start.5
  341.7 5.2 copy-start.7
  341.7 5.2 copy-start.29
  349.0 4.2 copy-start.1
  349.0 4.2 copy-start.11
  349.0 4.2 copy-start.23
  365.7 4.9 copy-start.28
  370.6 2.3 copy-start.6
  370.6 2.3 copy-start.8
  372.9 3.4 copy-start.3
  379.5 3.6 copy-start.17
  383.2 3.3 copy-start.26
  537.8 8.3 %copy-start.13 = (f32[128,2176]{1,0:T(8,128)S(1)}, f32[128,2176]{1,0:T(8,128)}, u32[]{:S(2)}) copy-start(f32[128,2176]{1,0:T(8,128)} %get-tuple-element.59) | copy-start | bytes 3342340
  537.8 8.3 %copy-start.14 = (f32[128,2048]{1,0:T(8,128)S(1)}, f32[128,2048]{1,0:T(8,128)}, u32[]{:S(2)}) copy-start(f32[128,2048]{1,0:T(8,128)} %get-tuple-element.52) | copy-start | bytes 3145732
  546.2 1.2 copy-start.25
  546.2 3.3 copy-start.16
  546.2 4.3 copy-start.21
  547.3 4.0 copy-start.20
  549.5 2.6 copy-start.19
  550.5 2.4 copy-start.18

commit v5 on v4

--- a/solution.py
+++ b/solution.py
@@ -499,38 +499,6 @@
         self.core_s, self.core_r, self.side_s, self.side_r, self.line_s, self.line_r = sems
         self.z, self.y, self.c, self.x = place()
         self.top, self.bottom = line_ends(self.z)
-        self.sent = []
-
-    def slot_of(self, turn, side, core):
-        return index_of(level_at(turn, self.z), (self.y + side) % 2, (self.c + core) % 2)
-
-    def to_core(self, part, turn, side):
-        j = side * LEVELS + turn
-        copy = remote(
-            part,
-            self.from_core.at[j],
-            self.core_s.at[j],
-            self.core_r.at[j],
-            (index_of(self.z, self.y, 1 - self.c), self.x),
-        )
-        copy.start()
-        self.sent.append(copy)
-
-    def core_arrived(self, turn, side):
-        j = side * LEVELS + turn
-        here = self.from_core.at[j]
-        remote(here, here, self.core_s.at[j], self.core_r.at[j], (0, self.x)).wait_recv()
-
-    def to_side(self, turn):
-        copy = remote(
-            self.own.at[LEVELS + turn],
-            self.from_side.at[turn],
-            self.side_s.at[turn],
-            self.side_r.at[turn],
-            (index_of(self.z, 1 - self.y, self.c), self.x),
-        )
-        copy.start()
-        self.sent.append(copy)
 
     def side_arrived(self, turn):
         here = self.from_side.at[turn]
@@ -562,11 +530,6 @@
             (index_of(onward, y, c), x),
         )
         copy.start()
-        self.sent.append(copy)
-
-    def finish(self):
-        for copy in self.sent:
-            copy.wait_send()
 
 
 def add_block(one, two, out):
@@ -599,175 +562,6 @@
             def _(i):
                 rows = pl.ds(pl.multiple_of(i * step, step), step)
                 total[rows, :] = total[rows, :] + block[rows, :].astype(jnp.float32)
-
-
-def last_kernel(count, *refs):
-    parts, refs = refs[:count], refs[count:]
-    expert_parts, refs = refs[:2], refs[2:]
-    first_part, block_input, first_scale, first_gain, middle_grad, second_term = refs[:6]
-    refs = refs[6:]
-    totals, refs = refs[:count], refs[count:]
-    expert_landed, refs = refs[:2], refs[2:]
-    input_grad, gain_grads, refs = refs[0], refs[1], refs[2:]
-    buffers = [refs[i * count : (i + 1) * count] for i in range(4)]
-    refs = refs[4 * count :]
-    sems, own_sems, refs = refs[:6], refs[6], refs[7:]
-    first_other, gains, gains_in, pair_s, pair_r, gain_s, gain_r = refs
-    z, y, c, x = place()
-    own = index_of(z, y, c)
-    plane_greet(pair=True, far=True)
-    plans = [
-        PlaneSums(*(b[a] for b in buffers), tuple(s.at[a] for s in sems)) for a in range(count)
-    ]
-    swaps = [
-        remote(src, dst, pair_s.at[i], pair_r.at[i], (own, 1 - x))
-        for i, (src, dst) in enumerate(
-            [(first_part.at[1 - x], first_other)] + list(zip(expert_parts, expert_landed))
-        )
-    ]
-    swaps[0].start()
-    loads = {}
-    for a, plan in enumerate(plans):
-        for side in (1, 0):
-            for turn in range(LEVELS):
-                plan.to_core(parts[a].at[plan.slot_of(turn, side, 1)], turn, side)
-                j = side * LEVELS + turn
-                load = pltpu.make_async_copy(
-                    parts[a].at[plan.slot_of(turn, side, 0)], plan.own.at[j], own_sems.at[a, j]
-                )
-                load.start()
-                loads[a, j] = load
-
-    def core_step(turn, side):
-        for a, plan in enumerate(plans):
-            j = side * LEVELS + turn
-            loads[a, j].wait()
-            plan.core_arrived(turn, side)
-            add_block(plan.own.at[j], plan.from_core.at[j], plan.own.at[j])
-            if side == 1:
-                plan.to_side(turn)
-
-    def line_step(turn):
-        for plan in plans:
-            plan.side_arrived(turn)
-            add_block(plan.own.at[turn], plan.from_side.at[turn], plan.own.at[turn])
-            if turn < LEVELS - 1:
-                plan.to_line(turn)
-
-    def finish_norm():
-        swaps[0].wait_recv()
-        step = 16
-        width = input_grad.shape[1]
-        gains[...] = jnp.concatenate(
-            [jnp.zeros((1, width), jnp.float32), second_term[...], jnp.zeros((6, width), jnp.float32)],
-            axis=0,
-        )
-        gain = first_gain[...]
-
-        @pl.loop(0, input_grad.shape[0] // step)
-        def _(i):
-            rows = pl.ds(pl.multiple_of(i * step, step), step)
-            value = first_part[x, rows, :].astype(jnp.float32)
-            value = value + first_other[rows, :].astype(jnp.float32)
-            entry, scale = block_input[rows, :], first_scale[rows, :]
-            weighted = value * gain
-            mean = jnp.mean(weighted * entry, axis=1, keepdims=True)
-            input_grad[rows, :] = middle_grad[rows, :] + scale * (
-                weighted - entry * (scale * scale * mean)
-            )
-            gains[0:1, :] = gains[0:1, :] + jnp.sum(value * entry * scale, axis=0, keepdims=True)
-
-    hops = [
-        (index_of(z, y, 1 - c), x),
-        (own, 1 - x),
-        (index_of(z + 1 - 2 * (z % 2), y, c), x),
-        (index_of((z + 2) % LEVELS, y, c), x),
-        (index_of(z, 1 - y, c), x),
-    ]
-
-    def gain_copy(i):
-        return remote(gains, gains_in.at[i], gain_s.at[i], gain_r.at[i], hops[i])
-
-    def gain_add(i):
-        gain_copy(i).wait()
-        gains[...] = gains[...] + gains_in[i]
-
-    core_step(0, 1)
-    for turn in range(LEVELS):
-        core_step(turn, 0)
-    finish_norm()
-    for i in range(4):
-        gain_copy(i).start()
-        gain_add(i)
-    gain_copy(4).start()
-    for swap in swaps[1:]:
-        swap.start()
-    for turn in range(1, LEVELS):
-        core_step(turn, 1)
-    line_step(0)
-    gain_add(4)
-    gain_grads[...] = gains[...]
-    for turn in range(1, LEVELS):
-        line_step(turn)
-    for a, plan in enumerate(plans):
-        total_block(plan, totals[a])
-    for plan in plans:
-        plan.finish()
-    swaps[0].wait_send()
-    for swap in swaps[1:]:
-        swap.wait()
-
-
-def sum_gradients(parts, expert_parts, first_part, norm_args, collective_id):
-    f32 = jnp.float32
-    count = len(parts)
-    shapes = [p.shape[1:] for p in parts]
-    types = [p.dtype for p in parts]
-    hbm = pl.BlockSpec(memory_space=pl.ANY)
-    vmem = pl.BlockSpec(memory_space=pltpu.VMEM)
-    width = first_part.shape[2]
-
-    def scratch(blocks):
-        return [pltpu.VMEM((blocks,) + s, t) for s, t in zip(shapes, types)]
-
-    def sems(blocks):
-        return [pltpu.SemaphoreType.DMA((count, blocks))] * 2
-
-    nbytes = sum(p.size * p.dtype.itemsize for p in parts)
-    outs = pl.pallas_call(
-        functools.partial(last_kernel, count),
-        out_shape=[jax.ShapeDtypeStruct(s, f32) for s in shapes]
-        + [jax.ShapeDtypeStruct(p.shape, p.dtype) for p in expert_parts]
-        + [
-            jax.ShapeDtypeStruct(first_part.shape[1:], f32),
-            jax.ShapeDtypeStruct((8, width), f32),
-        ],
-        in_specs=[hbm] * (count + 2) + [vmem] * 6,
-        out_specs=[vmem] * count + [hbm] * 2 + [vmem] * 2,
-        scratch_shapes=scratch(2 * LEVELS)
-        + scratch(2 * LEVELS)
-        + scratch(LEVELS)
-        + scratch(LEVELS + 1)
-        + sems(2 * LEVELS)
-        + sems(LEVELS)
-        + sems(LEVELS + 1)
-        + [pltpu.SemaphoreType.DMA((count, 2 * LEVELS))]
-        + [
-            pltpu.VMEM(first_part.shape[1:], first_part.dtype),
-            pltpu.VMEM((8, width), f32),
-            pltpu.VMEM((5, 8, width), f32),
-            pltpu.SemaphoreType.DMA((3,)),
-            pltpu.SemaphoreType.DMA((3,)),
-            pltpu.SemaphoreType.DMA((5,)),
-            pltpu.SemaphoreType.DMA((5,)),
-        ],
-        compiler_params=pltpu.CompilerParams(
-            collective_id=collective_id, has_side_effects=True, vmem_limit_bytes=67_043_328
-        ),
-        cost_estimate=pl.CostEstimate(flops=0, bytes_accessed=4 * nbytes, transcendentals=0),
-        name="sum_gradients",
-    )(*parts, *expert_parts, first_part, *norm_args)
-    return outs[:count], outs[count : count + 2], outs[count + 2], outs[count + 3]
 
 
 ROUTE_COLS = 128
@@ -819,6 +613,7 @@
     up_mine,
     up_theirs,
     down_mine,
+    down_theirs,
     down_landed,
     rows_all,
     u_all,
@@ -871,13 +666,13 @@
                 (out_part.at[1 - x], middle_grad),
                 (out_part.at[x], middle),
                 (block_input, wide),
+                (down_own, wd.at[x]),
+                (down_other, wd.at[1 - x]),
+                (upstream_hbm, u_all),
                 (gate_own, wg.at[x]),
                 (up_own, wu.at[x]),
-                (down_own, wd.at[x]),
                 (gate_other, wg.at[1 - x]),
                 (up_other, wu.at[1 - x]),
-                (down_other, wd.at[1 - x]),
-                (upstream_hbm, u_all),
             )
         )
     ]
@@ -904,9 +699,17 @@
 
     meet = remote(tmp.at[0, 0], tmp.at[0, 1], pair_s.at[0], pair_r.at[0], partner)
     meet.start()
-    loads[1].wait()
-    loads[2].wait()
-    meet.wait_recv()
+    for load in loads[1:6]:
+        load.wait()
+
+    @pl.loop(0, pairs)
+    def _(b):
+        at_rows = pl.ds(pl.multiple_of(b * pair_rows_, pair_rows_), pair_rows_)
+        us = pair_block(u_all, b)
+        for h in range(halves):
+            ucot[h, at_rows, :] = nt(us, wd[h]).astype(bf16)
+
+    meet.wait()
     gain = second_gain[...]
 
     @pl.loop(0, half_rows // step)
@@ -921,13 +724,20 @@
     gather.start()
     again = pltpu.make_async_copy(upstream, wide, load_sems.at[2])
     again.start()
-    for load in loads[3:]:
+    for load in loads[6:]:
         load.wait()
 
     def forward_pair(b):
         turn = (0b11_10_11_01_10_00_01_00 >> (2 * b)) % 4
         side = (0b11_01_01_00 >> b) % 2
         return level_at(3 - turn, z) * 2 + (y + side) % 2
+
+    def mixture_out(b):
+        return pltpu.make_async_copy(
+            tmp.at[b % 2],
+            mixture_hbm.at[pl.ds(2 * forward_pair(b), 2), :, pl.ds(0, width)],
+            out_sems.at[b % 2],
+        )
 
     @pl.loop(0, 2 * pairs)
     def _(turn):
@@ -961,17 +771,16 @@
 
         pair = forward_pair(b)
         xs = pair_block(rows_all, pair)
-        us = pair_block(u_all, pair)
         lane = lax.broadcasted_iota(jnp.int32, (pair_rows_, ROUTE_COLS), 1)
         table = gates[pl.ds(2 * pair, 2)].reshape(pair_rows_, ROUTE_COLS)
         gate_rows = jnp.sum(jnp.where(lane == me, table, 0.0), axis=1, keepdims=True)
         gate_act = nn(xs, wg[h])
         up_act = nn(xs, wu[h])
-        hidden_cot = nt(us, wd[h])
+        at_rows = pl.ds(pl.multiple_of(pair * pair_rows_, pair_rows_), pair_rows_)
+        hidden_cot = ucot[h, at_rows, :].astype(f32)
         sig = lax.logistic(gate_act)
         act = gate_act * sig
         hid = act * up_act
-        at_rows = pl.ds(pl.multiple_of(pair * pair_rows_, pair_rows_), pair_rows_)
         hidden[h, at_rows, :] = (hid * gate_rows).astype(bf16)
         route = jnp.sum(hid * hidden_cot, axis=1, keepdims=True)
         scaled = hidden_cot * gate_rows
@@ -988,42 +797,20 @@
             placed = jnp.where(lane == me, total, 0.0).astype(bf16)
             rext[pl.ds(2 * pair, 2)] = placed.reshape(2, half_rows, ROUTE_COLS)
 
-    def down_panel(h, p):
-        units_at = pl.ds(pl.multiple_of(p * block, block), block)
-        us = u_all[...]
-        us = us.reshape(us.shape[0] * us.shape[1], width)
-        return tn(hidden[h, :, units_at], us).astype(bf16)
-
-    def down_send(p, k):
-        rows = pl.ds(pl.multiple_of(p * block, block), block)
-        return remote(
-            gstage.at[p, k // 2, k % 2],
-            down_landed.at[rows, pl.ds(k * units, units)],
-            pair_s.at[2 + 4 * p + k],
-            pair_r.at[2 + 4 * p + k],
-            partner,
-        )
-
-    def down_keep(p):
-        rows = pl.ds(pl.multiple_of(2 * p, 2), 2)
-        return pltpu.make_async_copy(tmp.at[p], down_mine.at[rows], out_sems.at[p])
-
-    @pl.loop(0, units // block)
-    def _(p):
-        part = down_panel(1 - x, p)
-        for k in range(width // units):
-            gstage[p, k // 2, k % 2] = part[:, k * units : (k + 1) * units]
-            down_send(p, k).start()
-
-    meet.wait_send()
-
-    @pl.loop(0, units // block)
-    def _(p):
-        tmp[p] = down_panel(x, p).reshape(2, half_rows, width)
-        down_keep(p).start()
-
-    for p in range(units // block):
-        down_keep(p).wait()
+            pl.when(b >= 2)(lambda: mixture_out(b - 2).wait())
+
+            @pl.loop(0, width // panel)
+            def _(n):
+                cols = pl.ds(pl.multiple_of(n * panel, panel), panel)
+                acc = nn(hidden[0, at_rows, :], wd[0, :, cols])
+                for h in range(1, halves):
+                    acc = acc + nn(hidden[h, at_rows, :], wd[h, :, cols])
+                tmp[b % 2, :, :, cols] = acc.astype(bf16).reshape(2, half_rows, panel)
+
+            mixture_out(b).start()
+
+    for b in (pairs - 2, pairs - 1):
+        mixture_out(b).wait()
 
     def core_send(b):
         return remote(
@@ -1105,40 +892,30 @@
     for b in (pairs - 2, pairs - 1):
         core_send(b).wait_send()
 
-    def mixture_out(b):
-        return pltpu.make_async_copy(
-            u_all.at[pl.ds(2 * b, 2)],
-            mixture_hbm.at[pl.ds(2 * b, 2), :, pl.ds(0, width)],
-            out_sems.at[b],
-        )
-
     route_out = pltpu.make_async_copy(
         rext, mixture_hbm.at[:, :, pl.ds(width, ROUTE_COLS)], load_sems.at[1]
     )
     route_out.start()
-
-    @pl.loop(0, pairs)
-    def _(b):
-        pl.when((b == 3) & (interior == 0))(lambda: line_step(1))
-        pl.when((b == 5) & (interior == 1))(lambda: line_step(0))
-        at_rows = pl.ds(pl.multiple_of(b * pair_rows_, pair_rows_), pair_rows_)
-
-        @pl.loop(0, width // panel)
-        def _(n):
-            cols = pl.ds(pl.multiple_of(n * panel, panel), panel)
-            acc = nn(hidden[0, at_rows, :], wd[0, :, cols])
-            for h in range(1, halves):
-                acc = acc + nn(hidden[h, at_rows, :], wd[h, :, cols])
-            u_all[pl.ds(2 * b, 2), :, cols] = acc.astype(bf16).reshape(2, half_rows, panel)
-
-        mixture_out(b).start()
-
-    for b in range(pairs):
-        mixture_out(b).wait()
-    route_out.wait()
-    for p in range(units // block):
-        for k in range(width // units):
-            down_send(p, k).wait()
+    down_send = remote(
+        wd.at[0, pl.ds(0, block)], down_landed, pair_s.at[2], pair_r.at[2], partner
+    )
+    down_later = pltpu.make_async_copy(wd.at[0, pl.ds(block, block)], down_theirs, load_sems.at[3])
+    down_keep = pltpu.make_async_copy(wd.at[1], down_mine, load_sems.at[4])
+
+    @pl.loop(0, 2 * units // block)
+    def _(p):
+        other, q = p // (units // block), p % (units // block)
+        pl.when((p == 1) & (interior == 0))(lambda: line_step(1))
+        pl.when((p == 2) & (interior == 1))(lambda: line_step(0))
+        units_at = pl.ds(pl.multiple_of(q * block, block), block)
+        us = u_all[...]
+        us = us.reshape(us.shape[0] * us.shape[1], width)
+        h = (1 - x) * (1 - other) + x * other
+        wd[other, units_at, :] = tn(hidden[h, :, units_at], us).astype(bf16)
+        pl.when(p == 0)(down_send.start)
+        pl.when(p == 1)(down_later.start)
+
+    down_keep.start()
 
     def part_outs(p):
         rows = pl.ds(pl.multiple_of(p * block, block), block)
@@ -1157,8 +934,8 @@
     @pl.loop(0, width // block)
     def _(p):
         pl.when((p == 1) & (interior == 0))(lambda: line_step(2))
-        pl.when((p == 2) & (interior == 1))(lambda: line_step(1))
-        pl.when((p == 3) & (interior == 1))(lambda: line_step(2))
+        pl.when((p == 1) & (interior == 1))(lambda: line_step(1))
+        pl.when((p == 2) & (interior == 1))(lambda: line_step(2))
         pl.when(p == 6)(last_step)
         pl.when(p >= 2)(lambda: wait_outs(p - 2))
         cols = pl.ds(pl.multiple_of(p * block, block), block)
@@ -1174,6 +951,10 @@
         wait_outs(p)
     pair_send().wait()
     pair_keep().wait()
+    route_out.wait()
+    down_send.wait()
+    down_later.wait()
+    down_keep.wait()
     gather.finish()
     for turn in range(LEVELS):
         remote(
@@ -1210,9 +991,10 @@
             shape((owner_count, half_rows, width + ROUTE_COLS), bf16),
         ]
         + [shape((width, units), bf16)] * 4
-        + [shape((units // half_rows,) + block, bf16), shape((units, width), bf16)],
+        + [shape((units, width), bf16)]
+        + [shape((256, width), bf16)] * 2,
         in_specs=[vmem, vmem] + [hbm] * 10,
-        out_specs=[vmem] * 3 + [hbm] * 8,
+        out_specs=[vmem] * 3 + [hbm] * 9,
         scratch_shapes=[
             pltpu.VMEM((owner_count,) + block, bf16),
             pltpu.VMEM((owner_count,) + block, bf16),
@@ -1241,8 +1023,8 @@
             dma((LEVELS + 1,)),
             dma((10,)),
             dma((8,)),
-            dma((10,)),
-            dma((10,)),
+            dma((3,)),
+            dma((3,)),
         ],
         compiler_params=pltpu.CompilerParams(
             collective_id=collective_id, has_side_effects=True, vmem_limit_bytes=67_043_328
@@ -1252,6 +1034,393 @@
         ),
         name="experts",
     )(gates, second_gain, out_part, block_input, upstream, upstream_all, *own, *other)
+
+
+def last_kernel(
+    mixture_part,
+    middle_pair,
+    normed_pair,
+    mixed_rows,
+    query_rows,
+    key_rows,
+    value_rows,
+    output_full,
+    query_full,
+    key_full,
+    value_full,
+    gate_theirs,
+    up_theirs,
+    down_theirs,
+    block_input,
+    first_scale,
+    first_gain,
+    middle_grad,
+    second_term,
+    query_total,
+    key_total,
+    value_total,
+    output_total,
+    mixture_total,
+    gate_landed,
+    up_landed,
+    down_landed,
+    input_grad,
+    gain_grads,
+    wide_core,
+    wide_side,
+    wide_line,
+    wide_own,
+    from_core,
+    from_side,
+    from_line,
+    tmp,
+    mixed_cot,
+    query_cot,
+    key_cot,
+    value_cot,
+    weight_one,
+    weight_two,
+    first_terms,
+    first_mine,
+    first_other,
+    gains,
+    gains_in,
+    core_s,
+    core_r,
+    side_s,
+    side_r,
+    line_s,
+    line_r,
+    own_sems,
+    load_sems,
+    pair_s,
+    pair_r,
+    gain_s,
+    gain_r,
+):
+    bf16, f32 = jnp.bfloat16, jnp.float32
+    z, y, c, x = place()
+    own = index_of(z, y, c)
+    rows, head_cols = mixed_rows.shape
+    half_rows, width = input_grad.shape
+    pairs = 2 * LEVELS
+    inv_root = HD ** (-0.5)
+    plane_greet(pair=True, far=True)
+
+    def swap(i, src, dst):
+        return remote(src, dst, pair_s.at[i], pair_r.at[i], (own, 1 - x))
+
+    expert_swaps = (
+        swap(0, gate_theirs, gate_landed),
+        swap(1, up_theirs, up_landed),
+        swap(2, down_theirs, down_landed),
+    )
+    first_swap = swap(3, first_mine, first_other)
+
+    def load(i, src, dst):
+        return pltpu.make_async_copy(src, dst, load_sems.at[i])
+
+    output_load, query_load = load(0, output_full, weight_one), load(1, query_full, weight_two)
+    value_load, key_load = load(2, value_full, weight_one), load(3, key_full, weight_two)
+    sums = [
+        PlaneSums(
+            core,
+            core,
+            side,
+            line,
+            tuple(s.at[a] for s in (core_s, core_r, side_s, side_r, line_s, line_r)),
+            LEVELS,
+        )
+        for a, (core, side, line) in enumerate(
+            [(wide_core, wide_side, wide_line)]
+            + [(from_core.at[i], from_side.at[i], from_line.at[i]) for i in range(4)]
+        )
+    ]
+
+    def slot_at(b, core):
+        level, side = level_at(b % LEVELS, z), (y + 1 - b // LEVELS) % 2
+        return index_of(level, side, (c + core) % 2)
+
+    def core_copy(a, b, src):
+        plan = sums[a]
+        return remote(
+            src,
+            plan.from_core.at[b],
+            plan.core_s.at[b],
+            plan.core_r.at[b],
+            (index_of(z, y, 1 - c), x),
+        )
+
+    def side_copy(a, b):
+        plan = sums[a]
+        return remote(
+            plan.from_core.at[b],
+            plan.from_side.at[b],
+            plan.side_s.at[b],
+            plan.side_r.at[b],
+            (index_of(z, 1 - y, c), x),
+        )
+
+    def line_step(a, turn):
+        plan = sums[a]
+        plan.side_arrived(turn)
+        mine = plan.from_core.at[LEVELS + turn]
+        add_block(mine, plan.from_side.at[turn], mine)
+        if turn < LEVELS - 1:
+            plan.to_line(turn)
+
+    for copy in expert_swaps[:2]:
+        copy.start()
+    output_load.start()
+    query_load.start()
+
+    def wide_load(b):
+        return pltpu.make_async_copy(
+            mixture_part.at[slot_at(b, 0)], wide_own.at[b], own_sems.at[b]
+        )
+
+    @pl.loop(0, pairs)
+    def _(b):
+        core_copy(0, b, mixture_part.at[slot_at(b, 1)]).start()
+        wide_load(b).start()
+
+    @pl.loop(0, pairs)
+    def _(b):
+        wide_load(b).wait()
+        core_copy(0, b, mixture_part.at[slot_at(b, 1)]).wait_recv()
+        add_block(wide_own.at[b], wide_core.at[b], wide_core.at[b])
+        pl.when(b < LEVELS)(lambda: side_copy(0, b).start())
+
+    def flat(ref):
+        value = ref[...]
+        return value.reshape(value.shape[0] * value.shape[1], value.shape[2])
+
+    output_load.wait()
+    mixed_cot[...] = nn(flat(middle_pair), flat(weight_one)).astype(bf16)
+    value_load.start()
+
+    def term(a, left, cot):
+        def send(b):
+            return core_copy(a, b, tmp.at[b % 2, 1 - c])
+
+        def take(b):
+            core = sums[a].from_core.at[b]
+            send(b).wait_recv()
+            add_block(tmp.at[b % 2, c], core, core)
+            pl.when(b < LEVELS)(lambda: side_copy(a, b).start())
+
+        @pl.loop(0, pairs)
+        def _(b):
+            pl.when(b >= 2)(lambda: send(b - 2).wait_send())
+            pair = level_at(b % LEVELS, z) * 2 + (y + 1 - b // LEVELS) % 2
+            cols = pl.ds(pl.multiple_of(pair * 2 * half_rows, 2 * half_rows), 2 * half_rows)
+            lhs = left[:, :, cols].reshape(rows, 2 * half_rows)
+            part = tn(lhs, cot[...])
+            tmp[b % 2] = part.astype(bf16).reshape(2, half_rows, head_cols)
+            send(b).start()
+            pl.when(b >= 1)(lambda: take(b - 1))
+
+        take(pairs - 1)
+        for b in (pairs - 2, pairs - 1):
+            send(b).wait_send()
+
+    top, bottom = line_ends(z)
+    interior = 1 - top - bottom
+
+    def head(h):
+        cols = pl.ds(pl.multiple_of(h * HD, HD), HD)
+        query, key, value = query_rows[:, cols], key_rows[:, cols], value_rows[:, cols]
+        mixed = mixed_cot[:, cols]
+        scores = nt(query, key) * inv_root
+        row_top = jnp.max(scores, axis=1, keepdims=True)
+        log_total = row_top + jnp.log(jnp.sum(jnp.exp(scores - row_top), axis=1, keepdims=True))
+        soft = jnp.exp(scores - log_total)
+        value_cot[:, cols] = tn(soft.astype(bf16), mixed).astype(bf16)
+        soft_cot = nt(mixed, value)
+        inner = jnp.sum(soft * soft_cot, axis=1, keepdims=True)
+        score_cot = (soft * (soft_cot - inner) * inv_root).astype(bf16)
+        query_cot[:, cols] = nn(score_cot, key).astype(bf16)
+        key_cot[:, cols] = tn(score_cot, query).astype(bf16)
+
+    term(1, middle_pair, mixed_rows)
+
+    @pl.when(interior == 0)
+    def _():
+        line_step(0, 0)
+        line_step(0, 1)
+
+    @pl.loop(0, head_cols // HD // 2)
+    def _(h):
+        pl.when((h == 1) & (interior == 1))(lambda: line_step(0, 0))
+        head(2 * h)
+        head(2 * h + 1)
+
+    pl.when(interior == 1)(lambda: line_step(0, 1))
+    line_step(0, 2)
+    term(2, normed_pair, value_cot)
+    line_step(0, 3)
+    term(3, normed_pair, query_cot)
+    line_step(1, 0)
+    line_step(1, 1)
+    term(4, normed_pair, key_cot)
+    line_step(1, 2)
+    line_step(1, 3)
+
+    panel = 4
+
+    def first_add(cot, weight, begin):
+        @pl.loop(0, weight.shape[0] // panel)
+        def _(n):
+            part = weight[pl.ds(n * panel, panel)].reshape(panel * half_rows, head_cols)
+            cols = pl.ds(pl.multiple_of(n * panel * half_rows, panel * half_rows), panel * half_rows)
+            value = nt(cot[...], part).reshape(2, half_rows, panel * half_rows)
+            if begin:
+                first_terms[:, :, cols] = value
+            else:
+                first_terms[:, :, cols] = first_terms[:, :, cols] + value
+
+    query_load.wait()
+    first_add(query_cot, weight_two, True)
+    key_load.start()
+    value_load.wait()
+    first_add(value_cot, weight_one, False)
+    key_load.wait()
+    first_add(key_cot, weight_two, False)
+    step = 16
+
+    @pl.loop(0, half_rows // step)
+    def _(i):
+        at = pl.ds(pl.multiple_of(i * step, step), step)
+        first_mine[at, :] = first_terms[1 - x, at, :].astype(bf16)
+
+    first_swap.start()
+    total_block(sums[0], mixture_total)
+    for turn in range(LEVELS):
+        line_step(2, turn)
+    total_block(sums[1], output_total)
+    line_step(3, 0)
+    line_step(3, 1)
+    first_swap.wait_recv()
+    gain = first_gain[...]
+    gains[...] = jnp.concatenate(
+        [jnp.zeros((1, width), f32), second_term[...], jnp.zeros((6, width), f32)], axis=0
+    )
+
+    @pl.loop(0, half_rows // step)
+    def _(i):
+        at = pl.ds(pl.multiple_of(i * step, step), step)
+        value = first_terms[x, at, :] + first_other[at, :].astype(f32)
+        entry, scale = block_input[at, :], first_scale[at, :]
+        weighted = value * gain
+        mean = jnp.mean(weighted * entry, axis=1, keepdims=True)
+        input_grad[at, :] = middle_grad[at, :] + scale * (weighted - entry * (scale * scale * mean))
+        gains[0:1, :] = gains[0:1, :] + jnp.sum(value * entry * scale, axis=0, keepdims=True)
+
+    hops = [
+        (index_of(z, y, 1 - c), x),
+        (own, 1 - x),
+        (index_of(z + 1 - 2 * (z % 2), y, c), x),
+        (index_of((z + 2) % LEVELS, y, c), x),
+        (index_of(z, 1 - y, c), x),
+    ]
+
+    def gain_copy(i):
+        return remote(gains, gains_in.at[i], gain_s.at[i], gain_r.at[i], hops[i])
+
+    def gain_add(i):
+        gain_copy(i).wait()
+        gains[...] = gains[...] + gains_in[i]
+
+    for i in range(2):
+        gain_copy(i).start()
+        gain_add(i)
+    expert_swaps[2].start()
+    gain_copy(2).start()
+    line_step(3, 2)
+    line_step(3, 3)
+    gain_add(2)
+    gain_copy(3).start()
+    total_block(sums[2], value_total)
+    line_step(4, 0)
+    gain_add(3)
+    gain_copy(4).start()
+    for turn in range(1, LEVELS):
+        line_step(4, turn)
+    total_block(sums[3], query_total)
+    gain_add(4)
+    gain_grads[...] = gains[...]
+    total_block(sums[4], key_total)
+
+    @pl.loop(0, pairs)
+    def _(b):
+        core_copy(0, b, mixture_part.at[slot_at(b, 1)]).wait_send()
+
+    for a in range(5):
+        for turn in range(LEVELS):
+            side_copy(a, turn).wait_send()
+        line = sums[a].from_line
+        for turn in range(LEVELS - 1):
+            remote(
+                line.at[0], line.at[turn], sums[a].line_s.at[turn], sums[a].line_r.at[turn], (own, 1 - x)
+            ).wait_send()
+    first_swap.wait_send()
+    for copy in expert_swaps:
+        copy.wait()
+
+
+def run_last(
+    mixture_part, pair_rows_in, attention_rows, weights_full, theirs, norm_args, collective_id
+):
+    f32, bf16 = jnp.float32, jnp.bfloat16
+    shape = jax.ShapeDtypeStruct
+    hbm = pl.BlockSpec(memory_space=pl.ANY)
+    vmem = pl.BlockSpec(memory_space=pltpu.VMEM)
+    dma = pltpu.SemaphoreType.DMA
+    rows, head_cols = attention_rows[0].shape
+    half_rows, width = norm_args[0].shape
+    wide = mixture_part.shape[1:]
+    block = (half_rows, head_cols)
+    pairs = 2 * LEVELS
+    flops = 2 * rows * head_cols * width * 8
+    nbytes = 2 * (mixture_part.size + 12 * weights_full[0].size)
+    outs = pl.pallas_call(
+        last_kernel,
+        out_shape=[shape(block, f32)] * 4
+        + [shape(wide, f32)]
+        + [shape(t.shape, t.dtype) for t in theirs]
+        + [shape((half_rows, width), f32), shape((8, width), f32)],
+        in_specs=[hbm] + [vmem] * 6 + [hbm] * 7 + [vmem] * 5,
+        out_specs=[vmem] * 5 + [hbm] * 3 + [vmem] * 2,
+        scratch_shapes=[
+            pltpu.VMEM((pairs,) + wide, bf16),
+            pltpu.VMEM((LEVELS,) + wide, bf16),
+            pltpu.VMEM((LEVELS + 1,) + wide, bf16),
+            pltpu.VMEM((pairs,) + wide, bf16),
+            pltpu.VMEM((4, pairs) + block, bf16),
+            pltpu.VMEM((4, LEVELS) + block, bf16),
+            pltpu.VMEM((4, LEVELS + 1) + block, bf16),
+            pltpu.VMEM((2, 2) + block, bf16),
+        ]
+        + [pltpu.VMEM((rows, head_cols), bf16)] * 4
+        + [pltpu.VMEM(weights_full[0].shape, bf16)] * 2
+        + [
+            pltpu.VMEM((2, half_rows, width), f32),
+            pltpu.VMEM((half_rows, width), bf16),
+            pltpu.VMEM((half_rows, width), bf16),
+            pltpu.VMEM((8, width), f32),
+            pltpu.VMEM((5, 8, width), f32),
+        ]
+        + [dma((5, pairs))] * 2
+        + [dma((5, LEVELS))] * 2
+        + [dma((5, LEVELS + 1))] * 2
+        + [dma((pairs,)), dma((4,)), dma((4,)), dma((4,)), dma((5,)), dma((5,))],
+        compiler_params=pltpu.CompilerParams(
+            collective_id=collective_id, has_side_effects=True, vmem_limit_bytes=67_043_328
+        ),
+        cost_estimate=pl.CostEstimate(flops=flops, bytes_accessed=nbytes, transcendentals=0),
+        name="last",
+    )(mixture_part, *pair_rows_in, *attention_rows, *weights_full, *theirs, *norm_args)
+    return outs[:5], outs[5:8], outs[8], outs[9]
 
 
 def gate_columns(route_rows, gate_rows, expert_count):
@@ -1341,6 +1510,7 @@
         up_mine,
         up_theirs,
         down_mine,
+        down_theirs,
         down_landed,
     ) = run_experts(
         gates_all,
@@ -1353,49 +1523,12 @@
         other_weights,
         2,
     )
-    middle_rows = middle_pair.reshape(seq_rows, model_width)
-    out_term = contract_rows(middle_rows, mixed_rows)
-    mixed_cot = (
-        jnp.dot(middle_rows, output_full, preferred_element_type=f32)
-        .astype(bf16)
-        .reshape(seq_rows, local_heads, HD)
-    )
-    value_cot = jnp.einsum("hst,shd->thd", soft_rounded, mixed_cot, preferred_element_type=f32)
-    value_cot = value_cot.astype(bf16).reshape(seq_rows, head_cols)
-    soft_cot = jnp.einsum("shd,thd->hst", mixed_cot, value_rows, preferred_element_type=f32)
-    score_cot = (
-        soft_weights
-        * (soft_cot - jnp.sum(soft_weights * soft_cot, axis=2, keepdims=True))
-        * inv_root
-    ).astype(bf16)
-    query_cot = (
-        jnp.einsum("hst,thd->shd", score_cot, key_rows, preferred_element_type=f32)
-        .astype(bf16)
-        .reshape(seq_rows, head_cols)
-    )
-    key_cot = (
-        jnp.einsum("hst,shd->thd", score_cot, query_rows, preferred_element_type=f32)
-        .astype(bf16)
-        .reshape(seq_rows, head_cols)
-    )
-    first_terms = (
-        contract_cols(query_cot, query_full)
-        + contract_cols(key_cot, key_full)
-        + contract_cols(value_cot, value_full)
-    )
-    sums, landed, input_grad, gain_grads = sum_gradients(
-        [
-            term.astype(bf16).reshape((owner_count,) + query_weight.shape)
-            for term in (
-                contract_rows(normed_rows, query_cot),
-                contract_rows(normed_rows, key_cot),
-                contract_rows(normed_rows, value_cot),
-                out_term,
-            )
-        ]
-        + [mixture_part],
-        (gate_theirs, up_theirs),
-        first_terms.astype(bf16).reshape(pair_count, local_rows, model_width),
+    sums, landed, input_grad, gain_grads = run_last(
+        mixture_part,
+        (middle_pair, normed_pair),
+        (mixed_rows,) + tuple(r.reshape(seq_rows, head_cols) for r in (query_rows, key_rows, value_rows)),
+        (gathered[3], gathered[0], gathered[1], gathered[2]),
+        (gate_theirs, up_theirs, down_theirs),
         (block_input, first_scale, first_gain[None], middle_grad, second_term),
         4,
     )
@@ -1405,7 +1538,7 @@
         for mine, theirs in (
             (gate_mine, landed[0]),
             (up_mine, landed[1]),
-            (down_mine.reshape(down_landed.shape), down_landed),
+            (down_mine, jnp.concatenate([down_landed, landed[2]], axis=0)),
         )
     )
     block_output = middle + mixture[:, :model_width]

time: 561 us -> 511 us (0.911); the launches traced: 554 us -> 510 us
  matrix products: 52.7 us -> 12.3 us
    dot_general x9 -> x0, matrix products: 26.5 us -> none  [the longest x4 13.5 us: contract_rows(): lax.dot_general(left_block, right_block, (((0,), (0,)), ((), ())), prefer...]
    dot_general x4 -> x1, matrix products: 16.4 us -> 4.87 us  [contract_cols(): lax.dot_general(left_block, right_block, (((1,), (1,)), ((), ())), prefer...]
    pallas_call x1, Pallas kernels: 161 us -> 155 us  [run_experts(): pl.pallas_call(experts_kernel, out_shape=[shape(block, f32), shape(block,...]
where the time goes in v5:
time: 511 us; the launch traced here: 510 us
  Pallas kernels  465 us (91%)
  other arithmetic  17.4 us (3%)
  local copies, waits for them, and re-layouts  14.8 us (3%)
  matrix products  12.3 us (2%)
    pallas_call x1, Pallas kernels, run_last(): pl.pallas_call(last_kernel, out_shape=[shape(block, f32)] * 4 + [shape(wi...  155 us
    pallas_call x1, Pallas kernels, run_experts(): pl.pallas_call(experts_kernel, out_shape=[shape(block, f32), shape(block,...  155 us
    pallas_call x1, Pallas kernels, gather_weights(): pl.pallas_call(functools.partial(weights_kernel, count), out_shape=[jax.S...  155 us

profile of v5, /device:TPU:0, one launch (start us, length us, event | category | flops | bytes accessed | tf_op | source)
XLA Modules:
  0.0 510.2 jit_solution(9720340714429304322)
XLA Ops:
  0.7 0.8 constant_dynamic-slice_fusion.1
  1.6 0.5 copy-done.20
  2.1 0.7 constant_dynamic-slice_fusion
  2.9 1.0 select_reduce_fusion.refs_5_
  3.9 1.4 multiply_reduce_fusion.1
  5.2 0.5 fusion.10
  5.8 1.6 multiply_convert_fusion.refs_6_
  7.4 0.9 convert_element_type.42.refs_4_
  8.3 154.6 %gather_weights.1 = (bf16[16,128,1024]{2,1,0:T(8,128)(2,1)}, bf16[16,128,1024]{2,1,0:T(8,128)(2,1)}, bf16[16,128,1024]{2,1,0:T(8,128)(2,1)}, bf16[16,128,1024]{2...) custom-call(bf16[128,1024]{1,0:T(8,128)(2,1)} %refs_0_.1, ...), custom_call_target="tpu_custom_call" | custom-call | bytes 104857600 | tf_op jit(solution)/shard_map/gather_weights/pallas_call | solution.py:472
  162.9 3.9 convolution_convert_fusion.2.query_rows
  166.9 1.3 convolution_convert_fusion.1.key_rows
  168.2 0.4 multiply_reduce_fusion
  169.1 1.5 copy-done.3
  170.6 1.3 convolution_convert_fusion.3.value_rows
  172.1 0.6 copy-done.4
  172.7 0.5 convolution_convert_fusion
  173.3 4.9 fusion.7.out_part
  178.2 154.9 %experts.1 = (f32[128,2048]{1,0:T(8,128)}, f32[128,2048]{1,0:T(8,128)}, f32[1,2048]{1,0:T(1,128)}, bf16[2,128,2048]{2,1,0:T(8,128)(2,1)}, bf16[16,128,2176]{2,1,...) custom-call(f32[16,128,128]{2,1,0:T(8,128)} %get-tuple-element.44.ga, ...), custom_call_target="tpu_custom_call" | custom-call | flops 77309411328 | bytes 67108864 | tf_op jit(solution)/shard_map/experts/pallas_call | solution.py:984
  333.2 2.0 copy.47.mixed_rows
  335.2 1.4 copy.43.first_scale
  336.6 155.3 %last.1 = (f32[128,1024]{1,0:T(8,128)}, f32[128,1024]{1,0:T(8,128)}, f32[128,1024]{1,0:T(8,128)}, f32[128,1024]{1,0:T(8,128)}, f32[128,2176]{1,0:T(8,128)}, /*in...) custom-call(bf16[16,128,2176]{2,1,0:T(8,128)(2,1)} %get-tuple-elemen, ...), custom_call_target="tpu_custom_call" | custom-call | flops 8589934592 | bytes 59244544 | tf_op jit(solution)/shard_map/last/pallas_call | solution.py:1386
  491.9 5.2 %add_bitcast_fusion = f32[1,512,2048]{2,1,0:T(8,128)} fusion(bf16[512,2048]{1,0:T(8,128)(2,1)} %get-tuple-element.73, bf16[256,2048]{1,0:T(8,128)(2,1)} %get-tuple-element.75, bf16[256,2048]{1,0:T(8,128)(2,1)} %get-tuple-element.74), kind=kLoop, calls=%fused_computation | loop fusion | flops 6291456 | bytes 8388608 | tf_op jit(solution)/shard_map/broadcast_in_dim | solution.py:1560
  497.1 0.8 copy-done.10
  498.0 4.7 add_bitcast_fusion.1
  502.7 1.1 slice_add_fusion
  503.9 0.6 select_reduce_fusion.1
  504.5 1.5 fusion.11
  506.0 1.0 copy.69
  507.0 0.8 copy.70
  507.8 0.8 copy.71
  508.6 0.8 copy.72
  509.4 0.8 copy.73
  (48 shorter events, 1.1 us)
Async XLA Ops:
  0.6 5.1 %copy-start = (f32[128,2048]{1,0:T(8,128)S(1)}, f32[128,2048]{1,0:T(8,128)}, u32[]{:S(2)}) copy-start(f32[128,2048]{1,0:T(8,128)} %block_input.3) | copy-start | bytes 3145732
  0.7 6.8 %copy-start.14 = (f32[128,2048]{1,0:T(8,128)S(1)}, f32[128,2048]{1,0:T(8,128)}, u32[]{:S(2)}) copy-start(f32[128,2048]{1,0:T(8,128)} %upstream.1) | copy-start | bytes 3145732
  1.5 0.6 copy-start.20
  162.9 3.9 copy-start.2
  162.9 4.0 copy-start.12
  166.8 1.4 copy-start.5
  168.2 0.8 copy-start.6
  168.2 2.4 copy-start.3
  171.9 0.8 copy-start.4
  173.2 5.0 copy-start.1
  491.9 5.2 %copy-start.7 = (bf16[2048,512]{1,0:T(8,128)(2,1)S(1)}, bf16[2048,512]{1,0:T(8,128)(2,1)}, u32[]{:S(2)}) copy-start(bf16[2048,512]{1,0:T(8,128)(2,1)} %get-tuple-element.69) | copy-start | bytes 6291460
  491.9 5.2 %copy-start.8 = (bf16[2048,512]{1,0:T(8,128)(2,1)S(1)}, bf16[2048,512]{1,0:T(8,128)(2,1)}, u32[]{:S(2)}) copy-start(bf16[2048,512]{1,0:T(8,128)(2,1)} %get-tuple-element.71) | copy-start | bytes 6291460
  491.9 5.2 %copy-start.9 = (bf16[2048,512]{1,0:T(8,128)(2,1)S(1)}, bf16[2048,512]{1,0:T(8,128)(2,1)}, u32[]{:S(2)}) copy-start(bf16[2048,512]{1,0:T(8,128)(2,1)} %get-tuple-element.70) | copy-start | bytes 6291460
  491.9 6.0 %copy-start.10 = (bf16[2048,512]{1,0:T(8,128)(2,1)S(1)}, bf16[2048,512]{1,0:T(8,128)(2,1)}, u32[]{:S(2)}) copy-start(bf16[2048,512]{1,0:T(8,128)(2,1)} %get-tuple-element.72) | copy-start | bytes 6291460
  498.0 4.7 copy-start.11
  498.0 4.7 copy-start.13
  502.7 1.2 copy-start.21
  502.7 3.3 copy-start.15
  502.7 4.3 copy-start.19
  503.8 4.0 copy-start.18
  506.0 2.6 copy-start.17
  507.0 2.4 copy-start.16

commit v6 on v5

--- a/solution.py
+++ b/solution.py
@@ -419,77 +419,261 @@
 GATHER_SENDS = 17
 
 
-def weights_kernel(count, *refs):
-    mine, normed, experts = refs[:count], refs[count], refs[count + 1 : count + 4]
-    outs = refs[count + 4 : 2 * count + 8]
-    full, normed_pair, others = outs[:count], outs[count], outs[count + 1 :]
-    send_sems, recv_sems, own_sems, pair_s, pair_r = refs[2 * count + 8 :]
+def attend_kernel(
+    query_mine,
+    key_mine,
+    value_mine,
+    output_mine,
+    block_input,
+    upstream,
+    first_gain,
+    routes,
+    gate_values,
+    gate_own,
+    up_own,
+    down_own,
+    query_full,
+    key_full,
+    value_full,
+    output_full,
+    upstream_all,
+    gates_all,
+    normed_pair,
+    gate_other,
+    up_other,
+    down_other,
+    query_rows,
+    key_rows,
+    value_rows,
+    mixed_rows,
+    out_part,
+    first_scale,
+    weights,
+    normed,
+    upstream_mine,
+    gates_mine,
+    send_sems,
+    recv_sems,
+    wide_s,
+    wide_r,
+    own_sems,
+    keep_sems,
+    pair_s,
+    pair_r,
+):
+    bf16, f32 = jnp.bfloat16, jnp.float32
     z, y, c, x = place()
     own = index_of(z, y, c)
+    half_rows, width = block_input.shape
+    rows, head_cols = mixed_rows.shape
+    inv_root = HD ** (-0.5)
+    step = 16
+
+    mine = (query_mine, key_mine, value_mine, output_mine)
+    kept = [
+        pltpu.make_async_copy(mine[a], weights.at[a, own], own_sems.at[a]) for a in range(4)
+    ]
+    for copy in kept:
+        copy.start()
     plane_greet(pair=True)
     plans = [
-        PlaneGather(mine[a], full[a], send_sems.at[a], recv_sems.at[a]) for a in range(count)
+        PlaneGather(mine[a], weights.at[a], send_sems.at[a], recv_sems.at[a]) for a in range(4)
+    ] + [
+        PlaneGather(ref, full, wide_s.at[i], wide_r.at[i])
+        for i, (ref, full) in enumerate(((upstream_mine, upstream_all), (gates_mine, gates_all)))
     ]
+    first, output, wide = plans[:3], plans[3:4], plans[4:]
+    for plan in first:
+        plan.start()
+
+    def swap(i, src, dst):
+        return remote(src, dst, pair_s.at[i], pair_r.at[i], (own, 1 - x))
+
     swaps = [
-        remote(src, dst, pair_s.at[i], pair_r.at[i], (own, 1 - x))
+        swap(0, normed.at[x], normed.at[x]),
+        swap(1, gate_own, gate_other),
+        swap(2, up_own, up_other),
+        swap(3, down_own, down_other),
+    ]
+    gain = first_gain[...]
+
+    @pl.loop(0, half_rows // step)
+    def _(i):
+        at = pl.ds(pl.multiple_of(i * step, step), step)
+        value = block_input[at, :]
+        scale = lax.rsqrt(jnp.mean(value * value, axis=1, keepdims=True) + epsilon)
+        first_scale[at, :] = scale
+        normed[x, at, :] = (value * scale * gain).astype(bf16)
+
+    for copy in swaps:
+        copy.start()
+
+    @pl.loop(0, half_rows // step)
+    def _(i):
+        at = pl.ds(pl.multiple_of(i * step, step), step)
+        upstream_mine[at, :] = upstream[at, :].astype(bf16)
+
+    here = pl.ds(pl.multiple_of(x * half_rows, half_rows), half_rows)
+    names, values = routes[here, :], gate_values[here, :]
+    lane = lax.broadcasted_iota(jnp.int32, (half_rows, ROUTE_COLS), 1)
+    table = jnp.zeros((half_rows, ROUTE_COLS), f32)
+    for j in range(TOP):
+        table = table + jnp.where(lane == names[:, j : j + 1], values[:, j : j + 1], 0.0)
+    gates_mine[...] = table
+    wide_kept = [
+        pltpu.make_async_copy(upstream_mine, upstream_all.at[own], own_sems.at[4]),
+        pltpu.make_async_copy(gates_mine, gates_all.at[own], own_sems.at[5]),
+    ]
+    for copy in wide_kept:
+        copy.start()
+
+    def line(group, turn):
+        for plan in group:
+            plan.from_line(turn)
+
+    def side(group, turn):
+        for plan in group:
+            plan.from_side(turn)
+
+    def core(group):
+        for plan in group:
+            for turn in range(LEVELS):
+                for which in range(2):
+                    plan.from_core(turn, which)
+
+    line(first, 1)
+    side(first, 0)
+    line(first, 2)
+    side(first, 1)
+    line(first, 3)
+    for plan in output:
+        plan.start()
+    side(first, 2)
+    side(first, 3)
+    line(output, 1)
+    core(first)
+    line(output, 2)
+    for plan in wide:
+        plan.start()
+    swaps[0].wait_recv()
+    for copy in kept:
+        copy.wait()
+    keeps = [
+        pltpu.make_async_copy(src, dst, keep_sems.at[i])
         for i, (src, dst) in enumerate(
-            [(normed, normed_pair.at[x])] + list(zip(experts, others))
+            (
+                (weights.at[0], query_full),
+                (weights.at[1], key_full),
+                (weights.at[2], value_full),
+                (normed, normed_pair),
+                (weights.at[3], output_full),
+            )
         )
     ]
-    kept = [
-        pltpu.make_async_copy(src, dst, own_sems.at[i])
-        for i, (src, dst) in enumerate(
-            [(mine[a], full[a].at[own]) for a in range(count)] + [(normed, normed_pair.at[x])]
-        )
-    ]
-    for plan in plans:
-        plan.start()
-    for copy in swaps + kept:
+    for copy in keeps[:4]:
         copy.start()
-    for step in range(1, LEVELS):
-        for plan in plans:
-            plan.from_line(step)
-        for plan in plans:
-            plan.from_side(step - 1)
-    for plan in plans:
-        plan.from_side(LEVELS - 1)
-    for plan in plans:
-        for step in range(LEVELS):
-            for side in range(2):
-                plan.from_core(step, side)
+
+    def flat(ref):
+        value = ref[...]
+        return value.reshape(value.shape[0] * value.shape[1], value.shape[2])
+
+    for a, ref in enumerate((query_rows, key_rows, value_rows)):
+        ref[...] = nn(flat(normed), flat(weights.at[a])).astype(bf16)
+        if a == 0:
+            line(output, 3)
+            side(output, 0)
+    side(output, 1)
+    line(wide, 1)
+
+    def head(h):
+        cols = pl.ds(pl.multiple_of(h * HD, HD), HD)
+        scores = nt(query_rows[:, cols], key_rows[:, cols]) * inv_root
+        row_top = jnp.max(scores, axis=1, keepdims=True)
+        log_total = row_top + jnp.log(jnp.sum(jnp.exp(scores - row_top), axis=1, keepdims=True))
+        soft = jnp.exp(scores - log_total)
+        mixed_rows[:, cols] = nn(soft.astype(bf16), value_rows[:, cols]).astype(bf16)
+
+    @pl.loop(0, head_cols // HD // 2)
+    def _(h):
+        head(2 * h)
+        head(2 * h + 1)
+
+    side(output, 2)
+    side(output, 3)
+    line(wide, 2)
+    core(output)
+    keeps[4].start()
+    panel = 4
+
+    @pl.loop(0, weights.shape[1] // panel)
+    def _(n):
+        part = weights[3, pl.ds(n * panel, panel)].reshape(panel * half_rows, head_cols)
+        cols = pl.ds(pl.multiple_of(n * panel * half_rows, panel * half_rows), panel * half_rows)
+        out_part[:, :, cols] = nt(mixed_rows[...], part).reshape(2, half_rows, panel * half_rows)
+
+    side(wide, 0)
+    line(wide, 3)
+    for turn in range(1, LEVELS):
+        side(wide, turn)
+    core(wide)
     for plan in plans:
         plan.finish()
-    for copy in swaps + kept:
+    for copy in wide_kept + keeps:
         copy.wait()
-
-
-def gather_weights(arrays, normed, experts, collective_id):
+    swaps[0].wait_send()
+    for copy in swaps[1:]:
+        copy.wait()
+
+
+def run_attend(shards, block_input, upstream, first_gain, routes, gate_values, experts, collective_id):
+    bf16, f32 = jnp.bfloat16, jnp.float32
     owner_count = lax.axis_size("fsdp")
-    count = len(arrays)
+    half_rows, width = block_input.shape
+    head_cols = shards[0].shape[1]
+    rows = 2 * half_rows
+    shape = jax.ShapeDtypeStruct
     hbm = pl.BlockSpec(memory_space=pl.ANY)
     vmem = pl.BlockSpec(memory_space=pltpu.VMEM)
-    nbytes = sum(a.size * a.dtype.itemsize for a in arrays)
+    dma = pltpu.SemaphoreType.DMA
+    full = (owner_count,) + shards[0].shape
     outs = pl.pallas_call(
-        functools.partial(weights_kernel, count),
-        out_shape=[jax.ShapeDtypeStruct((owner_count,) + a.shape, a.dtype) for a in arrays]
-        + [jax.ShapeDtypeStruct((2,) + normed.shape, normed.dtype)]
-        + [jax.ShapeDtypeStruct(w.shape, w.dtype) for w in experts],
-        in_specs=[vmem] * (count + 1) + [hbm] * 3,
-        out_specs=[hbm] * (count + 4),
+        attend_kernel,
+        out_shape=[shape(full, bf16)] * 4
+        + [
+            shape((owner_count, half_rows, width), bf16),
+            shape((owner_count, half_rows, ROUTE_COLS), f32),
+            shape((2, half_rows, width), bf16),
+        ]
+        + [shape(w.shape, w.dtype) for w in experts]
+        + [shape((rows, head_cols), bf16)] * 4
+        + [shape((2, half_rows, width), f32), shape((half_rows, 1), f32)],
+        in_specs=[vmem] * 9 + [hbm] * 3,
+        out_specs=[hbm] * 10 + [vmem] * 6,
         scratch_shapes=[
-            pltpu.SemaphoreType.DMA((count, GATHER_SENDS)),
-            pltpu.SemaphoreType.DMA((count, owner_count)),
-            pltpu.SemaphoreType.DMA((count + 1,)),
-            pltpu.SemaphoreType.DMA((4,)),
-            pltpu.SemaphoreType.DMA((4,)),
+            pltpu.VMEM((4,) + full, bf16),
+            pltpu.VMEM((2, half_rows, width), bf16),
+            pltpu.VMEM((half_rows, width), bf16),
+            pltpu.VMEM((half_rows, ROUTE_COLS), f32),
+            dma((4, GATHER_SENDS)),
+            dma((4, owner_count)),
+            dma((2, GATHER_SENDS)),
+            dma((2, owner_count)),
+            dma((6,)),
+            dma((5,)),
+            dma((4,)),
+            dma((4,)),
         ],
-        compiler_params=pltpu.CompilerParams(collective_id=collective_id, has_side_effects=True),
+        compiler_params=pltpu.CompilerParams(
+            collective_id=collective_id, has_side_effects=True, vmem_limit_bytes=60 * 2**20
+        ),
         cost_estimate=pl.CostEstimate(
-            flops=0, bytes_accessed=owner_count * nbytes * 4, transcendentals=0
+            flops=2 * 4 * rows * head_cols * width,
+            bytes_accessed=16 * shards[0].size * owner_count,
+            transcendentals=0,
         ),
-        name="gather_weights",
-    )(*arrays, normed, *experts)
-    return outs[:count], outs[count], outs[count + 1 :]
+        name="attend",
+    )(*shards, block_input, upstream, first_gain, routes, gate_values, *experts)
+    return outs[:4], outs[4:7], outs[7:10], outs[10:14], outs[14], outs[15]
 
 
 class PlaneSums:
@@ -606,7 +790,6 @@
     middle,
     middle_grad,
     second_term,
-    middle_pair,
     mixture_hbm,
     gate_mine,
     gate_theirs,
@@ -856,17 +1039,7 @@
             mean = jnp.mean(weighted * mid, axis=1, keepdims=True)
             value = wide[at, :] + scale * (weighted - mid * (scale * scale * mean))
             middle_grad[at, :] = value
-            tmp[0, 0, at, :] = value.astype(bf16)
             second_term[...] = second_term[...] + jnp.sum(cot * mid * scale, axis=0, keepdims=True)
-
-        pair_send().start()
-        pair_keep().start()
-
-    def pair_send():
-        return remote(tmp.at[0, 0], middle_pair.at[x], pair_s.at[1], pair_r.at[1], partner)
-
-    def pair_keep():
-        return pltpu.make_async_copy(tmp.at[0, 0], middle_pair.at[x], load_sems.at[0])
 
     @pl.loop(0, pairs)
     def _(b):
@@ -897,7 +1070,7 @@
     )
     route_out.start()
     down_send = remote(
-        wd.at[0, pl.ds(0, block)], down_landed, pair_s.at[2], pair_r.at[2], partner
+        wd.at[0, pl.ds(0, block)], down_landed, pair_s.at[1], pair_r.at[1], partner
     )
     down_later = pltpu.make_async_copy(wd.at[0, pl.ds(block, block)], down_theirs, load_sems.at[3])
     down_keep = pltpu.make_async_copy(wd.at[1], down_mine, load_sems.at[4])
@@ -949,8 +1122,6 @@
 
     for p in (width // block - 2, width // block - 1):
         wait_outs(p)
-    pair_send().wait()
-    pair_keep().wait()
     route_out.wait()
     down_send.wait()
     down_later.wait()
@@ -987,14 +1158,13 @@
             shape(block, f32),
             shape(block, f32),
             shape((1, width), f32),
-            shape((2,) + block, bf16),
             shape((owner_count, half_rows, width + ROUTE_COLS), bf16),
         ]
         + [shape((width, units), bf16)] * 4
         + [shape((units, width), bf16)]
         + [shape((256, width), bf16)] * 2,
         in_specs=[vmem, vmem] + [hbm] * 10,
-        out_specs=[vmem] * 3 + [hbm] * 9,
+        out_specs=[vmem] * 3 + [hbm] * 8,
         scratch_shapes=[
             pltpu.VMEM((owner_count,) + block, bf16),
             pltpu.VMEM((owner_count,) + block, bf16),
@@ -1023,8 +1193,8 @@
             dma((LEVELS + 1,)),
             dma((10,)),
             dma((8,)),
-            dma((3,)),
-            dma((3,)),
+            dma((2,)),
+            dma((2,)),
         ],
         compiler_params=pltpu.CompilerParams(
             collective_id=collective_id, has_side_effects=True, vmem_limit_bytes=67_043_328
@@ -1038,7 +1208,6 @@
 
 def last_kernel(
     mixture_part,
-    middle_pair,
     normed_pair,
     mixed_rows,
     query_rows,
@@ -1074,6 +1243,7 @@
     from_side,
     from_line,
     tmp,
+    middle_pair,
     mixed_cot,
     query_cot,
     key_cot,
@@ -1169,6 +1339,13 @@
         if turn < LEVELS - 1:
             plan.to_line(turn)
 
+    @pl.loop(0, half_rows // 16)
+    def _(i):
+        at = pl.ds(pl.multiple_of(i * 16, 16), 16)
+        middle_pair[x, at, :] = middle_grad[at, :].astype(bf16)
+
+    middle_swap = swap(4, middle_pair.at[x], middle_pair.at[x])
+    middle_swap.start()
     for copy in expert_swaps[:2]:
         copy.start()
     output_load.start()
@@ -1196,6 +1373,7 @@
         return value.reshape(value.shape[0] * value.shape[1], value.shape[2])
 
     output_load.wait()
+    middle_swap.wait()
     mixed_cot[...] = nn(flat(middle_pair), flat(weight_one)).astype(bf16)
     value_load.start()
 
@@ -1369,7 +1547,7 @@
 
 
 def run_last(
-    mixture_part, pair_rows_in, attention_rows, weights_full, theirs, norm_args, collective_id
+    mixture_part, normed_pair, attention_rows, weights_full, theirs, norm_args, collective_id
 ):
     f32, bf16 = jnp.float32, jnp.bfloat16
     shape = jax.ShapeDtypeStruct
@@ -1389,7 +1567,7 @@
         + [shape(wide, f32)]
         + [shape(t.shape, t.dtype) for t in theirs]
         + [shape((half_rows, width), f32), shape((8, width), f32)],
-        in_specs=[hbm] + [vmem] * 6 + [hbm] * 7 + [vmem] * 5,
+        in_specs=[hbm] + [vmem] * 5 + [hbm] * 7 + [vmem] * 5,
         out_specs=[vmem] * 5 + [hbm] * 3 + [vmem] * 2,
         scratch_shapes=[
             pltpu.VMEM((pairs,) + wide, bf16),
@@ -1400,6 +1578,7 @@
             pltpu.VMEM((4, LEVELS) + block, bf16),
             pltpu.VMEM((4, LEVELS + 1) + block, bf16),
             pltpu.VMEM((2, 2) + block, bf16),
+            pltpu.VMEM((2, half_rows, width), bf16),
         ]
         + [pltpu.VMEM((rows, head_cols), bf16)] * 4
         + [pltpu.VMEM(weights_full[0].shape, bf16)] * 2
@@ -1413,13 +1592,13 @@
         + [dma((5, pairs))] * 2
         + [dma((5, LEVELS))] * 2
         + [dma((5, LEVELS + 1))] * 2
-        + [dma((pairs,)), dma((4,)), dma((4,)), dma((4,)), dma((5,)), dma((5,))],
+        + [dma((pairs,)), dma((4,)), dma((5,)), dma((5,)), dma((5,)), dma((5,))],
         compiler_params=pltpu.CompilerParams(
             collective_id=collective_id, has_side_effects=True, vmem_limit_bytes=67_043_328
         ),
         cost_estimate=pl.CostEstimate(flops=flops, bytes_accessed=nbytes, transcendentals=0),
         name="last",
-    )(mixture_part, *pair_rows_in, *attention_rows, *weights_full, *theirs, *norm_args)
+    )(mixture_part, normed_pair, *attention_rows, *weights_full, *theirs, *norm_args)
     return outs[:5], outs[5:8], outs[8], outs[9]
 
 
@@ -1448,62 +1627,29 @@
     routes,
     gate_values,
 ):
-    pair_count = lax.axis_size("tp")
-    owner_count = lax.axis_size("fsdp")
-    local_rows = block_input.shape[0]
-    seq_rows = local_rows * pair_count
-    model_width = block_input.shape[1]
-    head_cols = query_weight.shape[1]
-    local_heads = head_cols // HD
-    expert_count = EXP_DEV * owner_count
-    inv_root = HD ** (-0.5)
-    bf16, f32 = jnp.bfloat16, jnp.float32
-
-    my_routes, my_gates = half_of(routes), half_of(gate_values)
-    gate_table = gate_columns(my_routes, my_gates, ROUTE_COLS)
+    local_rows, model_width = block_input.shape
+    expert_count = EXP_DEV * lax.axis_size("fsdp")
+    f32 = jnp.float32
+    my_routes = half_of(routes)
     expert_names = jnp.arange(expert_count, dtype=jnp.int32)[None, :]
     own_weights = (gate_weight[0], up_weight[0], down_weight[0])
-
-    first_scale = lax.rsqrt(jnp.mean(block_input * block_input, axis=1, keepdims=True) + epsilon)
-    first_normed = (block_input * first_scale * first_gain).astype(bf16)
-    gathered, normed_pair, other_weights = gather_weights(
-        [
-            query_weight,
-            key_weight,
-            value_weight,
-            output_weight,
-            upstream_grad.astype(bf16),
-            gate_table,
-        ],
-        first_normed,
+    weights_full, gathered, other_weights, attention_rows, out_part, first_scale = run_attend(
+        (query_weight, key_weight, value_weight, output_weight),
+        block_input,
+        upstream_grad,
+        first_gain[None],
+        routes,
+        gate_values,
         own_weights,
         1,
     )
-    query_full, key_full, value_full, output_full = (w.reshape(-1, head_cols) for w in gathered[:4])
-    upstream_all, gates_all = gathered[4:]
-    normed_rows = normed_pair.reshape(seq_rows, model_width)
-
-    def heads_of(weight_full):
-        return (
-            jnp.dot(normed_rows, weight_full, preferred_element_type=f32)
-            .astype(bf16)
-            .reshape(seq_rows, local_heads, HD)
-        )
-
-    query_rows, key_rows, value_rows = heads_of(query_full), heads_of(key_full), heads_of(value_full)
-    scores = jnp.einsum("shd,thd->hst", query_rows, key_rows, preferred_element_type=f32) * inv_root
-    row_top = jnp.max(scores, axis=2, keepdims=True)
-    log_total = row_top + jnp.log(jnp.sum(jnp.exp(scores - row_top), axis=2, keepdims=True))
-    soft_weights = jnp.exp(scores - log_total)
-    soft_rounded = soft_weights.astype(bf16)
-    mixed_rows = jnp.einsum("hst,thd->shd", soft_rounded, value_rows, preferred_element_type=f32)
-    mixed_rows = mixed_rows.astype(bf16).reshape(seq_rows, head_cols)
-    out_part = contract_cols(mixed_rows, output_full).reshape(pair_count, local_rows, model_width)
+    query_full, key_full, value_full, output_full = weights_full
+    query_rows, key_rows, value_rows, mixed_rows = attention_rows
+    upstream_all, gates_all, normed_pair = gathered
     (
         middle,
         middle_grad,
         second_term,
-        middle_pair,
         mixture_part,
         gate_mine,
         gate_theirs,
@@ -1525,9 +1671,9 @@
     )
     sums, landed, input_grad, gain_grads = run_last(
         mixture_part,
-        (middle_pair, normed_pair),
-        (mixed_rows,) + tuple(r.reshape(seq_rows, head_cols) for r in (query_rows, key_rows, value_rows)),
-        (gathered[3], gathered[0], gathered[1], gathered[2]),
+        normed_pair,
+        (mixed_rows, query_rows, key_rows, value_rows),
+        (output_full, query_full, key_full, value_full),
         (gate_theirs, up_theirs, down_theirs),
         (block_input, first_scale, first_gain[None], middle_grad, second_term),
         4,

time: 511 us -> 488 us (0.955)
  matrix products: 12.3 us -> 0 us
  other arithmetic: 17.4 us -> 11.6 us
  local copies, waits for them, and re-layouts: 14.8 us -> 9.57 us
    dot_general x6 -> x0, matrix products: 12.3 us -> none  [the longest x3 6.44 us: heads_of(): jnp.dot(normed_rows, weight_full, preferred_element_type=f32).astype(bf16)]
    pallas_call x1, Pallas kernels: 155 us -> 148 us  [run_experts(): pl.pallas_call(experts_kernel, out_shape=[shape(block, f32), shape(block,...]
where the time goes in v6:
time: 488 us; the launch traced here: 487 us
  Pallas kernels  466 us (95%)
  other arithmetic  11.6 us (2%)
  local copies, waits for them, and re-layouts  9.57 us (2%)
    pallas_call x1, Pallas kernels, run_last(): pl.pallas_call(last_kernel, out_shape=[shape(block, f32)] * 4 + [shape(wi...  160 us
    pallas_call x1, Pallas kernels, run_attend(): pl.pallas_call(attend_kernel, out_shape=[shape(full, bf16)] * 4 + [shape(...  158 us
    pallas_call x1, Pallas kernels, run_experts(): pl.pallas_call(experts_kernel, out_shape=[shape(block, f32), shape(block,...  148 us

profile of v6, /device:TPU:0, one launch (start us, length us, event | category | flops | bytes accessed | tf_op | source)
XLA Modules:
  0.0 487.5 jit_solution(18232696216440474341)
XLA Ops:
  0.6 1.5 copy.28.routes
  2.1 1.5 copy.29.gate_values
  3.6 158.0 %attend.1 = (bf16[16,128,1024]{2,1,0:T(8,128)(2,1)}, bf16[16,128,1024]{2,1,0:T(8,128)(2,1)}, bf16[16,128,1024]{2,1,0:T(8,128)(2,1)}, bf16[16,128,1024]{2,1,0:T(8...) custom-call(bf16[128,1024]{1,0:T(8,128)(2,1)} %query_mine.1, ...), custom_call_target="tpu_custom_call" | custom-call | flops 4294967296 | bytes 33554432 | tf_op jit(solution)/shard_map/attend/pallas_call | solution.py:639
  161.6 147.8 %experts.1 = (f32[128,2048]{1,0:T(8,128)}, f32[128,2048]{1,0:T(8,128)}, f32[1,2048]{1,0:T(1,128)}, bf16[16,128,2176]{2,1,0:T(8,128)(2,1)}, bf16[2048,512]{1,0:T(...) custom-call(f32[16,128,128]{2,1,0:T(8,128)} %get-tuple-element.49.ga, ...), custom_call_target="tpu_custom_call" | custom-call | flops 77309411328 | bytes 67108864 | tf_op jit(solution)/shard_map/experts/pallas_call | solution.py:1155
  309.4 159.7 %last.1 = (f32[128,1024]{1,0:T(8,128)}, f32[128,1024]{1,0:T(8,128)}, f32[128,1024]{1,0:T(8,128)}, f32[128,1024]{1,0:T(8,128)}, f32[128,2176]{1,0:T(8,128)}, /*in...) custom-call(bf16[16,128,2176]{2,1,0:T(8,128)(2,1)} %get-tuple-elemen, ...), custom_call_target="tpu_custom_call" | custom-call | flops 8589934592 | bytes 59244544 | tf_op jit(solution)/shard_map/last/pallas_call | solution.py:1564
  469.2 0.0 copy-start
  469.2 0.0 copy-start.1
  469.2 0.0 copy-start.2
  469.2 0.0 copy-start.3
  469.2 5.2 %add_bitcast_fusion = f32[1,512,2048]{2,1,0:T(8,128)} fusion(bf16[512,2048]{1,0:T(8,128)(2,1)} %get-tuple-element.83, bf16[256,2048]{1,0:T(8,128)(2,1)} %get-tuple-element.85, bf16[256,2048]{1,0:T(8,128)(2,1)} %get-tuple-element.84), kind=kLoop, calls=%fused_computation | loop fusion | flops 6291456 | bytes 8388608 | tf_op jit(solution)/shard_map/broadcast_in_dim | solution.py:1706
  474.4 0.0 copy-done
  474.4 0.0 copy-done.1
  474.4 0.0 copy-done.2
  474.4 0.8 copy-done.3
  475.2 4.7 add_bitcast_fusion.1
  480.0 0.0 copy-done.4
  480.0 0.0 copy-done.5
  480.0 0.0 copy-start.10
  480.0 1.1 slice_add_fusion
  481.1 0.1 copy.30
  481.1 0.0 copy-done.11
  481.1 0.6 select_reduce_fusion
  481.8 1.5 fusion
  483.3 0.0 copy-done.6
  483.3 1.0 copy.36
  484.3 0.0 copy-done.10
  484.3 0.8 copy.37
  485.1 0.0 copy-done.9
  485.1 0.8 copy.38
  485.9 0.0 copy-done.8
  485.9 0.8 copy.39
  486.7 0.8 copy.40
  (10 shorter events, 0.0 us)
Async XLA Ops:
  469.2 5.2 %copy-start = (bf16[2048,512]{1,0:T(8,128)(2,1)S(1)}, bf16[2048,512]{1,0:T(8,128)(2,1)}, u32[]{:S(2)}) copy-start(bf16[2048,512]{1,0:T(8,128)(2,1)} %get-tuple-element.79) | copy-start | bytes 6291460
  469.2 5.2 %copy-start.1 = (bf16[2048,512]{1,0:T(8,128)(2,1)S(1)}, bf16[2048,512]{1,0:T(8,128)(2,1)}, u32[]{:S(2)}) copy-start(bf16[2048,512]{1,0:T(8,128)(2,1)} %get-tuple-element.81) | copy-start | bytes 6291460
  469.2 5.2 %copy-start.2 = (bf16[2048,512]{1,0:T(8,128)(2,1)S(1)}, bf16[2048,512]{1,0:T(8,128)(2,1)}, u32[]{:S(2)}) copy-start(bf16[2048,512]{1,0:T(8,128)(2,1)} %get-tuple-element.80) | copy-start | bytes 6291460
  469.2 6.0 %copy-start.3 = (bf16[2048,512]{1,0:T(8,128)(2,1)S(1)}, bf16[2048,512]{1,0:T(8,128)(2,1)}, u32[]{:S(2)}) copy-start(bf16[2048,512]{1,0:T(8,128)(2,1)} %get-tuple-element.82) | copy-start | bytes 6291460
  475.2 4.7 copy-start.4
  475.2 4.7 copy-start.5
  480.0 1.2 copy-start.11
  480.0 3.3 copy-start.6
  480.0 4.3 copy-start.10
  481.1 4.0 copy-start.9
  483.3 2.6 copy-start.8
  484.3 2.4 copy-start.7

commit v7 on v6

--- a/solution.py
+++ b/solution.py
@@ -514,8 +514,9 @@
         upstream_mine[at, :] = upstream[at, :].astype(bf16)
 
     here = pl.ds(pl.multiple_of(x * half_rows, half_rows), half_rows)
-    names, values = routes[here, :], gate_values[here, :]
-    lane = lax.broadcasted_iota(jnp.int32, (half_rows, ROUTE_COLS), 1)
+    names = jnp.transpose(routes[:, here].astype(f32))
+    values = jnp.transpose(gate_values[:, here])
+    lane = lax.broadcasted_iota(jnp.int32, (half_rows, ROUTE_COLS), 1).astype(f32)
     table = jnp.zeros((half_rows, ROUTE_COLS), f32)
     for j in range(TOP):
         table = table + jnp.where(lane == names[:, j : j + 1], values[:, j : j + 1], 0.0)
@@ -1114,9 +1115,10 @@
         cols = pl.ds(pl.multiple_of(p * block, block), block)
         xp = rows_all[:, :, cols]
         xp = xp.reshape(xp.shape[0] * xp.shape[1], block)
+        xt = jnp.transpose(xp)
         for which, ref in enumerate((gcot, ucot)):
             for k, h in enumerate((x, 1 - x)):
-                gstage[p % 2, which, k] = tn(xp, ref[h]).astype(bf16)
+                gstage[p % 2, which, k] = nn(xt, ref[h]).astype(bf16)
         for copy in part_outs(p):
             copy.start()
 
@@ -1602,11 +1604,6 @@
     return outs[:5], outs[5:8], outs[8], outs[9]
 
 
-def gate_columns(route_rows, gate_rows, expert_count):
-    names = jnp.arange(expert_count, dtype=jnp.int32)[None, None, :]
-    return jnp.sum(jnp.where(route_rows[:, :, None] == names, gate_rows[:, :, None], 0.0), axis=1)
-
-
 def half_of(rows):
     count = rows.shape[0] // lax.axis_size("tp")
     return lax.dynamic_slice_in_dim(rows, lax.axis_index("tp") * count, count, axis=0)
@@ -1638,8 +1635,8 @@
         block_input,
         upstream_grad,
         first_gain[None],
-        routes,
-        gate_values,
+        routes.T,
+        gate_values.T,
         own_weights,
         1,
     )

time: 488 us -> 485 us (level)
  no operation moved by 1% of the time
where the time goes in v7:
time: 485 us
  Pallas kernels  466 us (96%)
  other arithmetic  11.6 us (2%)
  local copies, waits for them, and re-layouts  6.59 us (1%)
    pallas_call x1, Pallas kernels, run_last(): pl.pallas_call(last_kernel, out_shape=[shape(block, f32)] * 4 + [shape(wi...  160 us
    pallas_call x1, Pallas kernels, run_attend(): pl.pallas_call(attend_kernel, out_shape=[shape(full, bf16)] * 4 + [shape(...  158 us
    pallas_call x1, Pallas kernels, run_experts(): pl.pallas_call(experts_kernel, out_shape=[shape(block, f32), shape(block,...  148 us

profile of v7, /device:TPU:0, one launch (start us, length us, event | category | flops | bytes accessed | tf_op | source)
XLA Modules:
  0.0 484.5 jit_solution(13325980704473745762)
XLA Ops:
  0.6 158.0 %attend.1 = (bf16[16,128,1024]{2,1,0:T(8,128)(2,1)}, bf16[16,128,1024]{2,1,0:T(8,128)(2,1)}, bf16[16,128,1024]{2,1,0:T(8,128)(2,1)}, bf16[16,128,1024]{2,1,0:T(8...) custom-call(bf16[128,1024]{1,0:T(8,128)(2,1)} %query_mine.1, ...), custom_call_target="tpu_custom_call" | custom-call | flops 4294967296 | bytes 33554432 | tf_op jit(solution)/shard_map/attend/pallas_call | solution.py:640
  158.7 147.8 %experts.1 = (f32[128,2048]{1,0:T(8,128)}, f32[128,2048]{1,0:T(8,128)}, f32[1,2048]{1,0:T(1,128)}, bf16[16,128,2176]{2,1,0:T(8,128)(2,1)}, bf16[2048,512]{1,0:T(...) custom-call(f32[16,128,128]{2,1,0:T(8,128)} %get-tuple-element.49.ga, ...), custom_call_target="tpu_custom_call" | custom-call | flops 77309411328 | bytes 67108864 | tf_op jit(solution)/shard_map/experts/pallas_call | solution.py:1157
  306.5 159.7 %last.1 = (f32[128,1024]{1,0:T(8,128)}, f32[128,1024]{1,0:T(8,128)}, f32[128,1024]{1,0:T(8,128)}, f32[128,1024]{1,0:T(8,128)}, f32[128,2176]{1,0:T(8,128)}, /*in...) custom-call(bf16[16,128,2176]{2,1,0:T(8,128)(2,1)} %get-tuple-elemen, ...), custom_call_target="tpu_custom_call" | custom-call | flops 8589934592 | bytes 59244544 | tf_op jit(solution)/shard_map/last/pallas_call | solution.py:1566
  466.2 0.0 copy-start
  466.2 0.0 copy-start.1
  466.2 0.0 copy-start.2
  466.2 0.0 copy-start.3
  466.3 5.2 %add_bitcast_fusion = f32[1,512,2048]{2,1,0:T(8,128)} fusion(bf16[512,2048]{1,0:T(8,128)(2,1)} %get-tuple-element.83, bf16[256,2048]{1,0:T(8,128)(2,1)} %get-tuple-element.85, bf16[256,2048]{1,0:T(8,128)(2,1)} %get-tuple-element.84), kind=kLoop, calls=%fused_computation | loop fusion | flops 6291456 | bytes 8388608 | tf_op jit(solution)/shard_map/broadcast_in_dim | solution.py:1703
  471.4 0.0 copy-done
  471.4 0.0 copy-done.1
  471.5 0.0 copy-done.2
  471.5 0.8 copy-done.3
  472.3 0.0 copy-start.4
  472.3 4.7 add_bitcast_fusion.1
  477.0 0.0 copy-done.4
  477.0 0.0 copy-done.5
  477.0 0.0 copy-start.10
  477.0 1.1 slice_add_fusion
  478.1 0.1 copy.26
  478.2 0.0 copy-done.11
  478.2 0.6 select_reduce_fusion
  478.8 1.5 fusion
  480.3 0.0 copy-done.6
  480.3 1.0 copy.32
  481.3 0.0 copy-done.10
  481.3 0.8 copy.33
  482.1 0.0 copy-done.9
  482.1 0.8 copy.34
  482.9 0.0 copy-done.8
  482.9 0.8 copy.35
  483.7 0.0 copy-done.7
  483.7 0.8 copy.36
  (8 shorter events, 0.0 us)
Async XLA Ops:
  466.2 5.2 %copy-start = (bf16[2048,512]{1,0:T(8,128)(2,1)S(1)}, bf16[2048,512]{1,0:T(8,128)(2,1)}, u32[]{:S(2)}) copy-start(bf16[2048,512]{1,0:T(8,128)(2,1)} %get-tuple-element.79) | copy-start | bytes 6291460
  466.2 5.2 %copy-start.1 = (bf16[2048,512]{1,0:T(8,128)(2,1)S(1)}, bf16[2048,512]{1,0:T(8,128)(2,1)}, u32[]{:S(2)}) copy-start(bf16[2048,512]{1,0:T(8,128)(2,1)} %get-tuple-element.81) | copy-start | bytes 6291460
  466.2 5.2 %copy-start.2 = (bf16[2048,512]{1,0:T(8,128)(2,1)S(1)}, bf16[2048,512]{1,0:T(8,128)(2,1)}, u32[]{:S(2)}) copy-start(bf16[2048,512]{1,0:T(8,128)(2,1)} %get-tuple-element.80) | copy-start | bytes 6291460
  466.2 6.0 %copy-start.3 = (bf16[2048,512]{1,0:T(8,128)(2,1)S(1)}, bf16[2048,512]{1,0:T(8,128)(2,1)}, u32[]{:S(2)}) copy-start(bf16[2048,512]{1,0:T(8,128)(2,1)} %get-tuple-element.82) | copy-start | bytes 6291460
  472.3 4.7 copy-start.4
  472.3 4.7 copy-start.5
  477.0 1.2 copy-start.11
  477.0 3.3 copy-start.6
  477.0 4.3 copy-start.10
  478.1 4.0 copy-start.9
  480.3 2.6 copy-start.8
  481.3 2.4 copy-start.7

commit v8 on v7

--- a/solution.py
+++ b/solution.py
@@ -1341,6 +1341,16 @@
         if turn < LEVELS - 1:
             plan.to_line(turn)
 
+    def wide_load(b):
+        return pltpu.make_async_copy(
+            mixture_part.at[slot_at(b, 0)], wide_own.at[b], own_sems.at[b]
+        )
+
+    @pl.loop(0, pairs)
+    def _(b):
+        core_copy(0, b, mixture_part.at[slot_at(b, 1)]).start()
+        wide_load(b).start()
+
     @pl.loop(0, half_rows // 16)
     def _(i):
         at = pl.ds(pl.multiple_of(i * 16, 16), 16)
@@ -1350,18 +1360,6 @@
     middle_swap.start()
     for copy in expert_swaps[:2]:
         copy.start()
-    output_load.start()
-    query_load.start()
-
-    def wide_load(b):
-        return pltpu.make_async_copy(
-            mixture_part.at[slot_at(b, 0)], wide_own.at[b], own_sems.at[b]
-        )
-
-    @pl.loop(0, pairs)
-    def _(b):
-        core_copy(0, b, mixture_part.at[slot_at(b, 1)]).start()
-        wide_load(b).start()
 
     @pl.loop(0, pairs)
     def _(b):
@@ -1369,6 +1367,11 @@
         core_copy(0, b, mixture_part.at[slot_at(b, 1)]).wait_recv()
         add_block(wide_own.at[b], wide_core.at[b], wide_core.at[b])
         pl.when(b < LEVELS)(lambda: side_copy(0, b).start())
+
+        @pl.when(b == 0)
+        def _():
+            output_load.start()
+            query_load.start()
 
     def flat(ref):
         value = ref[...]

time: 485 us -> 482 us (level)
  no operation moved by 1% of the time
where the time goes in v8:
time: 482 us
  Pallas kernels  463 us (96%)
  other arithmetic  11.6 us (2%)
  local copies, waits for them, and re-layouts  6.59 us (1%)
    pallas_call x1, Pallas kernels, run_attend(): pl.pallas_call(attend_kernel, out_shape=[shape(full, bf16)] * 4 + [shape(...  158 us
    pallas_call x1, Pallas kernels, run_last(): pl.pallas_call(last_kernel, out_shape=[shape(block, f32)] * 4 + [shape(wi...  157 us
    pallas_call x1, Pallas kernels, run_experts(): pl.pallas_call(experts_kernel, out_shape=[shape(block, f32), shape(block,...  148 us

profile of v8, /device:TPU:0, one launch (start us, length us, event | category | flops | bytes accessed | tf_op | source)
XLA Modules:
  0.0 481.8 jit_solution(11694490440164029837)
XLA Ops:
  0.6 158.0 %attend.1 = (bf16[16,128,1024]{2,1,0:T(8,128)(2,1)}, bf16[16,128,1024]{2,1,0:T(8,128)(2,1)}, bf16[16,128,1024]{2,1,0:T(8,128)(2,1)}, bf16[16,128,1024]{2,1,0:T(8...) custom-call(bf16[128,1024]{1,0:T(8,128)(2,1)} %query_mine.1, ...), custom_call_target="tpu_custom_call" | custom-call | flops 4294967296 | bytes 33554432 | tf_op jit(solution)/shard_map/attend/pallas_call | solution.py:640
  158.7 147.8 %experts.1 = (f32[128,2048]{1,0:T(8,128)}, f32[128,2048]{1,0:T(8,128)}, f32[1,2048]{1,0:T(1,128)}, bf16[16,128,2176]{2,1,0:T(8,128)(2,1)}, bf16[2048,512]{1,0:T(...) custom-call(f32[16,128,128]{2,1,0:T(8,128)} %get-tuple-element.49.ga, ...), custom_call_target="tpu_custom_call" | custom-call | flops 77309411328 | bytes 67108864 | tf_op jit(solution)/shard_map/experts/pallas_call | solution.py:1157
  306.5 157.1 %last.1 = (f32[128,1024]{1,0:T(8,128)}, f32[128,1024]{1,0:T(8,128)}, f32[128,1024]{1,0:T(8,128)}, f32[128,1024]{1,0:T(8,128)}, f32[128,2176]{1,0:T(8,128)}, /*in...) custom-call(bf16[16,128,2176]{2,1,0:T(8,128)(2,1)} %get-tuple-elemen, ...), custom_call_target="tpu_custom_call" | custom-call | flops 8589934592 | bytes 59244544 | tf_op jit(solution)/shard_map/last/pallas_call | solution.py:1569
  463.5 0.0 copy-start
  463.6 0.0 copy-start.1
  463.6 0.0 copy-start.2
  463.6 0.0 copy-start.3
  463.6 5.2 %add_bitcast_fusion = f32[1,512,2048]{2,1,0:T(8,128)} fusion(bf16[512,2048]{1,0:T(8,128)(2,1)} %get-tuple-element.83, bf16[256,2048]{1,0:T(8,128)(2,1)} %get-tuple-element.85, bf16[256,2048]{1,0:T(8,128)(2,1)} %get-tuple-element.84), kind=kLoop, calls=%fused_computation | loop fusion | flops 6291456 | bytes 8388608 | tf_op jit(solution)/shard_map/broadcast_in_dim | solution.py:1706
  468.8 0.0 copy-done
  468.8 0.0 copy-done.1
  468.8 0.0 copy-done.2
  468.8 0.8 copy-done.3
  469.6 0.0 copy-start.4
  469.6 4.7 add_bitcast_fusion.1
  474.3 0.0 copy-done.4
  474.3 0.0 copy-done.5
  474.3 0.0 copy-start.10
  474.4 1.1 slice_add_fusion
  475.4 0.1 copy.26
  475.5 0.0 copy-done.11
  475.5 0.6 select_reduce_fusion
  476.1 1.5 fusion
  477.7 0.0 copy-done.6
  477.7 1.0 copy.32
  478.6 0.0 copy-done.10
  478.6 0.8 copy.33
  479.4 0.0 copy-done.9
  479.4 0.8 copy.34
  480.2 0.0 copy-done.8
  480.2 0.8 copy.35
  481.0 0.0 copy-done.7
  481.0 0.8 copy.36
  (8 shorter events, 0.0 us)
Async XLA Ops:
  463.5 5.2 %copy-start = (bf16[2048,512]{1,0:T(8,128)(2,1)S(1)}, bf16[2048,512]{1,0:T(8,128)(2,1)}, u32[]{:S(2)}) copy-start(bf16[2048,512]{1,0:T(8,128)(2,1)} %get-tuple-element.79) | copy-start | bytes 6291460
  463.6 5.2 %copy-start.1 = (bf16[2048,512]{1,0:T(8,128)(2,1)S(1)}, bf16[2048,512]{1,0:T(8,128)(2,1)}, u32[]{:S(2)}) copy-start(bf16[2048,512]{1,0:T(8,128)(2,1)} %get-tuple-element.81) | copy-start | bytes 6291460
  463.6 5.2 %copy-start.2 = (bf16[2048,512]{1,0:T(8,128)(2,1)S(1)}, bf16[2048,512]{1,0:T(8,128)(2,1)}, u32[]{:S(2)}) copy-start(bf16[2048,512]{1,0:T(8,128)(2,1)} %get-tuple-element.80) | copy-start | bytes 6291460
  463.6 6.0 %copy-start.3 = (bf16[2048,512]{1,0:T(8,128)(2,1)S(1)}, bf16[2048,512]{1,0:T(8,128)(2,1)}, u32[]{:S(2)}) copy-start(bf16[2048,512]{1,0:T(8,128)(2,1)} %get-tuple-element.82) | copy-start | bytes 6291460
  469.6 4.7 copy-start.4
  469.6 4.7 copy-start.5
  474.3 1.2 copy-start.11
  474.3 3.3 copy-start.6
  474.3 4.3 copy-start.10
  475.4 4.0 copy-start.9
  477.7 2.6 copy-start.8
  478.6 2.4 copy-start.7
